TPU v7x, 32 devices: a whole 2x2x4 slice. The times are simulated.
32 devices in a mesh: dp: 8 (over y, x, core), seq: 4 (over z).
Axes of the slice: x: 2, y: 2, z: 4, core: 2. Of those that a mesh axis runs over, the one named last changes fastest.
Arguments:
- tile_tokens: bfloat16 [8, 128, 3200], P('dp', 'seq'), may hold values from -6 to 6
- proj_weight: bfloat16 [3200, 8192], P('dp', 'seq')
- text_hidden: bfloat16 [8, 512, 8192], P('dp', 'seq'), may hold values from -6 to 6
- cotangent: bfloat16 [8, 512, 8192], P('dp', 'seq'), may hold values from -1.1953125 to 1.1953125
- norm_gain: float32 [8192], replicated, may hold values from 0.25 to 1.75
- placeholders: int32 [8, 128], P('dp'), may hold values from 0 to 511, as said below
- bucket_levels: int32 [8, 4, 3200], P('dp', 'seq'), may hold values from 2 to 16
- row_draws: float32 [8, 4, 3200], P('dp', 'seq'), may hold values from 0 to 1
- column_draws: float32 [8, 8192], P('dp', 'seq'), may hold values from 0 to 1
Outputs:
- weight_grad: float32 [3200, 8192], P('dp', 'seq')
- gain_grad: float32 [8192], replicated
Inputs may be any that keep to these rules, and one draw needn't show every extreme that they name: Each row is strictly increasing. Among the positions of one device's block of 128 positions stand at most 48 placeholders, and in every row some block holds exactly 48.
All inputs are finite; a program needn't handle non-finite values.
Results may differ from a plain program's by a relative error of at most 0.014.
Values may be sent and summed in bfloat16 or wider, within the bound.
No kernel may reach another device: no remote copies, remote signals or barrier semaphores. Data moves between devices by JAX's collectives and lax.ppermute only.
A program may use at most 64 MiB of HBM per device.

v0:
```python
import jax
import jax.numpy as jnp
from jax import lax
from jax.sharding import PartitionSpec as P

IMG_MOST = 48


EPSILON = 1e-06


def quantize(gradient, levels_now, rows_now, columns_now):
    bucket_norm = jnp.sqrt(jnp.sum(gradient * gradient, axis=1, keepdims=True) + EPSILON)
    step_count = levels_now.astype(jnp.float32)[:, None]
    offset = 0.25 + 0.25 * (rows_now[:, None] + columns_now[None, :])
    ratio = jnp.abs(gradient) / bucket_norm * step_count
    lower = jnp.floor(ratio)
    quantum = lower + jnp.clip(2.0 * (ratio - lower - offset) + 0.5, 0.0, 1.0)
    return jnp.sign(gradient) * bucket_norm * quantum / step_count


def on_device(
    tile_tokens,
    proj_weight,
    text_hidden,
    cotangent,
    norm_gain,
    placeholders,
    bucket_levels,
    row_draws,
    column_draws,
):
    seq_count = lax.axis_size("seq")
    seq_index = lax.axis_index("seq")
    replicas = lax.axis_size("dp")
    places = placeholders[0]
    image_total = places.shape[0]
    tok_rows = text_hidden.shape[1]
    model_width = text_hidden.shape[2]
    columns = proj_weight.shape[1]
    all_positions = tok_rows * seq_count
    zero_half = jnp.zeros((), jnp.bfloat16)
    own_text = text_hidden[0]
    own_cot = cotangent[0]
    gathered = lax.all_gather(tile_tokens[0], "seq", axis=0, tiled=True)
    patch_block = gathered
    embedded = jnp.dot(
        patch_block,
        lax.all_gather(proj_weight, "dp", axis=0, tiled=True),
        preferred_element_type=jnp.float32,
    ).astype(jnp.bfloat16)
    image_marks = jnp.zeros((all_positions,), jnp.int32).at[places].set(1)
    local_marks = lax.dynamic_slice_in_dim(image_marks, seq_index * tok_rows, tok_rows)
    is_image = local_marks[:, None] == 1
    owners = places // tok_rows
    owner_ids = jnp.arange(seq_count, dtype=jnp.int32)
    counts = jnp.sum((owners[:, None] == owner_ids[None, :]).astype(jnp.int32), axis=0)
    starts = jnp.cumsum(counts) - counts
    own_start = starts[seq_index]
    own_count = counts[seq_index]
    slot_ids = jnp.arange(IMG_MOST, dtype=jnp.int32)
    source_rows = jnp.clip(own_start + slot_ids, 0, image_total - 1)
    local_slots = jnp.clip(jnp.take(places, source_rows) - seq_index * tok_rows, 0, tok_rows - 1)
    slot_live = (slot_ids < own_count)[:, None]
    flat_index = owners * IMG_MOST + (
        jnp.arange(image_total, dtype=jnp.int32) - jnp.take(starts, owners)
    )
    outgoing = jnp.where(slot_live, jnp.take(own_cot, local_slots, axis=0), zero_half)
    returned = lax.all_to_all(outgoing[None], "seq", split_axis=2, concat_axis=0, tiled=True)
    image_cot = jnp.take(returned.reshape(-1, columns), flat_index, axis=0).astype(jnp.float32)
    emb_float = embedded.astype(jnp.float32)
    column_gain = lax.dynamic_slice_in_dim(norm_gain, seq_index * columns, columns)
    grad_in = image_cot * column_gain[None, :]
    squares, mixed = lax.psum(
        (jnp.sum(emb_float * emb_float, axis=1), jnp.sum(grad_in * emb_float, axis=1)), "seq"
    )
    inverse = lax.rsqrt(squares / model_width + EPSILON)[:, None]
    normed = emb_float * inverse
    emb_grad = ((grad_in - normed * (mixed[:, None] * inverse / model_width)) * inverse).astype(
        jnp.bfloat16
    )
    image_part = jnp.sum(image_cot * normed, axis=0)
    text_float = own_text.astype(jnp.float32)
    text_inverse = lax.rsqrt(jnp.mean(text_float * text_float, axis=1, keepdims=True) + EPSILON)
    text_terms = own_cot.astype(jnp.float32) * text_float * text_inverse
    text_part = jnp.sum(jnp.where(is_image, 0.0, text_terms), axis=0)
    placed_part = lax.dynamic_update_slice_in_dim(
        jnp.zeros((model_width,), jnp.float32), image_part, seq_index * columns, 0
    )
    gain_part = text_part + placed_part
    own_levels = bucket_levels[0, 0]
    own_row_draws = row_draws[0, 0]
    own_column_draws = column_draws[0]
    patch_block = gathered
    gradient = lax.dot_general(
        patch_block, emb_grad, (((0,), (0,)), ((), ())), preferred_element_type=jnp.float32
    )
    summed = lax.psum_scatter(
        quantize(gradient, own_levels, own_row_draws, own_column_draws).astype(jnp.bfloat16),
        "dp",
        scatter_dimension=0,
        tiled=True,
    ).astype(jnp.float32)
    gain_total = lax.psum(gain_part, ("dp", "seq"))
    return (summed / replicas, gain_total / replicas)


def solution(mesh):
    return jax.shard_map(
        on_device,
        mesh=mesh,
        in_specs=(
            P("dp", "seq", None),
            P("dp", "seq"),
            P("dp", "seq", None),
            P("dp", "seq", None),
            P(),
            P("dp", None),
            P("dp", "seq", None),
            P("dp", "seq", None),
            P("dp", "seq"),
        ),
        out_specs=(P("dp", "seq"), P()),
        check_vma=False,
    )
```

profile of v0, /device:TPU:0, one launch (start us, length us, event | category | flops | bytes accessed | tf_op | source)
XLA Modules:
  0.0 315.0 jit_solution(2458585537406789046)
XLA Ops:
  7.2 0.0 copy-start
  7.2 0.0 copy-start.6
  7.2 0.0 copy-start.5
  7.2 0.0 copy-start.4
  7.2 0.0 all-gather.3.cloned.1.call-start
  7.3 0.7 all-gather.3.cloned.1.call-update
  7.9 0.7 and_select_fusion.5
  8.6 0.1 convert_reduce_fusion.1
  8.7 0.2 reduce-window.9
  8.9 0.6 dynamic_slice.12
  9.5 0.7 fusion.34
  10.2 0.7 fusion.33
  10.9 1.4 gather_fusion
  12.3 0.7 fusion.31
  13.0 3.6 %gather_fusion.1 = bf16[48,8192]{1,0:T(8,128)(2,1)S(1)} fusion(bf16[128,8192]{1,0:T(8,128)(2,1)} %bitcast.74, s32[1024]{0:T(1024)S(1)} %pad_clamp_fusion.1), kind=kCustom, calls=%fused_computation.1 | custom fusion | bytes 1573056 | tf_op jit(solution)/shard_map/jit(_take)/gather | solution.py:68
  16.6 1.3 compare_and_fusion
  17.9 0.2 fusion.21
  18.1 6.8 %copy.22 = bf16[1,48,8192]{1,0,2:T(2,128)(2,1)} copy(bf16[1,48,8192]{2,1,0:T(8,128)(2,1)S(1)} %fusion.21) | data formatting | bytes 1572864 | tf_op jit(solution)/shard_map/jit(_where)/select_n | solution.py:68
  24.8 0.5 broadcast.575
  25.3 45.2 %reduce.4 = bf16[8192,48]{1,0:T(8,128)(2,1)S(1)} reduce(bf16[8192,1,48]{2,1,0:T(2,128)(2,1)} %bitcast.76, bf16[]{:T(256)} %broadcast.575), dimensions={1}, to_apply=%bitcast.63.reduce_sub_computation | reduce | bytes 1572866
  70.6 4.0 %reshape.423 = bf16[4,2,49152]{2,1,0:T(2,128)(2,1)} reshape(bf16[8192,48]{1,0:T(8,128)(2,1)S(1)} %reduce.4) | data formatting | bytes 1572864
  74.6 6.3 %all-to-all-start = ((bf16[4,2,49152]{2,1,0:T(2,128)(2,1)}), bf16[4,2,49152]{2,1,0:T(2,128)(2,1)S(1)}, u32[]{:S(2)}, u32[]{:S(2)}) async-start(bf16[4,2,49152]{2,1,0:T(2,128)(2,1)} %reshape.423), calls=%async_computation | async-start | bytes 1572864 | tf_op jit(solution)/shard_map/all_to_all | solution.py:69
  80.9 0.0 reduce-scatter.4.cloned.1.call-start
  80.9 0.7 dynamic_slice.14
  81.6 0.0 copy-done.6
  81.7 0.0 copy-done
  81.7 2.6 compare_and_fusion.1
  84.3 0.0 copy-done.5
  84.4 0.0 copy-done.4
  84.4 30.7 %all-gather = bf16[1,128,3200]{2,1,0:T(8,128)(2,1)S(1)} all-gather(bf16[1,32,3200]{2,1,0:T(8,128)(2,1)S(1)} %copy-done.4), channel_id=2, replica_groups=mesh['dp'=8,'seq'=4] {'seq'}, dimensions={1}, use_global_device_ids=true | all-gather | bytes 1024000 | tf_op jit(solution)/shard_map/all_gather | solution.py:45
  115.0 0.0 all-to-all-done
  115.0 4.6 %reshape.424 = bf16[8192,1,48]{2,1,0:T(2,128)(2,1)} reshape(bf16[4,2,49152]{2,1,0:T(2,128)(2,1)S(1)} %all-to-all-done) | data formatting | bytes 1572864
  119.6 8.1 %copy.23 = bf16[1,48,8192]{2,1,0:T(8,128)(2,1)S(1)} copy(bf16[1,48,8192]{1,0,2:T(2,128)(2,1)} %bitcast.77) | data formatting | bytes 1572864 | tf_op jit(solution)/shard_map/all_to_all | solution.py:69
  127.8 0.6 all_to_all.12
  128.4 0.4 copy.24
  128.8 0.9 gather_fusion.2
  129.7 0.0 copy-start.3
  129.8 0.0 all-gather.3.cloned.1.call-done
  129.8 7.1 %multiply_reduce_fusion.1 = (f32[128]{0:T(128)S(1)}, f32[128,2048]{1,0:T(8,128)S(1)}) fusion(bf16[3200,2048]{1,0:T(8,128)(2,1)} %all-gather.3.cloned.1.call-done, bf16[1,128,3200]{2,1,0:T(8,128)(2,1)S(1)} %all-gather), kind=kOutput, calls=%fused_computation.31 | convolution fusion | flops 1678770048 | bytes 14975488 | tf_op jit(solution)/shard_map/dot_general | solution.py:47
  136.8 0.0 copy-start.2
  136.9 11.1 %psum.21 = f32[128]{0:T(128)S(1)} all-reduce(f32[128]{0:T(128)S(1)} %get-tuple-element.22), channel_id=1, replica_groups=mesh['dp'=8,'seq'=4] {'seq'}, use_global_device_ids=true, to_apply=%region_3.4 | all-reduce | flops 128 | bytes 1024 | tf_op jit(solution)/shard_map/psum | solution.py:74
  148.0 0.4 fusion.17
  148.4 8.4 %psum.22 = f32[128]{0:T(128)S(1)} all-reduce(f32[128]{0:T(128)S(1)} %get-tuple-element.13), channel_id=1, replica_groups=mesh['dp'=8,'seq'=4] {'seq'}, use_global_device_ids=true, to_apply=%region_5.6 | all-reduce | flops 128 | bytes 1024 | tf_op jit(solution)/shard_map/psum | solution.py:74
  156.8 0.0 copy-done.3
  156.8 0.0 copy-done.2
  156.8 0.0 copy-start.7
  156.8 5.1 %multiply_reduce_fusion = (f32[3200]{0:T(1024)S(1)}, f32[2048,3200]{1,0:T(8,128)S(1)}) fusion(bf16[1,128,3200]{2,1,0:T(8,128)(2,1)S(1)} %all-gather, f32[128,2048]{1,0:T(8,128)} %copy-done.2, f32[128]{0:T(128)S(1)} %multiply_multiply_fusion, f32[128]{0:T(128)S(1)} %add_rsqrt_fusion.1, f32[2048]{0:T(1024)S(1)} %dynamic_slice.14, ...), kind=kOutput, calls=%fused_computation.12 | convolution fusion | flops 1692922752 | bytes 28628608 | tf_op jit(solution)/shard_map/dot_general | solution.py:95
  162.0 0.0 copy-done.7
  162.0 22.2 %fusion.6 = bf16[3200,2048]{0,1:T(8,128)(2,1)} fusion(f32[2048,3200]{1,0:T(8,128)S(1)} %get-tuple-element.25, f32[3200]{0:T(1024)S(1)} %convert_reduce_fusion, f32[2048]{0:T(1024)S(1)} %bitcast.79, f32[3200]{0:T(1024)S(1)} %reduce.2, f32[3200]{0:T(1024)S(1)} %add_sqrt_fusion), kind=kLoop, calls=%fused_computation.13 | loop fusion | flops 117964800 | bytes 39368192 | tf_op jit(solution)/shard_map/convert_element_type | solution.py:99
  184.1 18.3 %copy.26 = bf16[3200,2048]{1,0:T(8,128)(2,1)} copy(bf16[3200,2048]{0,1:T(8,128)(2,1)} %fusion.6) | data formatting | bytes 26214400
  202.5 0.0 copy-start.1
  202.5 0.0 reduce-scatter.4.cloned.1.call-update
  202.5 1.0 scatter_custom_fusion
  203.5 0.1 dynamic-slice_compare_fusion
  203.6 2.1 fusion.10
  205.7 0.0 copy-done.1
  205.7 2.6 fusion.9
  208.3 41.3 %psum.23 = f32[8192]{0:T(1024)S(1)} all-reduce(f32[8192]{0:T(1024)S(1)} %add_dynamic-update-slice_fusion), channel_id=1, replica_groups=mesh['dp'=8,'seq'=4] {'dp','seq'}, use_global_device_ids=true, to_apply=%region_12.13 | all-reduce | flops 8192 | bytes 65536 | tf_op jit(solution)/shard_map/psum | solution.py:104
  249.7 0.6 broadcast_multiply_fusion
  250.3 47.4 %reduce-scatter.4.cloned.1.call-done = bf16[400,2048]{1,0:T(8,128)(2,1)} async-done(((bf16[3200,2048]{1,0:T(8,128)(2,1)}), bf16[400,2048]{1,0:T(8,128)(2,1)}) %reduce-scatter.4.cloned.1.call-update) | async-done | bytes 1638416
  297.7 2.8 copy.27
  300.5 2.5 convert_multiply_fusion.2
  303.0 5.2 %copy.25 = f32[400,2048]{1,0:T(8,128)} copy(f32[400,2048]{0,1:T(8,128)} %convert_multiply_fusion.2) | data formatting | bytes 6553600
  (14 shorter events, 0.2 us)
Async XLA Ops:
  7.2 74.5 %copy-start = (s32[1,128]{1,0:T(1,128)S(1)}, s32[1,128]{1,0:T(1,128)}, u32[]{:S(2)}) copy-start(s32[1,128]{1,0:T(1,128)} %param.14) | copy-start | bytes 1540
  7.2 74.5 %copy-start.6 = (f32[1,1,3200]{2,1,0:T(1,128)S(1)}, f32[1,1,3200]{2,1,0:T(1,128)}, u32[]{:S(2)}) copy-start(f32[1,1,3200]{2,1,0:T(1,128)} %param.16) | copy-start | bytes 38404
  7.2 77.1 %copy-start.5 = (s32[1,1,3200]{2,1,0:T(1,128)S(1)}, s32[1,1,3200]{2,1,0:T(1,128)}, u32[]{:S(2)}) copy-start(s32[1,1,3200]{2,1,0:T(1,128)} %param.15) | copy-start | bytes 38404
  7.2 77.2 %copy-start.4 = (bf16[1,32,3200]{2,1,0:T(8,128)(2,1)S(1)}, bf16[1,32,3200]{2,1,0:T(8,128)(2,1)}, u32[]{:S(2)}) copy-start(bf16[1,32,3200]{2,1,0:T(8,128)(2,1)} %param.9) | copy-start | bytes 614404
  7.2 122.6 %all-gather.3.cloned.1.call-start = ((), (), s32[]{:S(2)}) async-start(), calls=%async_computation.2 | async-start | bytes 14745600 | tf_op jit(solution)/shard_map/all_gather | solution.py:49
  74.6 40.5 %all-to-all-start = ((bf16[4,2,49152]{2,1,0:T(2,128)(2,1)}), bf16[4,2,49152]{2,1,0:T(2,128)(2,1)S(1)}, u32[]{:S(2)}, u32[]{:S(2)}) async-start(bf16[4,2,49152]{2,1,0:T(2,128)(2,1)} %reshape.423), calls=%async_computation | async-start | bytes 1572864 | tf_op jit(solution)/shard_map/all_to_all | solution.py:69
  80.9 216.8 %reduce-scatter.4.cloned.1.call-start = ((), (), s32[]{:S(2)}) async-start(), calls=%async_computation.3 | async-start | bytes 14745600
  129.7 27.0 %copy-start.3 = (bf16[128,2048]{1,0:T(8,128)(2,1)}, bf16[128,2048]{1,0:T(8,128)(2,1)S(1)}, u32[]{:S(2)}) copy-start(bf16[128,2048]{1,0:T(8,128)(2,1)S(1)} %gather_fusion.2) | copy-start | bytes 1572868
  136.8 19.9 %copy-start.2 = (f32[128,2048]{1,0:T(8,128)}, f32[128,2048]{1,0:T(8,128)S(1)}, u32[]{:S(2)}) copy-start(f32[128,2048]{1,0:T(8,128)S(1)} %get-tuple-element.23) | copy-start | bytes 3145732
  156.8 5.2 %copy-start.7 = (f32[1,2048]{1,0:T(1,128)S(1)}, f32[1,2048]{1,0:T(1,128)}, u32[]{:S(2)}) copy-start(f32[1,2048]{1,0:T(1,128)} %param.17) | copy-start | bytes 24580
  202.5 3.2 %copy-start.1 = (bf16[1,128,8192]{2,1,0:T(8,128)(2,1)S(1)}, bf16[1,128,8192]{2,1,0:T(8,128)(2,1)}, u32[]{:S(2)}) copy-start(bf16[1,128,8192]{2,1,0:T(8,128)(2,1)} %param.12) | copy-start | bytes 6291460
Sparse Core Ops, SparseCore 0:
  9.9 76.9 all-gather.2
  202.6 95.0 reduce-scatter.3
where the time goes:
time: 316 us; the launch traced here: 315 us
  blocking collectives  91.5 us (29%)
  other arithmetic  82.2 us (26%)
  local copies, waits for them, and re-layouts  60.3 us (19%)
  waiting for transfers between devices  48.1 us (15%)
  between operations  14.3 us (5%)
  matrix products  12.2 us (4%)
  starting transfers between devices  6.39 us (2%)
    unnamed x3, waiting for transfers between devices  48.1 us
    unnamed x2, other arithmetic  45.3 us
    psum x1, blocking collectives, on_device(): gain_total = lax.psum(gain_part, ('dp', 'seq'))  41.3 us
    unnamed x22, local copies, waits for them, and re-layouts  35.4 us
    all_gather x1, blocking collectives, on_device(): gathered = lax.all_gather(tile_tokens[0], 'seq', axis=0, tiled=True)  30.7 us
    convert_element_type x1, other arithmetic, on_device(): quantize(gradient, own_levels, own_row_draws, own_column_draws)  22.2 us
    psum x2, blocking collectives, on_device(): lax.psum((jnp.sum(emb_float * emb_float, axis=1), jnp.sum(grad_in * emb_f...  19.5 us
    all_to_all x3, local copies, waits for them, and re-layouts, on_device(): lax.all_to_all(outgoing[None], 'seq', split_axis=2, concat_axis=0, tiled=...  9.14 us
  transfers between devices with their start and end apart: 3, of which 1 were waited for; matrix products, arithmetic and copies ran while one was open for 29% of the time, Pallas kernels for 0%

commit v1 on v0

v1 whole, which is shorter than its diff:
```python
import functools

import jax
import jax.numpy as jnp
from jax import lax
from jax.experimental import pallas as pl
from jax.experimental.pallas import tpu as pltpu
from jax.sharding import PartitionSpec as P


IMG_MOST = 48
META_ROWS = 16
EXTRA_ROWS = 8
EPSILON = 1e-06
FLOAT = jnp.float32
HALF = jnp.bfloat16


def whole(*_):
    return pl.BlockSpec(memory_space=pltpu.VMEM)


def scalar():
    return pl.BlockSpec(memory_space=pltpu.SMEM)


def grant(mebibytes):
    return pltpu.CompilerParams(vmem_limit_bytes=mebibytes << 20)


def lanes(count):
    return -(-count // 128) * 128


def flip(value, bit):
    count = lax.axis_size("dp")
    return lax.ppermute(value, "dp", [(i, i ^ (1 << bit)) for i in range(count)])


def swap(value, step):
    count = lax.axis_size("seq")
    return lax.ppermute(value, "seq", [(i, i ^ step) for i in range(count)])


def pieces(value):
    high = lax.reduce_precision(value, 8, 7)
    rest = value - high
    mid = lax.reduce_precision(rest, 8, 7)
    return high, mid, rest - mid


def cast_pieces(value):
    high = value.astype(HALF).astype(FLOAT)
    rest = value - high
    mid = rest.astype(HALF).astype(FLOAT)
    return high, mid, rest - mid


def stacked_lines(values, lines, width):
    line = lax.broadcasted_iota(jnp.int32, (lines, width), 0)
    block = jnp.zeros((lines, width), FLOAT)
    for index, value in enumerate(values):
        block = jnp.where(line == index, value, block)
    return block


def pack_kernel(tile_ref, level_ref, draw_ref, out_ref):
    owners, _, width = out_ref.shape
    rows, full = tile_ref.shape
    terms = (level_ref[...].astype(FLOAT),) + cast_pieces(draw_ref[...])
    extra = stacked_lines(terms, META_ROWS, full).astype(HALF)
    for owner in range(owners):
        cut = slice(owner * width, (owner + 1) * width)
        out_ref[owner, :rows, :] = tile_ref[:, cut]
        out_ref[owner, rows:, :] = extra[:, cut]


def unpack_kernel(order, place_ref, in_ref, tile_ref, meta_ref, tile_scratch, meta_scratch):
    replicas, rows, width = in_ref.shape
    tokens = rows - META_ROWS
    kept = tile_ref.shape[0]
    tile_scratch[...] = jnp.zeros_like(tile_scratch)
    meta_scratch[...] = jnp.zeros_like(meta_scratch)
    for slot, relative in enumerate(order):
        block = in_ref[place_ref[0] ^ relative].astype(FLOAT)
        tile_scratch[slot * tokens : (slot + 1) * tokens, :width] = block[:tokens]
        meta = block[tokens:]
        meta_scratch[relative : relative + 1, :width] = meta[0:1]
        meta_scratch[replicas + relative : replicas + relative + 1, :width] = (
            meta[1:2] + meta[2:3] + meta[3:4]
        )
    tile_ref[...] = tile_scratch[...].T[:kept].astype(HALF)
    meta_ref[...] = meta_scratch[...].T[:kept]


def regroup_kernel(order, tokens, *refs):
    count = len(refs) - len(order)
    for slot, relative in enumerate(order):
        cut = slice(slot * tokens, (slot + 1) * tokens)
        refs[count + relative][...] = jnp.concatenate([ref[:, cut] for ref in refs[:count]], axis=1)


def text_kernel(place_ref, row_ref, column_ref, text_ref, cot_ref, out_ref):
    owners, _, columns = out_ref.shape
    rows, full = text_ref.shape
    count = row_ref.shape[1]
    mine = place_ref[0]
    base = mine * rows
    position = lax.broadcasted_iota(jnp.int32, (rows, count), 0)
    hits = (row_ref[...] - base == position).astype(FLOAT)
    is_text = 1.0 - jnp.max(hits, axis=1, keepdims=True)
    start = jnp.sum((row_ref[...] < base).astype(jnp.int32), axis=1, keepdims=True)
    token = lax.broadcasted_iota(jnp.int32, (IMG_MOST, count), 1)
    slot = lax.broadcasted_iota(jnp.int32, (IMG_MOST, count), 0)
    chosen = (token - start == slot).astype(HALF)
    spread = (
        column_ref[...] - base == lax.broadcasted_iota(jnp.int32, (count, rows), 1)
    ).astype(HALF)
    select = jnp.dot(chosen, spread, preferred_element_type=FLOAT).astype(HALF)
    total = jnp.zeros((rows, 1), FLOAT)
    for owner in range(owners):
        text = text_ref[:, owner * columns : (owner + 1) * columns].astype(FLOAT)
        total = total + jnp.sum(text * text, axis=1, keepdims=True)
    inverse = lax.rsqrt(total / full + EPSILON) * is_text
    for step in range(owners):
        owner = mine ^ step
        cut = pl.ds(pl.multiple_of(owner * columns, columns), columns)
        cot = cot_ref[:, cut]
        terms = cot.astype(FLOAT) * text_ref[:, cut].astype(FLOAT) * inverse
        part = jnp.sum(terms, axis=0, keepdims=True)
        out_ref[step, :IMG_MOST, :] = jnp.dot(
            select, cot, preferred_element_type=FLOAT
        ).astype(HALF)
        out_ref[step, IMG_MOST:, :] = stacked_lines(
            cast_pieces(part), EXTRA_ROWS, columns
        ).astype(HALF)


def quantize_kernel(slots, replicas, adds, *refs):
    count = len(slots)
    tile_refs = refs[:count]
    meta_ref = refs[count]
    loads = refs[count + 1 : 2 * count + 1]
    total_ref = refs[2 * count + 1] if adds else None
    out_ref, gradient, half_draw, row_half, lever, weight = refs[-6:]
    rows, columns = out_ref.shape
    tokens = tile_refs[0].shape[1]
    groups = rows // 8
    strips = [slice(at, at + 128) for at in range(0, columns, 128)]
    unroll = 5 if groups % 5 == 0 else 2
    for index, relative in enumerate(slots):
        load = loads[index]
        gradient[...] = jnp.dot(
            tile_refs[index][...], load[:tokens, :], preferred_element_type=FLOAT
        )
        extra = load[tokens:, :].astype(FLOAT)
        draw = 0.5 * (extra[3:4] + extra[4:5] + extra[5:6])
        half_draw[...] = jnp.broadcast_to(draw, (8, columns))

        def sum_group(step, carry):
            cut = pl.ds(pl.multiple_of(step * 8, 8), 8)
            parts = [gradient[cut, strip] for strip in strips]
            parts = [part * part for part in parts]
            while len(parts) > 1:
                parts = [a + b for a, b in zip(parts[::2], parts[1::2])] + parts[len(parts) & ~1 :]
            lever[cut, :] = parts[0]
            return carry

        lax.fori_loop(0, groups, sum_group, 0, unroll=unroll)
        norm = jnp.sqrt(jnp.sum(lever[...], axis=1, keepdims=True) + EPSILON)
        levels = meta_ref[:, relative : relative + 1]
        row_draw = meta_ref[:, replicas + relative : replicas + relative + 1]
        row_half[...] = jnp.broadcast_to(0.5 * row_draw, lever.shape)
        lever[...] = jnp.broadcast_to(levels / norm, lever.shape)
        weight[...] = jnp.broadcast_to(norm / (levels * replicas), lever.shape)

        def group(step, carry):
            cut = pl.ds(pl.multiple_of(step * 8, 8), 8)
            factor = lever[cut, :]
            scale = weight[cut, :]
            opposite = -scale
            row_shift = row_half[cut, :]
            for strip in strips:
                entry = gradient[cut, strip]
                ratio = jnp.abs(entry) * factor
                lower = jnp.floor(ratio)
                part = ratio - lower
                shift = half_draw[:, strip] + row_shift
                quantum = lower + jnp.clip(part + part - shift, 0.0, 1.0)
                term = jnp.where(entry < 0.0, opposite, scale) * quantum
                if index > 0:
                    term = term + out_ref[cut, strip]
                elif adds:
                    term = term + total_ref[cut, strip]
                out_ref[cut, strip] = term
            return carry

        lax.fori_loop(0, groups, group, 0, unroll=unroll)


def quantized_sum(tiles, meta, loads, slots, replicas, total, last):
    rows, _ = tiles[0].shape
    columns = loads[0].shape[1]
    adds = total is not None
    return pl.pallas_call(
        functools.partial(quantize_kernel, slots, replicas, adds),
        in_specs=[whole()] * (2 * len(slots) + 1 + adds),
        out_specs=whole(),
        out_shape=jax.ShapeDtypeStruct((rows, columns), FLOAT),
        scratch_shapes=[
            pltpu.VMEM((rows, columns), FLOAT),
            pltpu.VMEM((8, columns), FLOAT),
            pltpu.VMEM((rows, 128), FLOAT),
            pltpu.VMEM((rows, 128), FLOAT),
            pltpu.VMEM((rows, 128), FLOAT),
        ],
        input_output_aliases={2 * len(slots) + 1: 0} if adds and not last else {},
        compiler_params=grant(12),
        cost_estimate=pl.CostEstimate(
            flops=len(slots) * rows * columns * 1200, bytes_accessed=0, transcendentals=0
        ),
        name="quantized_sum",
    )(*[tiles[slot] for slot in slots], meta, *loads, *([total] if adds else []))


def stack_blocks(stats, step):
    return jnp.stack([stats[:, at ^ step] for at in range(stats.shape[1])], axis=1)


def half_of(value, bit, taken):
    shape = value.shape
    high = shape[0] // (2 * bit)
    cut = value.reshape((high, 2, bit) + shape[1:])[:, taken]
    return cut.reshape((high * bit,) + shape[1:])


def on_device(
    tile_tokens,
    proj_weight,
    text_hidden,
    cotangent,
    norm_gain,
    placeholders,
    bucket_levels,
    row_draws,
    column_draws,
):
    seq_count = lax.axis_size("seq")
    seq_index = lax.axis_index("seq")
    replicas = lax.axis_size("dp")
    replica = lax.axis_index("dp")
    levels_of_bits = replicas.bit_length() - 1
    assert replicas == 1 << levels_of_bits
    places = placeholders[0]
    image_total = places.shape[0]
    tok_rows, model_width = text_hidden.shape[1:]
    tile_rows, _ = tile_tokens.shape[1:]
    width, columns = proj_weight.shape
    padded = -(-width // 16) * 16
    order = tuple(range(0, replicas, 2)) + tuple(range(1, replicas, 2))
    here = replica.astype(jnp.int32).reshape(1)
    there = seq_index.astype(jnp.int32).reshape(1)

    packed = pl.pallas_call(
        pack_kernel,
        in_specs=[whole()] * 3,
        out_specs=whole(),
        out_shape=jax.ShapeDtypeStruct((replicas, tile_rows + META_ROWS, width), HALF),
        compiler_params=grant(4),
        name="pack",
    )(tile_tokens[0], bucket_levels[0], row_draws[0])
    exchanged = lax.all_to_all(packed, "dp", 0, 0, tiled=True)
    own_tile, meta = pl.pallas_call(
        functools.partial(unpack_kernel, order),
        in_specs=[scalar(), whole()],
        out_specs=[whole(), whole()],
        out_shape=[
            jax.ShapeDtypeStruct((padded, replicas * tile_rows), HALF),
            jax.ShapeDtypeStruct((padded, lanes(2 * replicas)), FLOAT),
        ],
        scratch_shapes=[
            pltpu.VMEM((lanes(replicas * tile_rows), lanes(width)), FLOAT),
            pltpu.VMEM((lanes(2 * replicas), lanes(width)), FLOAT),
        ],
        compiler_params=grant(8),
        name="unpack",
    )(here, exchanged)
    tile_blocks = [own_tile]
    for step in range(1, seq_count):
        tile_blocks.append(swap(own_tile, step))

    outgoing = pl.pallas_call(
        text_kernel,
        in_specs=[scalar()] + [whole()] * 4,
        out_specs=whole(),
        out_shape=jax.ShapeDtypeStruct((seq_count, IMG_MOST + EXTRA_ROWS, columns), HALF),
        cost_estimate=pl.CostEstimate(
            flops=tok_rows * model_width * 4000, bytes_accessed=0, transcendentals=0
        ),
        compiler_params=grant(16),
        name="text_part",
    )(there, placeholders, places.reshape(image_total, 1), text_hidden[0], cotangent[0])
    outgoing, last = lax.optimization_barrier((outgoing, tile_blocks[-1]))
    tile_blocks[-1] = last
    returned = [outgoing[0]]
    for step in range(1, seq_count):
        returned.append(swap(outgoing[step], step))

    weight = jnp.pad(proj_weight, ((0, padded - width), (0, 0)))
    even = (replicas // 2) * tile_rows
    split = seq_count // 2
    bit_orders = (
        tuple(range(1, levels_of_bits)),
        tuple(reversed(range(1, levels_of_bits))),
    )
    parts = (tile_blocks[:split], tile_blocks[split:])
    embedded_parts = []
    for group, bits in zip(parts, bit_orders):

        def product(cut, kind):
            left = jnp.concatenate([block[:, cut] for block in group], axis=1)
            out = lax.dot_general(
                left, weight, (((0,), (0,)), ((), ())), preferred_element_type=FLOAT
            ).astype(kind)
            out = out.reshape(len(group), replicas // 2, tile_rows, columns)
            return jnp.transpose(out, (1, 0, 2, 3))

        sent = product(slice(even, 2 * even), HALF)
        held = product(slice(0, even), FLOAT)
        arrived = flip(sent, 0)
        remaining = list(range(1, levels_of_bits))
        for bit in bits:
            stride = 1 << remaining.index(bit)
            remaining.remove(bit)
            held = held + arrived.astype(FLOAT)
            sent = half_of(held, stride, 1).astype(HALF)
            held = half_of(held, stride, 0)
            arrived = flip(sent, bit)
        held = held + arrived.astype(FLOAT)
        embedded_parts.append(held.reshape(-1, columns))
    emb_float = jnp.concatenate(embedded_parts, axis=0).astype(HALF).astype(FLOAT)

    tokens = jnp.arange(image_total, dtype=jnp.int32)
    absolute = ((tokens // tile_rows) ^ there) * tile_rows + tokens % tile_rows
    sources = jnp.arange(seq_count, dtype=jnp.int32) ^ there
    starts = jnp.sum((places[None, :] < (sources * tok_rows)[:, None]).astype(jnp.int32), axis=1)
    wanted = (absolute[:, None] - starts[None, :])[:, :, None]
    match = (wanted == jnp.arange(IMG_MOST, dtype=jnp.int32)[None, None, :]).astype(HALF)
    arrived = jnp.concatenate([block[:IMG_MOST] for block in returned], axis=0)
    image_cot = jnp.dot(
        match.reshape(image_total, seq_count * IMG_MOST), arrived, preferred_element_type=FLOAT
    )
    text_part = sum(
        jnp.sum(block[IMG_MOST : IMG_MOST + 3].astype(FLOAT), axis=0) for block in returned
    )

    column_gain = lax.dynamic_slice_in_dim(norm_gain, seq_index * columns, columns)
    grad_in = image_cot * column_gain[None, :]
    stats = jnp.stack(
        [jnp.sum(emb_float * emb_float, axis=1), jnp.sum(grad_in * emb_float, axis=1)]
    ).reshape(2, seq_count, tile_rows)
    for_all = stats
    for step in range(1, seq_count):
        for_all = for_all + swap(stack_blocks(stats, step), step)
    squares, mixed = for_all.reshape(2, image_total)
    inverse = lax.rsqrt(squares / model_width + EPSILON)[:, None]
    normed = emb_float * inverse
    emb_grad = ((grad_in - normed * (mixed[:, None] * inverse / model_width)) * inverse).astype(HALF)
    gain_part = text_part + jnp.sum(image_cot * normed, axis=0)
    extra = jnp.stack(
        pieces(gain_part)
        + pieces(column_draws[0])
        + (jnp.zeros_like(gain_part),) * (EXTRA_ROWS - 6)
    ).astype(HALF)
    own_load = jnp.concatenate([emb_grad, extra], axis=0)

    tiles = pl.pallas_call(
        functools.partial(regroup_kernel, order, tile_rows),
        in_specs=[whole()] * seq_count,
        out_specs=[whole()] * replicas,
        out_shape=[jax.ShapeDtypeStruct((padded, image_total), HALF)] * replicas,
        cost_estimate=pl.CostEstimate(
            flops=replicas * padded * image_total * 2000, bytes_accessed=0, transcendentals=0
        ),
        compiler_params=grant(8),
        name="regroup",
    )(*tile_blocks)

    loads = {0: own_load}
    if levels_of_bits == 3:
        loads[1] = flip(own_load, 0)
        loads[2] = flip(own_load, 1)
        loads[4] = flip(own_load, 2)
        is_low = (replica & 1) == 0
        passed = jnp.where(is_low, loads[2], loads[4])
        pairs = [(i, i ^ (4 if i % 2 == 0 else 2)) for i in range(replicas)]
        loads[6] = lax.ppermute(passed, "dp", pairs)
        for slot in (2, 4, 6):
            loads[slot + 1] = flip(loads[slot], 0)
        batches = ((0, 1), (2, 4), (3, 5), (6, 7))
    else:
        for bit in tuple(range(1, levels_of_bits)) + (0,):
            loads.update({slot ^ (1 << bit): flip(load, bit) for slot, load in list(loads.items())})
        batches = tuple((slot, slot + 1) for slot in range(0, replicas, 2))
    total = None
    for slots in batches:
      total = quantized_sum(tiles, meta, [loads[slot] for slot in slots], slots, replicas, total, slots == batches[-1])
    gain_rows = sum(
        jnp.sum(load[image_total : image_total + 3].astype(FLOAT), axis=0) for load in loads.values()
    )
    gain_rows = (gain_rows / replicas).reshape(8, columns // 8)
    gains = jnp.stack([gain_rows] + [swap(gain_rows, step) for step in range(1, seq_count)])
    gain_total = jnp.take(gains, sources, axis=0)
    return total[:width], gain_total.reshape(model_width)


def solution(mesh):
    return jax.shard_map(
        on_device,
        mesh=mesh,
        in_specs=(
            P("dp", "seq", None),
            P("dp", "seq"),
            P("dp", "seq", None),
            P("dp", "seq", None),
            P(),
            P("dp", None),
            P("dp", "seq", None),
            P("dp", "seq", None),
            P("dp", "seq"),
        ),
        out_specs=(P("dp", "seq"), P()),
        check_vma=False,
    )
```

time: 316 us -> 158 us (0.50)
  blocking collectives: 91.5 us -> 0 us
  other arithmetic: 82.2 us -> 4.35 us
  local copies, waits for them, and re-layouts: 60.3 us -> 22.7 us
  Pallas kernels: 0 us -> 32.3 us
  starting transfers between devices: 6.39 us -> 30.5 us
  waiting for transfers between devices: 48.1 us -> 62.1 us
  between operations: 14.3 us -> 1.31 us
  matrix products: 12.2 us -> 4.27 us
    ppermute x0 -> x25, waiting for transfers between devices: none -> 62 us  [the longest x12 40.8 us: swap(): return lax.ppermute(value, 'seq', [(i, i ^ step) for i in range(count)])]
    psum x3 -> x0, blocking collectives: 60.8 us -> none  [the longest x1 41.3 us: on_device(): gain_total = lax.psum(gain_part, ('dp', 'seq'))]
    unnamed x3 -> x0, waiting for transfers between devices: 48.1 us -> none
    unnamed x2 -> x1, other arithmetic: 45.3 us -> 0.07 us
    pallas_call x0 -> x8, Pallas kernels: none -> 32.3 us  [the longest x4 28.7 us: quantized_sum(): pl.pallas_call(functools.partial(quantize_kernel, slots, replicas, adds),...]
    all_gather x1 -> x0, blocking collectives: 30.7 us -> none  [on_device(): gathered = lax.all_gather(tile_tokens[0], 'seq', axis=0, tiled=True)]
    ppermute x0 -> x25, starting transfers between devices: none -> 25.3 us  [the longest x12 17 us: swap(): return lax.ppermute(value, 'seq', [(i, i ^ step) for i in range(count)])]
    convert_element_type x2 -> x0, other arithmetic: 22.2 us -> none  [the longest x1 22.2 us: on_device(): quantize(gradient, own_levels, own_row_draws, own_column_draws)]
  transfers between devices with their start and end apart: 3 -> 26, of which waited for: 1 -> 14; matrix products, arithmetic and copies ran while one was open for 29% -> 5% of each run, Pallas kernels for 0% -> 20%
where the time goes in v1:
time: 158 us
  waiting for transfers between devices  62.1 us (39%)
  Pallas kernels  32.3 us (20%)
  starting transfers between devices  30.5 us (19%)
  local copies, waits for them, and re-layouts  22.7 us (14%)
  other arithmetic  4.35 us (3%)
  matrix products  4.27 us (3%)
    ppermute x12, waiting for transfers between devices, swap(): return lax.ppermute(value, 'seq', [(i, i ^ step) for i in range(count)])  40.8 us
    pallas_call x4, Pallas kernels, quantized_sum(): pl.pallas_call(functools.partial(quantize_kernel, slots, replicas, adds),...  28.7 us
    ppermute x12, waiting for transfers between devices, flip(): return lax.ppermute(value, 'dp', [(i, i ^ 1 << bit) for i in range(count)])  21.2 us
    unnamed x54, local copies, waits for them, and re-layouts  17.4 us
    ppermute x12, starting transfers between devices, swap(): return lax.ppermute(value, 'seq', [(i, i ^ step) for i in range(count)])  17 us
    ppermute x12, starting transfers between devices, flip(): return lax.ppermute(value, 'dp', [(i, i ^ 1 << bit) for i in range(count)])  8.31 us
    all_to_all x1, starting transfers between devices, on_device(): exchanged = lax.all_to_all(packed, 'dp', 0, 0, tiled=True)  5.2 us
  transfers between devices with their start and end apart: 26, of which 14 were waited for; matrix products, arithmetic and copies ran while one was open for 5% of the time, Pallas kernels for 20%

profile of v1, /device:TPU:0, one launch (start us, length us, event | category | flops | bytes accessed | tf_op | source)
XLA Modules:
  0.0 157.5 jit_solution(17931381682037514374)
XLA Ops:
  0.7 1.0 copy-done.5
  1.7 0.7 copy-done.16
  2.4 0.7 copy-done.17
  3.1 0.9 pack.1
  4.0 5.2 %all-to-all-start = ((bf16[8,48,400]{2,1,0:T(8,128)(2,1)}), bf16[8,48,400]{2,1,0:T(8,128)(2,1)S(1)}, u32[]{:S(2)}, u32[]{:S(2)}) async-start(bf16[8,48,400]{2,1,0:T(8,128)(2,1)} %pack.1), calls=%async_computation | async-start | bytes 786432 | tf_op jit(solution)/shard_map/all_to_all | solution.py:272
  9.4 0.8 copy.21.column_ref
  10.1 0.8 convert_reduce_fusion.12
  11.0 0.7 dynamic_slice.3
  11.8 0.6 copy-done.18
  12.5 1.6 %copy-done.19 = bf16[1,128,8192]{2,1,0:T(8,128)(2,1)S(1)} copy-done((bf16[1,128,8192]{2,1,0:T(8,128)(2,1)S(1)}, bf16[1,128,8192]{2,1,0:T(8,128)(2,1)}, u32[]{:S(2)}) %copy-start.19) | copy-done | bytes 2097176
  14.1 1.6 %copy-done.20 = bf16[1,128,8192]{2,1,0:T(8,128)(2,1)S(1)} copy-done((bf16[1,128,8192]{2,1,0:T(8,128)(2,1)S(1)}, bf16[1,128,8192]{2,1,0:T(8,128)(2,1)}, u32[]{:S(2)}) %copy-start.20) | copy-done | bytes 2097176
  15.7 1.7 %text_part.1 = bf16[4,56,2048]{2,1,0:T(8,128)(2,1)S(1)} custom-call(s32[1]{0:T(128)} %bitcast.4.place_ref, s32[1,128]{1,0:T(1,128)S(1)} %copy-done.18, s32[128,1]{1,0:T(8,128)S(1)} %copy.21.column_ref, bf16[128,8192]{1,0:T(8,128)(2,1)S(1)} %bitcast.103, bf16[128,8192]{1,0:T(8,128)(2,1)S(1)} %bitcast.104), custom_call_target="tpu_custom_call" | custom-call | flops 4194304000 | tf_op jit(solution)/shard_map/text_part/pallas_call | solution.py:292
  17.8 3.7 %collective-permute-start.2 = (bf16[400,256]{1,0:T(8,128)(2,1)S(1)}, bf16[400,256]{1,0:T(8,128)(2,1)S(1)}, u32[]{:S(2)}, u32[]{:S(2)}) collective-permute-start(bf16[400,256]{1,0:T(8,128)(2,1)S(1)} %get-tuple-element.14.refs_0_), channel_id=1, source_target_pairs={{0,3},{1,2},{2,1},{3,0},{4,7},{5,6},{6,5},{7,4},{8,11},{9,10},{10,... | collective-permute-start | bytes 614408 | tf_op jit(solution)/shard_map/ppermute | solution.py:42
  21.4 0.8 collective-permute-start
  22.2 5.5 %collective-permute-done.2.refs_3_ = bf16[400,256]{1,0:T(8,128)(2,1)S(1)} collective-permute-done((bf16[400,256]{1,0:T(8,128)(2,1)S(1)}, bf16[400,256]{1,0:T(8,128)(2,1)S(1)}, u32[]{:S(2)}, u32[]{:S(2)}) %collective-permute-start.2) | collective-permute-done | bytes 204832 | tf_op jit(solution)/shard_map/ppermute | solution.py:42
  27.8 11.5 %collective-permute-done.1.refs_2_ = bf16[400,256]{1,0:T(8,128)(2,1)S(1)} collective-permute-done((bf16[400,256]{1,0:T(8,128)(2,1)S(1)}, bf16[400,256]{1,0:T(8,128)(2,1)S(1)}, u32[]{:S(2)}, u32[]{:S(2)}) %collective-permute-start.1) | collective-permute-done | bytes 204832 | tf_op jit(solution)/shard_map/ppermute | solution.py:42
  39.4 0.7 copy-done.8
  40.0 0.7 convolution_convert_fusion
  40.9 0.7 convolution_convert_fusion.1
  41.6 0.7 fusion.36
  42.6 2.5 %collective-permute-start.5 = (bf16[56,2048]{1,0:T(8,128)(2,1)S(1)}, bf16[56,2048]{1,0:T(8,128)(2,1)S(1)}, u32[]{:S(2)}, u32[]{:S(2)}) collective-permute-start(bf16[56,2048]{1,0:T(8,128)(2,1)S(1)} %get-tuple-element.31), channel_id=1, source_target_pairs={{0,3},{1,2},{2,1},{3,0},{4,7},{5,6},{6,5},{7,4},{8,11},{9,10},{10,... | collective-permute-start | bytes 688136 | tf_op jit(solution)/shard_map/ppermute | solution.py:42
  45.1 0.9 collective-permute-start.4
  46.1 0.7 fusion.29
  46.8 3.7 %collective-permute-done.3 = bf16[56,2048]{1,0:T(8,128)(2,1)S(1)} collective-permute-done((bf16[56,2048]{1,0:T(8,128)(2,1)S(1)}, bf16[56,2048]{1,0:T(8,128)(2,1)S(1)}, u32[]{:S(2)}, u32[]{:S(2)}) %collective-permute-start.3) | collective-permute-done | bytes 229408 | tf_op jit(solution)/shard_map/ppermute | solution.py:42
  50.6 6.0 %collective-permute-done.5 = bf16[56,2048]{1,0:T(8,128)(2,1)S(1)} collective-permute-done((bf16[56,2048]{1,0:T(8,128)(2,1)S(1)}, bf16[56,2048]{1,0:T(8,128)(2,1)S(1)}, u32[]{:S(2)}, u32[]{:S(2)}) %collective-permute-start.5) | collective-permute-done | bytes 229408 | tf_op jit(solution)/shard_map/ppermute | solution.py:42
  56.5 10.0 %collective-permute-done.4 = bf16[56,2048]{1,0:T(8,128)(2,1)S(1)} collective-permute-done((bf16[56,2048]{1,0:T(8,128)(2,1)S(1)}, bf16[56,2048]{1,0:T(8,128)(2,1)S(1)}, u32[]{:S(2)}, u32[]{:S(2)}) %collective-permute-start.4) | collective-permute-done | bytes 229408 | tf_op jit(solution)/shard_map/ppermute | solution.py:42
  66.6 0.4 convert_add_fusion
  67.5 1.7 %collective-permute-start.10 = (bf16[2,2,32,2048]{3,2,1,0:T(8,128)(2,1)S(1)}, bf16[2,2,32,2048]{3,2,1,0:T(8,128)(2,1)S(1)}, u32[]{:S(2)}, u32[]{:S(2)}) collective-permute-start(bf16[2,2,32,2048]{3,2,1,0:T(8,128)(2,1)S(1)} %fusion.22), channel_id=1, source_target_pairs={{0,16},{4,20},{8,24},{12,28},{16,0},{20,4},{24,8},{28,12},{1,17},{... | collective-permute-start | bytes 1572872 | tf_op jit(solution)/shard_map/ppermute | solution.py:37
  69.6 1.5 collective-permute-start.7
  71.1 9.6 %collective-permute-done.10 = bf16[2,2,32,2048]{3,2,1,0:T(8,128)(2,1)S(1)} collective-permute-done((bf16[2,2,32,2048]{3,2,1,0:T(8,128)(2,1)S(1)}, bf16[2,2,32,2048]{3,2,1,0:T(8,128)(2,1)S(1)}, u32[]{:S(2)}, u32[]{:S(2)}) %collective-permute-start.10) | collective-permute-done | bytes 524320 | tf_op jit(solution)/shard_map/ppermute | solution.py:37
  80.9 1.7 %collective-permute-start.11 = (bf16[1,2,32,2048]{3,2,1,0:T(8,128)(2,1)S(1)}, bf16[1,2,32,2048]{3,2,1,0:T(8,128)(2,1)S(1)}, u32[]{:S(2)}, u32[]{:S(2)}) collective-permute-start(bf16[1,2,32,2048]{3,2,1,0:T(8,128)(2,1)S(1)} %fusion.28), channel_id=1, source_target_pairs={{0,8},{4,12},{8,0},{12,4},{16,24},{20,28},{24,16},{28,20},{1,9},{5... | collective-permute-start | bytes 786440 | tf_op jit(solution)/shard_map/ppermute | solution.py:37
  82.6 0.5 collective-permute-done.7
  83.3 1.0 collective-permute-start.8
  84.4 3.8 %collective-permute-done.11 = bf16[1,2,32,2048]{3,2,1,0:T(8,128)(2,1)S(1)} collective-permute-done((bf16[1,2,32,2048]{3,2,1,0:T(8,128)(2,1)S(1)}, bf16[1,2,32,2048]{3,2,1,0:T(8,128)(2,1)S(1)}, u32[]{:S(2)}, u32[]{:S(2)}) %collective-permute-start.11) | collective-permute-done | bytes 262176 | tf_op jit(solution)/shard_map/ppermute | solution.py:37
  88.2 1.5 collective-permute-done.8
  89.8 1.3 fusion.7
  91.5 3.2 %collective-permute-start.12 = (f32[2,4,32]{2,1,0:T(4,128)S(1)}, f32[2,4,32]{2,1,0:T(4,128)S(1)}, u32[]{:S(2)}, u32[]{:S(2)}) collective-permute-start(f32[2,4,32]{2,1,0:T(4,128)S(1)} %get-tuple-element.49), channel_id=1, source_target_pairs={{0,1},{1,0},{2,3},{3,2},{4,5},{5,4},{6,7},{7,6},{8,9},{9,8},{10,11... | collective-permute-start | bytes 3080 | tf_op jit(solution)/shard_map/ppermute | solution.py:42
  94.6 1.3 collective-permute-start.14
  96.2 3.8 %collective-permute-done.14 = f32[2,4,32]{2,1,0:T(4,128)S(1)} collective-permute-done((f32[2,4,32]{2,1,0:T(4,128)S(1)}, f32[2,4,32]{2,1,0:T(4,128)S(1)}, u32[]{:S(2)}, u32[]{:S(2)}) %collective-permute-start.14) | collective-permute-done | bytes 1056 | tf_op jit(solution)/shard_map/ppermute | solution.py:42
  100.2 1.6 %fusion.5 = (f32[2048]{0:T(1024)S(1)}, bf16[128,2048]{1,0:T(8,128)(2,1)S(1)}) fusion(f32[128,2048]{1,0:T(8,128)} %get-tuple-element.57, f32[128]{0:T(128)S(1)} %rsqrt.14, bf16[64,2048]{1,0:T(8,128)(2,1)S(1)} %bitcast.116, bf16[64,2048]{1,0:T(8,128)(2,1)S(1)} %bitcast.118, f32[128]{0:T(128)S(1)} %multiply_multiply_fusion, f32[2048]{0:T(1024)S(1)} %dynamic_slice.3), kind=kLoop, calls=%fused_computation.13 | loop fusion | flops 3143680 | bytes 2114560 | tf_op jit(solution)/shard_map/reduce_sum | solution.py:369
  101.9 2.1 %concatenate.31.refs_3_ = bf16[136,2048]{1,0:T(8,128)(2,1)} concatenate(bf16[128,2048]{1,0:T(8,128)(2,1)S(1)} %get-tuple-element.29, bf16[1,2048]{1,0:T(2,128)(2,1)S(1)} %get-tuple-element.46, bf16[1,2048]{1,0:T(2,128)(2,1)S(1)} %get-tuple-element.45, bf16[1,2048]{1,0:T(2,128)(2,1)S(1)} %get-tuple-element.44, bf16[1,2048]{1,0:T(2,128)(2,1)S(1)} %get-tuple-element.58, ...), dimensions={0} | concatenate | bytes 1114112 | tf_op jit(solution)/shard_map/concatenate | solution.py:375
  104.1 0.9 collective-permute-start.16
  105.0 0.6 collective-permute-start.15
  105.7 0.9 copy-done.7
  106.6 0.9 copy-done.9
  107.6 0.9 copy-done.11
  108.5 0.7 regroup.1
  109.2 0.6 copy-done.12
  109.8 0.6 copy-done.14
  110.5 3.4 %collective-permute-done.16.refs_4_ = bf16[136,2048]{1,0:T(8,128)(2,1)S(1)} collective-permute-done((bf16[136,2048]{1,0:T(8,128)(2,1)}, bf16[136,2048]{1,0:T(8,128)(2,1)S(1)}, u32[]{:S(2)}, u32[]{:S(2)}) %collective-permute-start.16) | collective-permute-done | bytes 557088 | tf_op jit(solution)/shard_map/ppermute | solution.py:37
  113.9 2.4 %collective-permute-done.15.refs_3_ = bf16[136,2048]{1,0:T(8,128)(2,1)S(1)} collective-permute-done((bf16[136,2048]{1,0:T(8,128)(2,1)}, bf16[136,2048]{1,0:T(8,128)(2,1)S(1)}, u32[]{:S(2)}, u32[]{:S(2)}) %collective-permute-start.15) | collective-permute-done | bytes 557088 | tf_op jit(solution)/shard_map/ppermute | solution.py:37
  116.6 6.4 %quantized_sum.4.refs_5_ = f32[400,2048]{1,0:T(8,128)S(1)} custom-call(bf16[400,128]{1,0:T(8,128)(2,1)S(1)} %get-tuple-element.24.refs_0_, bf16[400,128]{1,0:T(8,128)(2,1)S(1)} %get-tuple-element.25.refs_1_, f32[400,128]{1,0:T(8,128)S(1)} %get-tuple-element.18.refs_2_, bf16[136,2048]{1,0:T(8,128)(2,1)} %concatenate.31.refs_3_, ...), custom_call_target="tpu_custom_call" | custom-call | flops 1966080000 | tf_op jit(solution)/shard_map/quantized_sum/pallas_call | solution.py:205
  123.0 0.6 collective-permute-start.19
  123.6 7.7 %quantized_sum.5.refs_5_ = f32[400,2048]{1,0:T(8,128)S(1)} custom-call(bf16[400,128]{1,0:T(8,128)(2,1)S(1)} %get-tuple-element.22.refs_0_, bf16[400,128]{1,0:T(8,128)(2,1)S(1)} %get-tuple-element.23.refs_1_, f32[400,128]{1,0:T(8,128)S(1)} %get-tuple-element.18.refs_2_, ...), custom_call_target="tpu_custom_call", output_to_operand_aliasing={{}: (5, {})} | custom-call | flops 1966080000 | tf_op jit(solution)/shard_map/quantized_sum/pallas_call | solution.py:205
  131.5 7.5 %quantized_sum.6.refs_5_ = f32[400,2048]{1,0:T(8,128)S(1)} custom-call(bf16[400,128]{1,0:T(8,128)(2,1)S(1)} %get-tuple-element.20.refs_0_, bf16[400,128]{1,0:T(8,128)(2,1)S(1)} %get-tuple-element.21.refs_1_, f32[400,128]{1,0:T(8,128)S(1)} %get-tuple-element.18.refs_2_, ...), custom_call_target="tpu_custom_call", output_to_operand_aliasing={{}: (5, {})} | custom-call | flops 1966080000 | tf_op jit(solution)/shard_map/quantized_sum/pallas_call | solution.py:205
  139.0 1.7 %copy-done.1 = f32[400,2048]{1,0:T(8,128)} copy-done((f32[400,2048]{1,0:T(8,128)}, f32[400,2048]{1,0:T(8,128)S(1)}, u32[]{:S(2)}) %copy-start.1) | copy-done | bytes 3276824
  140.8 0.8 copy-done.3
  141.6 1.4 collective-permute-start.24
  143.0 3.0 %collective-permute-start.22 = (f32[8,256]{1,0:T(8,128)S(1)}, f32[8,256]{1,0:T(8,128)S(1)}, u32[]{:S(2)}, u32[]{:S(2)}) collective-permute-start(f32[8,256]{1,0:T(8,128)S(1)} %reshape.400), channel_id=1, source_target_pairs={{0,1},{1,0},{2,3},{3,2},{4,5},{5,4},{6,7},{7,6},{8,9},{9,8},{10,11... | collective-permute-start | bytes 24584 | tf_op jit(solution)/shard_map/ppermute | solution.py:42
  146.1 1.9 %copy-done.2 = f32[400,2048]{1,0:T(8,128)S(1)} copy-done((f32[400,2048]{1,0:T(8,128)S(1)}, f32[400,2048]{1,0:T(8,128)}, u32[]{:S(2)}) %copy-start.2) | copy-done | bytes 3276824
  148.0 1.1 copy-done.4
  149.0 7.2 %quantized_sum.7 = f32[400,2048]{1,0:T(8,128)} custom-call(bf16[400,128]{1,0:T(8,128)(2,1)S(1)} %copy-done.13, bf16[400,128]{1,0:T(8,128)(2,1)S(1)} %copy-done.15, f32[400,128]{1,0:T(8,128)S(1)} %get-tuple-element.18.refs_2_, bf16[136,2048]{1,0:T(8,128)(2,1)S(1)} %collective-permute-done.17.refs_3_, bf16[136,2048]{1,0:T(8,128)(2,1)S(1)} %copy-done.4, ...), custom_call_target="tpu_custom_call" | custom-call | flops 1966080000 | tf_op jit(solution)/shard_map/quantized_sum/pallas_call | solution.py:205
  156.3 0.6 gather_fusion
  156.9 0.6 copy.28
  (128 shorter events, 4.2 us)
Async XLA Ops:
  0.6 39.4 %copy-start = (bf16[400,2048]{1,0:T(8,128)(2,1)S(1)}, bf16[400,2048]{1,0:T(8,128)(2,1)}, u32[]{:S(2)}) copy-start(bf16[400,2048]{1,0:T(8,128)(2,1)} %param.10) | copy-start | bytes 4915204
  0.6 1.1 copy-start.5
  1.7 0.7 copy-start.16
  2.4 0.7 copy-start.17
  4.0 13.5 %all-to-all-start = ((bf16[8,48,400]{2,1,0:T(8,128)(2,1)}), bf16[8,48,400]{2,1,0:T(8,128)(2,1)S(1)}, u32[]{:S(2)}, u32[]{:S(2)}) async-start(bf16[8,48,400]{2,1,0:T(8,128)(2,1)} %pack.1), calls=%async_computation | async-start | bytes 786432 | tf_op jit(solution)/shard_map/all_to_all | solution.py:272
  11.8 0.7 copy-start.18
  12.5 1.6 %copy-start.19 = (bf16[1,128,8192]{2,1,0:T(8,128)(2,1)S(1)}, bf16[1,128,8192]{2,1,0:T(8,128)(2,1)}, u32[]{:S(2)}) copy-start(bf16[1,128,8192]{2,1,0:T(8,128)(2,1)} %param.11) | copy-start | bytes 6291460
  14.1 1.6 %copy-start.20 = (bf16[1,128,8192]{2,1,0:T(8,128)(2,1)S(1)}, bf16[1,128,8192]{2,1,0:T(8,128)(2,1)}, u32[]{:S(2)}) copy-start(bf16[1,128,8192]{2,1,0:T(8,128)(2,1)} %param.12) | copy-start | bytes 6291460
  17.8 10.0 %collective-permute-start.2 = (bf16[400,256]{1,0:T(8,128)(2,1)S(1)}, bf16[400,256]{1,0:T(8,128)(2,1)S(1)}, u32[]{:S(2)}, u32[]{:S(2)}) collective-permute-start(bf16[400,256]{1,0:T(8,128)(2,1)S(1)} %get-tuple-element.14.refs_0_), channel_id=1, source_target_pairs={{0,3},{1,2},{2,1},{3,0},{4,7},{5,6},{6,5},{7,4},{8,11},{9,10},{10,... | collective-permute-start | bytes 614408 | tf_op jit(solution)/shard_map/ppermute | solution.py:42
  21.4 17.9 %collective-permute-start.1 = (bf16[400,256]{1,0:T(8,128)(2,1)S(1)}, bf16[400,256]{1,0:T(8,128)(2,1)S(1)}, u32[]{:S(2)}, u32[]{:S(2)}) collective-permute-start(bf16[400,256]{1,0:T(8,128)(2,1)S(1)} %get-tuple-element.14.refs_0_), channel_id=1, source_target_pairs={{0,2},{1,3},{2,0},{3,1},{4,6},{5,7},{6,4},{7,5},{8,10},{9,11},{10,... | collective-permute-start | bytes 614408 | tf_op jit(solution)/shard_map/ppermute | solution.py:42
  21.4 19.4 %collective-permute-start = (bf16[400,256]{1,0:T(8,128)(2,1)S(1)}, bf16[400,256]{1,0:T(8,128)(2,1)S(1)}, u32[]{:S(2)}, u32[]{:S(2)}) collective-permute-start(bf16[400,256]{1,0:T(8,128)(2,1)S(1)} %get-tuple-element.14.refs_0_), channel_id=1, source_target_pairs={{0,1},{1,0},{2,3},{3,2},{4,5},{5,4},{6,7},{7,6},{8,9},{9,8},{10,11... | collective-permute-start | bytes 614408 | tf_op jit(solution)/shard_map/ppermute | solution.py:42
  27.7 11.6 %copy-start.6 = (bf16[400,256]{1,0:T(8,128)(2,1)}, bf16[400,256]{1,0:T(8,128)(2,1)S(1)}, u32[]{:S(2)}) copy-start(bf16[400,256]{1,0:T(8,128)(2,1)S(1)} %collective-permute-done.2.refs_3_) | copy-start | bytes 614404
  39.3 0.7 copy-start.8
  40.8 25.8 %collective-permute-start.9 = (bf16[4,2,32,2048]{3,2,0,1:T(8,128)(2,1)S(1)}, bf16[4,2,32,2048]{3,2,0,1:T(8,128)(2,1)S(1)}, u32[]{:S(2)}, u32[]{:S(2)}) collective-permute-start(bf16[4,2,32,2048]{3,2,0,1:T(8,128)(2,1)S(1)} %bitcast.114), channel_id=1, source_target_pairs={{0,4},{4,0},{8,12},{12,8},{16,20},{20,16},{24,28},{28,24},{1,5},{5... | collective-permute-start | bytes 3145736 | tf_op jit(solution)/shard_map/ppermute | solution.py:37
  40.9 1.5 copy-start.10
  42.5 8.1 %collective-permute-start.3 = (bf16[56,2048]{1,0:T(8,128)(2,1)S(1)}, bf16[56,2048]{1,0:T(8,128)(2,1)S(1)}, u32[]{:S(2)}, u32[]{:S(2)}) collective-permute-start(bf16[56,2048]{1,0:T(8,128)(2,1)S(1)} %get-tuple-element.30), channel_id=1, source_target_pairs={{0,1},{1,0},{2,3},{3,2},{4,5},{5,4},{6,7},{7,6},{8,9},{9,8},{10,11... | collective-permute-start | bytes 688136 | tf_op jit(solution)/shard_map/ppermute | solution.py:42
  42.6 13.9 %collective-permute-start.5 = (bf16[56,2048]{1,0:T(8,128)(2,1)S(1)}, bf16[56,2048]{1,0:T(8,128)(2,1)S(1)}, u32[]{:S(2)}, u32[]{:S(2)}) collective-permute-start(bf16[56,2048]{1,0:T(8,128)(2,1)S(1)} %get-tuple-element.31), channel_id=1, source_target_pairs={{0,3},{1,2},{2,1},{3,0},{4,7},{5,6},{6,5},{7,4},{8,11},{9,10},{10,... | collective-permute-start | bytes 688136 | tf_op jit(solution)/shard_map/ppermute | solution.py:42
  45.1 21.4 %collective-permute-start.4 = (bf16[56,2048]{1,0:T(8,128)(2,1)S(1)}, bf16[56,2048]{1,0:T(8,128)(2,1)S(1)}, u32[]{:S(2)}, u32[]{:S(2)}) collective-permute-start(bf16[56,2048]{1,0:T(8,128)(2,1)S(1)} %get-tuple-element.32), channel_id=1, source_target_pairs={{0,2},{1,3},{2,0},{3,1},{4,6},{5,7},{6,4},{7,5},{8,10},{9,11},{10,... | collective-permute-start | bytes 688136 | tf_op jit(solution)/shard_map/ppermute | solution.py:42
  46.1 23.1 %collective-permute-start.6 = (bf16[4,2,32,2048]{3,2,1,0:T(8,128)(2,1)S(1)}, bf16[4,2,32,2048]{3,2,1,0:T(8,128)(2,1)S(1)}, u32[]{:S(2)}, u32[]{:S(2)}) collective-permute-start(bf16[4,2,32,2048]{3,2,1,0:T(8,128)(2,1)S(1)} %bitcast.113), channel_id=1, source_target_pairs={{0,4},{4,0},{8,12},{12,8},{16,20},{20,16},{24,28},{28,24},{1,5},{5... | collective-permute-start | bytes 3145736 | tf_op jit(solution)/shard_map/ppermute | solution.py:37
  50.6 16.4 %copy-start.23 = (bf16[56,2048]{1,0:T(8,128)(2,1)}, bf16[56,2048]{1,0:T(8,128)(2,1)S(1)}, u32[]{:S(2)}) copy-start(bf16[56,2048]{1,0:T(8,128)(2,1)S(1)} %collective-permute-done.3) | copy-start | bytes 688132
  56.5 10.4 %copy-start.24 = (bf16[56,2048]{1,0:T(8,128)(2,1)}, bf16[56,2048]{1,0:T(8,128)(2,1)S(1)}, u32[]{:S(2)}) copy-start(bf16[56,2048]{1,0:T(8,128)(2,1)S(1)} %collective-permute-done.5) | copy-start | bytes 688132
  66.5 0.7 copy-start.21
  67.5 13.2 %collective-permute-start.10 = (bf16[2,2,32,2048]{3,2,1,0:T(8,128)(2,1)S(1)}, bf16[2,2,32,2048]{3,2,1,0:T(8,128)(2,1)S(1)}, u32[]{:S(2)}, u32[]{:S(2)}) collective-permute-start(bf16[2,2,32,2048]{3,2,1,0:T(8,128)(2,1)S(1)} %fusion.22), channel_id=1, source_target_pairs={{0,16},{4,20},{8,24},{12,28},{16,0},{20,4},{24,8},{28,12},{1,17},{... | collective-permute-start | bytes 1572872 | tf_op jit(solution)/shard_map/ppermute | solution.py:37
  69.6 13.5 %collective-permute-start.7 = (bf16[2,2,32,2048]{3,2,1,0:T(8,128)(2,1)S(1)}, bf16[2,2,32,2048]{3,2,1,0:T(8,128)(2,1)S(1)}, u32[]{:S(2)}, u32[]{:S(2)}) collective-permute-start(bf16[2,2,32,2048]{3,2,1,0:T(8,128)(2,1)S(1)} %fusion.21), channel_id=1, source_target_pairs={{0,8},{4,12},{8,0},{12,4},{16,24},{20,28},{24,16},{28,20},{1,9},{5... | collective-permute-start | bytes 1572872 | tf_op jit(solution)/shard_map/ppermute | solution.py:37
  80.9 7.3 %collective-permute-start.11 = (bf16[1,2,32,2048]{3,2,1,0:T(8,128)(2,1)S(1)}, bf16[1,2,32,2048]{3,2,1,0:T(8,128)(2,1)S(1)}, u32[]{:S(2)}, u32[]{:S(2)}) collective-permute-start(bf16[1,2,32,2048]{3,2,1,0:T(8,128)(2,1)S(1)} %fusion.28), channel_id=1, source_target_pairs={{0,8},{4,12},{8,0},{12,4},{16,24},{20,28},{24,16},{28,20},{1,9},{5... | collective-permute-start | bytes 786440 | tf_op jit(solution)/shard_map/ppermute | solution.py:37
  83.2 6.5 %slice-start = ((bf16[56,2048]{1,0:T(8,128)(2,1)}), bf16[48,2048]{1,0:T(8,128)(2,1)S(1)}, s32[]{:S(2)}) async-start(bf16[56,2048]{1,0:T(8,128)(2,1)} %copy-done.21), calls=%async_computation.1 | async-start | bytes 393216 | tf_op jit(solution)/shard_map/slice | solution.py:349
  83.3 6.5 %slice-start.1 = ((bf16[56,2048]{1,0:T(8,128)(2,1)}), bf16[48,2048]{1,0:T(8,128)(2,1)S(1)}, s32[]{:S(2)}) async-start(bf16[56,2048]{1,0:T(8,128)(2,1)} %copy-done.23), calls=%async_computation.2 | async-start | bytes 393216 | tf_op jit(solution)/shard_map/slice | solution.py:349
  83.3 6.5 %slice-start.2 = ((bf16[56,2048]{1,0:T(8,128)(2,1)}), bf16[48,2048]{1,0:T(8,128)(2,1)S(1)}, s32[]{:S(2)}) async-start(bf16[56,2048]{1,0:T(8,128)(2,1)} %copy-done.24), calls=%async_computation.3 | async-start | bytes 393216 | tf_op jit(solution)/shard_map/slice | solution.py:349
  83.3 6.4 %collective-permute-start.8 = (bf16[1,2,32,2048]{3,2,1,0:T(8,128)(2,1)S(1)}, bf16[1,2,32,2048]{3,2,1,0:T(8,128)(2,1)S(1)}, u32[]{:S(2)}, u32[]{:S(2)}) collective-permute-start(bf16[1,2,32,2048]{3,2,1,0:T(8,128)(2,1)S(1)} %fusion.27), channel_id=1, source_target_pairs={{0,16},{4,20},{8,24},{12,28},{16,0},{20,4},{24,8},{28,12},{1,17},{... | collective-permute-start | bytes 786440 | tf_op jit(solution)/shard_map/ppermute | solution.py:37
  89.8 6.1 %copy-start.22 = (bf16[56,2048]{1,0:T(8,128)(2,1)S(1)}, bf16[56,2048]{1,0:T(8,128)(2,1)}, u32[]{:S(2)}) copy-start(bf16[56,2048]{1,0:T(8,128)(2,1)} %copy-done.21) | copy-start | bytes 688132
  91.2 10.7 %copy-start.25 = (f32[1,2048]{1,0:T(1,128)S(1)}, f32[1,2048]{1,0:T(1,128)}, u32[]{:S(2)}) copy-start(f32[1,2048]{1,0:T(1,128)} %param.17) | copy-start | bytes 24580
  91.4 4.6 %collective-permute-start.13 = (f32[2,4,32]{2,1,0:T(4,128)S(1)}, f32[2,4,32]{2,1,0:T(4,128)S(1)}, u32[]{:S(2)}, u32[]{:S(2)}) collective-permute-start(f32[2,4,32]{2,1,0:T(4,128)S(1)} %pad_maximum_fusion.3), channel_id=1, source_target_pairs={{0,2},{1,3},{2,0},{3,1},{4,6},{5,7},{6,4},{7,5},{8,10},{9,11},{10,... | collective-permute-start | bytes 3080 | tf_op jit(solution)/shard_map/ppermute | solution.py:42
  91.5 4.7 %collective-permute-start.12 = (f32[2,4,32]{2,1,0:T(4,128)S(1)}, f32[2,4,32]{2,1,0:T(4,128)S(1)}, u32[]{:S(2)}, u32[]{:S(2)}) collective-permute-start(f32[2,4,32]{2,1,0:T(4,128)S(1)} %get-tuple-element.49), channel_id=1, source_target_pairs={{0,1},{1,0},{2,3},{3,2},{4,5},{5,4},{6,7},{7,6},{8,9},{9,8},{10,11... | collective-permute-start | bytes 3080 | tf_op jit(solution)/shard_map/ppermute | solution.py:42
  94.6 5.4 %collective-permute-start.14 = (f32[2,4,32]{2,1,0:T(4,128)S(1)}, f32[2,4,32]{2,1,0:T(4,128)S(1)}, u32[]{:S(2)}, u32[]{:S(2)}) collective-permute-start(f32[2,4,32]{2,1,0:T(4,128)S(1)} %get-tuple-element.50), channel_id=1, source_target_pairs={{0,3},{1,2},{2,1},{3,0},{4,7},{5,6},{6,5},{7,4},{8,11},{9,10},{10,... | collective-permute-start | bytes 3080 | tf_op jit(solution)/shard_map/ppermute | solution.py:42
  104.1 9.8 %collective-permute-start.16 = (bf16[136,2048]{1,0:T(8,128)(2,1)}, bf16[136,2048]{1,0:T(8,128)(2,1)S(1)}, u32[]{:S(2)}, u32[]{:S(2)}) collective-permute-start(bf16[136,2048]{1,0:T(8,128)(2,1)} %concatenate.31.refs_3_), channel_id=1, source_target_pairs={{0,16},{4,20},{8,24},{12,28},{16,0},{20,4},{24,8},{28,12},{1,17},{... | collective-permute-start | bytes 1671176 | tf_op jit(solution)/shard_map/ppermute | solution.py:37
  105.0 11.4 %collective-permute-start.15 = (bf16[136,2048]{1,0:T(8,128)(2,1)}, bf16[136,2048]{1,0:T(8,128)(2,1)S(1)}, u32[]{:S(2)}, u32[]{:S(2)}) collective-permute-start(bf16[136,2048]{1,0:T(8,128)(2,1)} %concatenate.31.refs_3_), channel_id=1, source_target_pairs={{0,8},{4,12},{8,0},{12,4},{16,24},{20,28},{24,16},{28,20},{1,9},{5... | collective-permute-start | bytes 1671176 | tf_op jit(solution)/shard_map/ppermute | solution.py:37
  105.6 10.9 %collective-permute-start.21 = (bf16[136,2048]{1,0:T(8,128)(2,1)}, bf16[136,2048]{1,0:T(8,128)(2,1)S(1)}, u32[]{:S(2)}, u32[]{:S(2)}) collective-permute-start(bf16[136,2048]{1,0:T(8,128)(2,1)} %concatenate.31.refs_3_), channel_id=1, source_target_pairs={{0,4},{4,0},{8,12},{12,8},{16,20},{20,16},{24,28},{28,24},{1,5},{5... | collective-permute-start | bytes 1671176 | tf_op jit(solution)/shard_map/ppermute | solution.py:37
  105.7 0.9 copy-start.7
  106.6 0.9 copy-start.9
  107.6 0.9 copy-start.11
  109.2 0.6 copy-start.12
  109.8 0.6 copy-start.14
  116.4 14.9 %collective-permute-start.17 = (bf16[136,2048]{1,0:T(8,128)(2,1)S(1)}, bf16[136,2048]{1,0:T(8,128)(2,1)S(1)}, u32[]{:S(2)}, u32[]{:S(2)}) collective-permute-start(bf16[136,2048]{1,0:T(8,128)(2,1)S(1)} %broadcast_select_fusion), channel_id=1, source_target_pairs={{0,16},{4,12},{8,24},{12,4},{16,0},{20,28},{24,8},{28,20},{1,17},{... | collective-permute-start | bytes 1671176 | tf_op jit(solution)/shard_map/ppermute | solution.py:397
  116.5 14.9 %collective-permute-start.20 = (bf16[136,2048]{1,0:T(8,128)(2,1)S(1)}, bf16[136,2048]{1,0:T(8,128)(2,1)S(1)}, u32[]{:S(2)}, u32[]{:S(2)}) collective-permute-start(bf16[136,2048]{1,0:T(8,128)(2,1)S(1)} %collective-permute-done.16.refs_4_), channel_id=1, source_target_pairs={{0,4},{4,0},{8,12},{12,8},{16,20},{20,16},{24,28},{28,24},{1,5},{5... | collective-permute-start | bytes 1671176 | tf_op jit(solution)/shard_map/ppermute | solution.py:37
  123.0 8.4 %collective-permute-start.19 = (bf16[136,2048]{1,0:T(8,128)(2,1)S(1)}, bf16[136,2048]{1,0:T(8,128)(2,1)S(1)}, u32[]{:S(2)}, u32[]{:S(2)}) collective-permute-start(bf16[136,2048]{1,0:T(8,128)(2,1)S(1)} %collective-permute-done.15.refs_3_), channel_id=1, source_target_pairs={{0,4},{4,0},{8,12},{12,8},{16,20},{20,16},{24,28},{28,24},{1,5},{5... | collective-permute-start | bytes 1671176 | tf_op jit(solution)/shard_map/ppermute | solution.py:37
  131.3 9.5 %collective-permute-start.18 = (bf16[136,2048]{1,0:T(8,128)(2,1)S(1)}, bf16[136,2048]{1,0:T(8,128)(2,1)S(1)}, u32[]{:S(2)}, u32[]{:S(2)}) collective-permute-start(bf16[136,2048]{1,0:T(8,128)(2,1)S(1)} %collective-permute-done.17.refs_3_), channel_id=1, source_target_pairs={{0,4},{4,0},{8,12},{12,8},{16,20},{20,16},{24,28},{28,24},{1,5},{5... | collective-permute-start | bytes 1671176 | tf_op jit(solution)/shard_map/ppermute | solution.py:37
  131.5 14.6 %copy-start.13 = (bf16[400,128]{1,0:T(8,128)(2,1)S(1)}, bf16[400,128]{1,0:T(8,128)(2,1)}, u32[]{:S(2)}) copy-start(bf16[400,128]{1,0:T(8,128)(2,1)} %copy-done.12) | copy-start | bytes 307204
  131.5 14.6 %copy-start.15 = (bf16[400,128]{1,0:T(8,128)(2,1)S(1)}, bf16[400,128]{1,0:T(8,128)(2,1)}, u32[]{:S(2)}) copy-start(bf16[400,128]{1,0:T(8,128)(2,1)} %copy-done.14) | copy-start | bytes 307204
  139.0 1.7 %copy-start.1 = (f32[400,2048]{1,0:T(8,128)}, f32[400,2048]{1,0:T(8,128)S(1)}, u32[]{:S(2)}) copy-start(f32[400,2048]{1,0:T(8,128)S(1)} %quantized_sum.6.refs_5_) | copy-start | bytes 9830404
  140.7 0.8 copy-start.3
  141.6 14.6 %collective-permute-start.24 = (f32[8,256]{1,0:T(8,128)S(1)}, f32[8,256]{1,0:T(8,128)S(1)}, u32[]{:S(2)}, u32[]{:S(2)}) collective-permute-start(f32[8,256]{1,0:T(8,128)S(1)} %reshape.400), channel_id=1, source_target_pairs={{0,3},{1,2},{2,1},{3,0},{4,7},{5,6},{6,5},{7,4},{8,11},{9,10},{10,... | collective-permute-start | bytes 24584 | tf_op jit(solution)/shard_map/ppermute | solution.py:42
  143.0 13.2 %collective-permute-start.23 = (f32[8,256]{1,0:T(8,128)S(1)}, f32[8,256]{1,0:T(8,128)S(1)}, u32[]{:S(2)}, u32[]{:S(2)}) collective-permute-start(f32[8,256]{1,0:T(8,128)S(1)} %reshape.400), channel_id=1, source_target_pairs={{0,2},{1,3},{2,0},{3,1},{4,6},{5,7},{6,4},{7,5},{8,10},{9,11},{10,... | collective-permute-start | bytes 24584 | tf_op jit(solution)/shard_map/ppermute | solution.py:42
  143.0 13.2 %collective-permute-start.22 = (f32[8,256]{1,0:T(8,128)S(1)}, f32[8,256]{1,0:T(8,128)S(1)}, u32[]{:S(2)}, u32[]{:S(2)}) collective-permute-start(f32[8,256]{1,0:T(8,128)S(1)} %reshape.400), channel_id=1, source_target_pairs={{0,1},{1,0},{2,3},{3,2},{4,5},{5,4},{6,7},{7,6},{8,9},{9,8},{10,11... | collective-permute-start | bytes 24584 | tf_op jit(solution)/shard_map/ppermute | solution.py:42
  146.1 1.9 %copy-start.2 = (f32[400,2048]{1,0:T(8,128)S(1)}, f32[400,2048]{1,0:T(8,128)}, u32[]{:S(2)}) copy-start(f32[400,2048]{1,0:T(8,128)} %copy-done.1) | copy-start | bytes 9830404
  148.0 1.1 copy-start.4

commit v2 on v1

--- a/solution.py
+++ b/solution.py
@@ -35,6 +35,25 @@
 def flip(value, bit):
     count = lax.axis_size("dp")
     return lax.ppermute(value, "dp", [(i, i ^ (1 << bit)) for i in range(count)])
+
+
+def exchanged_label(label, levels):
+    upper = levels - 1
+    if upper % 2:
+        return label
+    half = upper // 2
+    mask = (1 << half) - 1
+    first, second = (label >> 1) & mask, (label >> (1 + half)) & mask
+    return (label & 1) | (second << 1) | (first << (1 + half))
+
+
+def flip_label(value, bit):
+    count = lax.axis_size("dp")
+    levels = count.bit_length() - 1
+    odd = exchanged_label(1 << bit, levels)
+    return lax.ppermute(
+        value, "dp", [(i, i ^ (odd if i % 2 else 1 << bit)) for i in range(count)]
+    )
 
 
 def swap(value, step):
@@ -79,10 +98,13 @@
     replicas, rows, width = in_ref.shape
     tokens = rows - META_ROWS
     kept = tile_ref.shape[0]
+    levels = replicas.bit_length() - 1
+    core = place_ref[0] & 1
     tile_scratch[...] = jnp.zeros_like(tile_scratch)
     meta_scratch[...] = jnp.zeros_like(meta_scratch)
     for slot, relative in enumerate(order):
-        block = in_ref[place_ref[0] ^ relative].astype(FLOAT)
+        other = exchanged_label(relative, levels)
+        block = in_ref[place_ref[0] ^ (relative + core * (other - relative))].astype(FLOAT)
         tile_scratch[slot * tokens : (slot + 1) * tokens, :width] = block[:tokens]
         meta = block[tokens:]
         meta_scratch[relative : relative + 1, :width] = meta[0:1]
@@ -94,10 +116,13 @@
 
 
 def regroup_kernel(order, tokens, *refs):
-    count = len(refs) - len(order)
+    out_ref = refs[-1]
+    total = tokens * (len(refs) - 1)
     for slot, relative in enumerate(order):
         cut = slice(slot * tokens, (slot + 1) * tokens)
-        refs[count + relative][...] = jnp.concatenate([ref[:, cut] for ref in refs[:count]], axis=1)
+        out_ref[:, relative * total : (relative + 1) * total] = jnp.concatenate(
+            [ref[:, cut] for ref in refs[:-1]], axis=1
+        )
 
 
 def text_kernel(place_ref, row_ref, column_ref, text_ref, cot_ref, out_ref):
@@ -138,20 +163,21 @@
 
 def quantize_kernel(slots, replicas, adds, *refs):
     count = len(slots)
-    tile_refs = refs[:count]
-    meta_ref = refs[count]
-    loads = refs[count + 1 : 2 * count + 1]
-    total_ref = refs[2 * count + 1] if adds else None
+    tile_ref, meta_ref = refs[:2]
+    loads = refs[2 : count + 2]
+    total_ref = refs[count + 2] if adds else None
     out_ref, gradient, half_draw, row_half, lever, weight = refs[-6:]
     rows, columns = out_ref.shape
-    tokens = tile_refs[0].shape[1]
+    tokens = tile_ref.shape[1] // replicas
     groups = rows // 8
     strips = [slice(at, at + 128) for at in range(0, columns, 128)]
     unroll = 5 if groups % 5 == 0 else 2
     for index, relative in enumerate(slots):
         load = loads[index]
         gradient[...] = jnp.dot(
-            tile_refs[index][...], load[:tokens, :], preferred_element_type=FLOAT
+            tile_ref[:, relative * tokens : (relative + 1) * tokens],
+            load[:tokens, :],
+            preferred_element_type=FLOAT,
         )
         extra = load[tokens:, :].astype(FLOAT)
         draw = 0.5 * (extra[3:4] + extra[4:5] + extra[5:6])
@@ -198,13 +224,22 @@
         lax.fori_loop(0, groups, group, 0, unroll=unroll)
 
 
-def quantized_sum(tiles, meta, loads, slots, replicas, total, last):
-    rows, _ = tiles[0].shape
+def gain_kernel(replicas, *refs):
+    tokens = refs[0].shape[0] - EXTRA_ROWS
+    total = jnp.zeros(refs[-1].shape, FLOAT)
+    for ref in refs[:-1]:
+        extra = ref[tokens:, :].astype(FLOAT)
+        total = total + (extra[0:1] + extra[1:2] + extra[2:3])
+    refs[-1][...] = total / replicas
+
+
+def quantized_sum(tiles, meta, loads, slots, replicas, total):
+    rows = tiles.shape[0]
     columns = loads[0].shape[1]
     adds = total is not None
     return pl.pallas_call(
         functools.partial(quantize_kernel, slots, replicas, adds),
-        in_specs=[whole()] * (2 * len(slots) + 1 + adds),
+        in_specs=[whole()] * (len(slots) + 2 + adds),
         out_specs=whole(),
         out_shape=jax.ShapeDtypeStruct((rows, columns), FLOAT),
         scratch_shapes=[
@@ -214,13 +249,12 @@
             pltpu.VMEM((rows, 128), FLOAT),
             pltpu.VMEM((rows, 128), FLOAT),
         ],
-        input_output_aliases={2 * len(slots) + 1: 0} if adds and not last else {},
         compiler_params=grant(12),
         cost_estimate=pl.CostEstimate(
             flops=len(slots) * rows * columns * 1200, bytes_accessed=0, transcendentals=0
         ),
         name="quantized_sum",
-    )(*[tiles[slot] for slot in slots], meta, *loads, *([total] if adds else []))
+    )(tiles, meta, *loads, *([total] if adds else []))
 
 
 def stack_blocks(stats, step):
@@ -257,7 +291,8 @@
     tile_rows, _ = tile_tokens.shape[1:]
     width, columns = proj_weight.shape
     padded = -(-width // 16) * 16
-    order = tuple(range(0, replicas, 2)) + tuple(range(1, replicas, 2))
+    kept_labels = tuple(range(0, replicas, 2))
+    order = kept_labels + tuple(exchanged_label(label, levels_of_bits) ^ 1 for label in kept_labels)
     here = replica.astype(jnp.int32).reshape(1)
     there = seq_index.astype(jnp.int32).reshape(1)
 
@@ -300,22 +335,13 @@
         compiler_params=grant(16),
         name="text_part",
     )(there, placeholders, places.reshape(image_total, 1), text_hidden[0], cotangent[0])
-    outgoing, last = lax.optimization_barrier((outgoing, tile_blocks[-1]))
-    tile_blocks[-1] = last
-    returned = [outgoing[0]]
-    for step in range(1, seq_count):
-        returned.append(swap(outgoing[step], step))
 
     weight = jnp.pad(proj_weight, ((0, padded - width), (0, 0)))
     even = (replicas // 2) * tile_rows
     split = seq_count // 2
-    bit_orders = (
-        tuple(range(1, levels_of_bits)),
-        tuple(reversed(range(1, levels_of_bits))),
-    )
-    parts = (tile_blocks[:split], tile_blocks[split:])
+    parts = [tile_blocks[:split]] + [[block] for block in tile_blocks[split:]]
     embedded_parts = []
-    for group, bits in zip(parts, bit_orders):
+    for part, group in enumerate(parts):
 
         def product(cut, kind):
             left = jnp.concatenate([block[:, cut] for block in group], axis=1)
@@ -327,15 +353,20 @@
 
         sent = product(slice(even, 2 * even), HALF)
         held = product(slice(0, even), FLOAT)
+        if part == 0:
+            outgoing, sent = lax.optimization_barrier((outgoing, sent))
+            returned = [outgoing[0]]
+            for step in range(1, seq_count):
+                returned.append(swap(outgoing[step], step))
         arrived = flip(sent, 0)
         remaining = list(range(1, levels_of_bits))
-        for bit in bits:
+        for bit in range(1, levels_of_bits):
             stride = 1 << remaining.index(bit)
             remaining.remove(bit)
             held = held + arrived.astype(FLOAT)
             sent = half_of(held, stride, 1).astype(HALF)
             held = half_of(held, stride, 0)
-            arrived = flip(sent, bit)
+            arrived = flip_label(sent, bit)
         held = held + arrived.astype(FLOAT)
         embedded_parts.append(held.reshape(-1, columns))
     emb_float = jnp.concatenate(embedded_parts, axis=0).astype(HALF).astype(FLOAT)
@@ -377,8 +408,8 @@
     tiles = pl.pallas_call(
         functools.partial(regroup_kernel, order, tile_rows),
         in_specs=[whole()] * seq_count,
-        out_specs=[whole()] * replicas,
-        out_shape=[jax.ShapeDtypeStruct((padded, image_total), HALF)] * replicas,
+        out_specs=whole(),
+        out_shape=jax.ShapeDtypeStruct((padded, replicas * image_total), HALF),
         cost_estimate=pl.CostEstimate(
             flops=replicas * padded * image_total * 2000, bytes_accessed=0, transcendentals=0
         ),
@@ -389,28 +420,35 @@
     loads = {0: own_load}
     if levels_of_bits == 3:
         loads[1] = flip(own_load, 0)
-        loads[2] = flip(own_load, 1)
-        loads[4] = flip(own_load, 2)
-        is_low = (replica & 1) == 0
-        passed = jnp.where(is_low, loads[2], loads[4])
-        pairs = [(i, i ^ (4 if i % 2 == 0 else 2)) for i in range(replicas)]
-        loads[6] = lax.ppermute(passed, "dp", pairs)
-        for slot in (2, 4, 6):
-            loads[slot + 1] = flip(loads[slot], 0)
-        batches = ((0, 1), (2, 4), (3, 5), (6, 7))
+        loads[2] = flip_label(own_load, 1)
+        loads[5] = flip(loads[2], 0)
+        loads[4] = flip_label(own_load, 2)
+        loads[3] = flip(loads[4], 0)
+        loads[6] = flip_label(loads[2], 2)
+        loads[7] = flip(loads[6], 0)
+        batches = ((0, 1), (2, 5), (4,), (3, 6), (7,))
     else:
-        for bit in tuple(range(1, levels_of_bits)) + (0,):
-            loads.update({slot ^ (1 << bit): flip(load, bit) for slot, load in list(loads.items())})
+        for bit in range(1, levels_of_bits):
+            for slot, load in list(loads.items()):
+                loads[slot ^ (1 << bit)] = flip_label(load, bit)
+        for slot, load in list(loads.items()):
+            loads[exchanged_label(slot, levels_of_bits) ^ 1] = flip(load, 0)
         batches = tuple((slot, slot + 1) for slot in range(0, replicas, 2))
+    gain_row = pl.pallas_call(
+        functools.partial(gain_kernel, replicas),
+        in_specs=[whole()] * replicas,
+        out_specs=whole(),
+        out_shape=jax.ShapeDtypeStruct((1, columns), FLOAT),
+        compiler_params=grant(12),
+        name="gain",
+    )(*[loads[slot] for slot in range(replicas)])
+    gains = [gain_row]
+    for step in range(1, seq_count):
+        gains.append(swap(gain_row, step))
     total = None
     for slots in batches:
-      total = quantized_sum(tiles, meta, [loads[slot] for slot in slots], slots, replicas, total, slots == batches[-1])
-    gain_rows = sum(
-        jnp.sum(load[image_total : image_total + 3].astype(FLOAT), axis=0) for load in loads.values()
-    )
-    gain_rows = (gain_rows / replicas).reshape(8, columns // 8)
-    gains = jnp.stack([gain_rows] + [swap(gain_rows, step) for step in range(1, seq_count)])
-    gain_total = jnp.take(gains, sources, axis=0)
+        total = quantized_sum(tiles, meta, [loads[slot] for slot in slots], slots, replicas, total)
+    gain_total = jnp.take(jnp.concatenate(gains, axis=0), sources, axis=0)
     return total[:width], gain_total.reshape(model_width)
 
 

time: 158 us -> 163 us (1.032)
  waiting for transfers between devices: 62.1 us -> 79.5 us
  local copies, waits for them, and re-layouts: 22.7 us -> 12.3 us
  Pallas kernels: 32.3 us -> 27.1 us
  starting transfers between devices: 30.5 us -> 32.4 us
    ppermute x1 -> x9, waiting for transfers between devices: 0.01 us -> 41.1 us  [flip_label(): lax.ppermute(value, 'dp', [(i, i ^ (odd if i % 2 else 1 << bit)) for i in...]
    ppermute x12 -> x7, waiting for transfers between devices: 21.2 us -> 0.02 us  [flip(): return lax.ppermute(value, 'dp', [(i, i ^ 1 << bit) for i in range(count)])]
    unnamed x54 -> x36, local copies, waits for them, and re-layouts: 17.4 us -> 7.4 us
    ppermute x1 -> x9, starting transfers between devices: 0.07 us -> 9.5 us  [flip_label(): lax.ppermute(value, 'dp', [(i, i ^ (odd if i % 2 else 1 << bit)) for i in...]
    ppermute x12 -> x7, starting transfers between devices: 8.31 us -> 0.73 us  [flip(): return lax.ppermute(value, 'dp', [(i, i ^ 1 << bit) for i in range(count)])]
    pallas_call x4 -> x5, Pallas kernels: 28.7 us -> 23.4 us  [quantized_sum(): pl.pallas_call(functools.partial(quantize_kernel, slots, replicas, adds),...]
    ppermute x12, waiting for transfers between devices: 40.8 us -> 38.5 us  [swap(): return lax.ppermute(value, 'seq', [(i, i ^ step) for i in range(count)])]
    dot_general x4 -> x6, matrix products: 2.92 us -> 3.34 us  [product(): lax.dot_general(left, weight, (((0,), (0,)), ((), ())), preferred_element...]
  transfers between devices with their start and end apart: 26 -> 29, of which waited for: 14 -> 14; matrix products, arithmetic and copies ran while one was open for 5% -> 5% of each run, Pallas kernels for 20% -> 16%
where the time goes in v2:
time: 163 us
  waiting for transfers between devices  79.5 us (49%)
  starting transfers between devices  32.4 us (20%)
  Pallas kernels  27.1 us (17%)
  local copies, waits for them, and re-layouts  12.3 us (8%)
  other arithmetic  5.53 us (3%)
  matrix products  4.68 us (3%)
    ppermute x9, waiting for transfers between devices, flip_label(): lax.ppermute(value, 'dp', [(i, i ^ (odd if i % 2 else 1 << bit)) for i in...  41.1 us
    ppermute x12, waiting for transfers between devices, swap(): return lax.ppermute(value, 'seq', [(i, i ^ step) for i in range(count)])  38.5 us
    pallas_call x5, Pallas kernels, quantized_sum(): pl.pallas_call(functools.partial(quantize_kernel, slots, replicas, adds),...  23.4 us
    ppermute x12, starting transfers between devices, swap(): return lax.ppermute(value, 'seq', [(i, i ^ step) for i in range(count)])  17 us
    ppermute x9, starting transfers between devices, flip_label(): lax.ppermute(value, 'dp', [(i, i ^ (odd if i % 2 else 1 << bit)) for i in...  9.5 us
    unnamed x36, local copies, waits for them, and re-layouts  7.4 us
    all_to_all x1, starting transfers between devices, on_device(): exchanged = lax.all_to_all(packed, 'dp', 0, 0, tiled=True)  5.2 us
    dot_general x6, matrix products, product(): lax.dot_general(left, weight, (((0,), (0,)), ((), ())), preferred_element...  3.34 us
  transfers between devices with their start and end apart: 29, of which 14 were waited for; matrix products, arithmetic and copies ran while one was open for 5% of the time, Pallas kernels for 16%

profile of v2, /device:TPU:0, one launch (start us, length us, event | category | flops | bytes accessed | tf_op | source)
XLA Modules:
  0.0 162.7 jit_solution(13177906310271721450)
XLA Ops:
  0.7 1.0 copy-done.1
  1.7 0.7 copy-done.8
  2.4 0.7 copy-done.9
  3.1 0.9 pack.1
  4.0 5.2 %all-to-all-start = ((bf16[8,48,400]{2,1,0:T(8,128)(2,1)}), bf16[8,48,400]{2,1,0:T(8,128)(2,1)S(1)}, u32[]{:S(2)}, u32[]{:S(2)}) async-start(bf16[8,48,400]{2,1,0:T(8,128)(2,1)} %pack.1), calls=%async_computation | async-start | bytes 786432 | tf_op jit(solution)/shard_map/all_to_all | solution.py:307
  9.4 0.7 fusion.51
  10.1 0.8 copy.21.column_ref
  10.8 0.8 convert_reduce_fusion.4
  11.8 0.7 dynamic_slice.3
  12.6 0.6 copy-done.10
  13.2 1.6 copy-done.11
  14.8 1.6 copy-done.12
  16.4 1.7 %text_part.1 = bf16[4,56,2048]{2,1,0:T(8,128)(2,1)S(1)} custom-call(s32[1]{0:T(128)} %bitcast.6.place_ref, s32[1,128]{1,0:T(1,128)S(1)} %copy-done.10, s32[128,1]{1,0:T(8,128)S(1)} %copy.21.column_ref, bf16[128,8192]{1,0:T(8,128)(2,1)S(1)} %bitcast.126, bf16[128,8192]{1,0:T(8,128)(2,1)S(1)} %bitcast.127), custom_call_target="tpu_custom_call" | custom-call | flops 4194304000 | tf_op jit(solution)/shard_map/text_part/pallas_call | solution.py:327
  18.1 0.2 unpack.1
  18.3 3.7 %collective-permute-start.2 = (bf16[400,256]{1,0:T(8,128)(2,1)S(1)}, bf16[400,256]{1,0:T(8,128)(2,1)S(1)}, u32[]{:S(2)}, u32[]{:S(2)}) collective-permute-start(bf16[400,256]{1,0:T(8,128)(2,1)S(1)} %get-tuple-element.6.refs_0_), channel_id=1, source_target_pairs={{0,3},{1,2},{2,1},{3,0},{4,7},{5,6},{6,5},{7,4},{8,11},{9,10},{10,... | collective-permute-start | bytes 614408 | tf_op jit(solution)/shard_map/ppermute | solution.py:61
  22.0 0.8 collective-permute-start
  22.8 13.1 %collective-permute-done.refs_1_ = bf16[400,256]{1,0:T(8,128)(2,1)S(1)} collective-permute-done((bf16[400,256]{1,0:T(8,128)(2,1)S(1)}, bf16[400,256]{1,0:T(8,128)(2,1)S(1)}, u32[]{:S(2)}, u32[]{:S(2)}) %collective-permute-start) | collective-permute-done | bytes 204832 | tf_op jit(solution)/shard_map/ppermute | solution.py:61
  35.9 0.7 convolution_convert_fusion
  36.8 0.5 convolution_convert_fusion.1
  37.4 0.7 fusion.36
  38.1 0.5 fusion.45
  38.6 1.5 collective-permute-done.1.refs_2_
  40.0 0.5 convolution_convert_fusion.2
  40.6 1.5 collective-permute-start.3
  42.1 1.1 collective-permute-start.5
  43.3 0.9 collective-permute-start.4
  44.2 0.5 fusion.48
  44.7 4.0 %collective-permute-done.3 = bf16[56,2048]{1,0:T(8,128)(2,1)S(1)} collective-permute-done((bf16[56,2048]{1,0:T(8,128)(2,1)S(1)}, bf16[56,2048]{1,0:T(8,128)(2,1)S(1)}, u32[]{:S(2)}, u32[]{:S(2)}) %collective-permute-start.3) | collective-permute-done | bytes 229408 | tf_op jit(solution)/shard_map/ppermute | solution.py:61
  48.6 6.0 %collective-permute-done.5 = bf16[56,2048]{1,0:T(8,128)(2,1)S(1)} collective-permute-done((bf16[56,2048]{1,0:T(8,128)(2,1)S(1)}, bf16[56,2048]{1,0:T(8,128)(2,1)S(1)}, u32[]{:S(2)}, u32[]{:S(2)}) %collective-permute-start.5) | collective-permute-done | bytes 229408 | tf_op jit(solution)/shard_map/ppermute | solution.py:61
  54.6 9.9 %collective-permute-done.4 = bf16[56,2048]{1,0:T(8,128)(2,1)S(1)} collective-permute-done((bf16[56,2048]{1,0:T(8,128)(2,1)S(1)}, bf16[56,2048]{1,0:T(8,128)(2,1)S(1)}, u32[]{:S(2)}, u32[]{:S(2)}) %collective-permute-start.4) | collective-permute-done | bytes 229408 | tf_op jit(solution)/shard_map/ppermute | solution.py:61
  64.8 0.4 copy-done.13
  65.3 1.6 %collective-permute-start.13 = (bf16[2,1,32,2048]{3,2,0,1:T(8,128)(2,1)S(1)}, bf16[2,1,32,2048]{3,2,0,1:T(8,128)(2,1)S(1)}, u32[]{:S(2)}, u32[]{:S(2)}) collective-permute-start(bf16[2,1,32,2048]{3,2,0,1:T(8,128)(2,1)S(1)} %fusion.28), channel_id=1, source_target_pairs={{0,8},{4,20},{8,0},{12,28},{16,24},{20,4},{24,16},{28,12},{1,9},{5... | collective-permute-start | bytes 786440 | tf_op jit(solution)/shard_map/ppermute | solution.py:54
  67.0 0.5 collective-permute-start.10
  67.5 4.1 %collective-permute-done.13 = bf16[2,1,32,2048]{3,2,0,1:T(8,128)(2,1)S(1)} collective-permute-done((bf16[2,1,32,2048]{3,2,0,1:T(8,128)(2,1)S(1)}, bf16[2,1,32,2048]{3,2,0,1:T(8,128)(2,1)S(1)}, u32[]{:S(2)}, u32[]{:S(2)}) %collective-permute-start.13) | collective-permute-done | bytes 262176 | tf_op jit(solution)/shard_map/ppermute | solution.py:54
  71.7 1.7 %collective-permute-start.14 = (bf16[1,1,32,2048]{3,2,1,0:T(8,128)(2,1)S(1)}, bf16[1,1,32,2048]{3,2,1,0:T(8,128)(2,1)S(1)}, u32[]{:S(2)}, u32[]{:S(2)}) collective-permute-start(bf16[1,1,32,2048]{3,2,1,0:T(8,128)(2,1)S(1)} %fusion.43), channel_id=1, source_target_pairs={{0,16},{4,12},{8,24},{12,4},{16,0},{20,28},{24,8},{28,20},{1,17},{... | collective-permute-start | bytes 393224 | tf_op jit(solution)/shard_map/ppermute | solution.py:54
  73.4 2.7 %collective-permute-done.10 = bf16[2,1,32,2048]{3,2,0,1:T(8,128)(2,1)S(1)} collective-permute-done((bf16[2,1,32,2048]{3,2,0,1:T(8,128)(2,1)S(1)}, bf16[2,1,32,2048]{3,2,0,1:T(8,128)(2,1)S(1)}, u32[]{:S(2)}, u32[]{:S(2)}) %collective-permute-start.10) | collective-permute-done | bytes 262176 | tf_op jit(solution)/shard_map/ppermute | solution.py:54
  76.1 1.7 %collective-permute-start.11 = (bf16[1,1,32,2048]{3,2,1,0:T(8,128)(2,1)S(1)}, bf16[1,1,32,2048]{3,2,1,0:T(8,128)(2,1)S(1)}, u32[]{:S(2)}, u32[]{:S(2)}) collective-permute-start(bf16[1,1,32,2048]{3,2,1,0:T(8,128)(2,1)S(1)} %fusion.41), channel_id=1, source_target_pairs={{0,16},{4,12},{8,24},{12,4},{16,0},{20,28},{24,8},{28,20},{1,17},{... | collective-permute-start | bytes 393224 | tf_op jit(solution)/shard_map/ppermute | solution.py:54
  77.8 0.3 bitcast_add_fusion
  78.3 1.5 collective-permute-start.7
  79.8 2.7 %collective-permute-done.11 = bf16[1,1,32,2048]{3,2,1,0:T(8,128)(2,1)S(1)} collective-permute-done((bf16[1,1,32,2048]{3,2,1,0:T(8,128)(2,1)S(1)}, bf16[1,1,32,2048]{3,2,1,0:T(8,128)(2,1)S(1)}, u32[]{:S(2)}, u32[]{:S(2)}) %collective-permute-start.11) | collective-permute-done | bytes 131104 | tf_op jit(solution)/shard_map/ppermute | solution.py:54
  82.6 5.0 %collective-permute-done.7 = bf16[2,2,32,2048]{3,2,1,0:T(8,128)(2,1)S(1)} collective-permute-done((bf16[2,2,32,2048]{3,2,1,0:T(8,128)(2,1)S(1)}, bf16[2,2,32,2048]{3,2,1,0:T(8,128)(2,1)S(1)}, u32[]{:S(2)}, u32[]{:S(2)}) %collective-permute-start.7) | collective-permute-done | bytes 524320 | tf_op jit(solution)/shard_map/ppermute | solution.py:54
  87.8 0.4 collective-permute-start.8
  88.3 5.9 %collective-permute-done.8 = bf16[1,2,32,2048]{3,2,1,0:T(8,128)(2,1)S(1)} collective-permute-done((bf16[1,2,32,2048]{3,2,1,0:T(8,128)(2,1)S(1)}, bf16[1,2,32,2048]{3,2,1,0:T(8,128)(2,1)S(1)}, u32[]{:S(2)}, u32[]{:S(2)}) %collective-permute-start.8) | collective-permute-done | bytes 262176 | tf_op jit(solution)/shard_map/ppermute | solution.py:54
  94.3 1.3 fusion.7
  96.0 3.1 %collective-permute-start.15 = (f32[2,4,32]{2,1,0:T(4,128)S(1)}, f32[2,4,32]{2,1,0:T(4,128)S(1)}, u32[]{:S(2)}, u32[]{:S(2)}) collective-permute-start(f32[2,4,32]{2,1,0:T(4,128)S(1)} %get-tuple-element.29), channel_id=1, source_target_pairs={{0,1},{1,0},{2,3},{3,2},{4,5},{5,4},{6,7},{7,6},{8,9},{9,8},{10,11... | collective-permute-start | bytes 3080 | tf_op jit(solution)/shard_map/ppermute | solution.py:61
  99.1 1.3 collective-permute-start.17
  100.5 0.2 collective-permute-done.15
  100.7 3.8 %collective-permute-done.17 = f32[2,4,32]{2,1,0:T(4,128)S(1)} collective-permute-done((f32[2,4,32]{2,1,0:T(4,128)S(1)}, f32[2,4,32]{2,1,0:T(4,128)S(1)}, u32[]{:S(2)}, u32[]{:S(2)}) %collective-permute-start.17) | collective-permute-done | bytes 1056 | tf_op jit(solution)/shard_map/ppermute | solution.py:61
  104.7 2.5 %fusion.5 = (f32[2048]{0:T(1024)S(1)}, bf16[128,2048]{1,0:T(8,128)(2,1)}) fusion(f32[128,2048]{1,0:T(8,128)} %get-tuple-element.37, f32[128]{0:T(128)S(1)} %rsqrt.14, bf16[32,2048]{1,0:T(8,128)(2,1)S(1)} %fusion.42, bf16[32,2048]{1,0:T(8,128)(2,1)S(1)} %fusion.40, bf16[64,2048]{1,0:T(8,128)(2,1)S(1)} %bitcast.141, f32[128]{0:T(128)S(1)} %multiply_multiply_fusion, ...), kind=kLoop, calls=%fused_computation.13 | loop fusion | flops 3667968 | bytes 2114560 | tf_op jit(solution)/shard_map/reduce_sum | solution.py:400
  107.2 2.0 %concatenate.25.refs_2_.refs_0_ = bf16[136,2048]{1,0:T(8,128)(2,1)S(1)} concatenate(bf16[128,2048]{1,0:T(8,128)(2,1)} %get-tuple-element.13, bf16[1,2048]{1,0:T(2,128)(2,1)S(1)} %get-tuple-element.26, bf16[1,2048]{1,0:T(2,128)(2,1)S(1)} %get-tuple-element.25, bf16[1,2048]{1,0:T(2,128)(2,1)S(1)} %get-tuple-element.24, bf16[1,2048]{1,0:T(2,128)(2,1)S(1)} %get-tuple-element.23, ...), dimensions={0} | concatenate | bytes 1114112 | tf_op jit(solution)/shard_map/concatenate | solution.py:406
  109.2 2.1 %collective-permute-start.18 = (bf16[136,2048]{1,0:T(8,128)(2,1)S(1)}, bf16[136,2048]{1,0:T(8,128)(2,1)S(1)}, u32[]{:S(2)}, u32[]{:S(2)}) collective-permute-start(bf16[136,2048]{1,0:T(8,128)(2,1)S(1)} %concatenate.25.refs_2_.refs_0_), channel_id=1, source_target_pairs={{0,8},{4,20},{8,0},{12,28},{16,24},{20,4},{24,16},{28,12},{1,9},{5... | collective-permute-start | bytes 1671176 | tf_op jit(solution)/shard_map/ppermute | solution.py:54
  111.3 12.5 %collective-permute-done.18.refs_2_ = bf16[136,2048]{1,0:T(8,128)(2,1)S(1)} collective-permute-done((bf16[136,2048]{1,0:T(8,128)(2,1)S(1)}, bf16[136,2048]{1,0:T(8,128)(2,1)S(1)}, u32[]{:S(2)}, u32[]{:S(2)}) %collective-permute-start.18) | collective-permute-done | bytes 557088 | tf_op jit(solution)/shard_map/ppermute | solution.py:54
  123.8 0.5 collective-permute-start.23
  124.5 0.7 regroup.1.refs_0_
  125.2 8.1 %collective-permute-done.19.refs_3_.refs_6_ = bf16[136,2048]{1,0:T(8,128)(2,1)S(1)} collective-permute-done((bf16[136,2048]{1,0:T(8,128)(2,1)S(1)}, bf16[136,2048]{1,0:T(8,128)(2,1)S(1)}, u32[]{:S(2)}, u32[]{:S(2)}) %collective-permute-start.19) | collective-permute-done | bytes 557088 | tf_op jit(solution)/shard_map/ppermute | solution.py:54
  133.4 5.3 %quantized_sum.5.refs_4_ = f32[400,2048]{1,0:T(8,128)S(1)} custom-call(bf16[400,1024]{1,0:T(8,128)(2,1)S(1)} %regroup.1.refs_0_, f32[400,128]{1,0:T(8,128)S(1)} %get-tuple-element.7.refs_1_, bf16[136,2048]{1,0:T(8,128)(2,1)S(1)} %concatenate.25.refs_2_.refs_0_, bf16[136,2048]{1,0:T(8,128)(2,1)S(1)} %collective-permute-done.24.refs_3_.refs_1_), custom_call_target="tpu_custom_call" | custom-call | flops 1966080000 | tf_op jit(solution)/shard_map/quantized_sum/pallas_call | solution.py:240
  138.7 5.5 %quantized_sum.6.refs_3_ = f32[400,2048]{1,0:T(8,128)S(1)} custom-call(bf16[400,1024]{1,0:T(8,128)(2,1)S(1)} %regroup.1.refs_0_, f32[400,128]{1,0:T(8,128)S(1)} %get-tuple-element.7.refs_1_, bf16[136,2048]{1,0:T(8,128)(2,1)S(1)} %collective-permute-done.18.refs_2_, bf16[136,2048]{1,0:T(8,128)(2,1)S(1)} %collective-permute-done.23.refs_3_.refs_5_, ...), custom_call_target="tpu_custom_call" | custom-call | flops 1966080000 | tf_op jit(solution)/shard_map/quantized_sum/pallas_call | solution.py:240
  144.2 2.7 %quantized_sum.7.refs_4_ = f32[400,2048]{1,0:T(8,128)S(1)} custom-call(bf16[400,1024]{1,0:T(8,128)(2,1)S(1)} %regroup.1.refs_0_, f32[400,128]{1,0:T(8,128)S(1)} %get-tuple-element.7.refs_1_, bf16[136,2048]{1,0:T(8,128)(2,1)S(1)} %collective-permute-done.21.refs_2_.refs_4_, f32[400,2048]{1,0:T(8,128)S(1)} %quantized_sum.6.refs_3_), custom_call_target="tpu_custom_call" | custom-call | flops 983040000 | tf_op jit(solution)/shard_map/quantized_sum/pallas_call | solution.py:240
  147.0 5.4 %quantized_sum.8.refs_3_ = f32[400,2048]{1,0:T(8,128)S(1)} custom-call(bf16[400,1024]{1,0:T(8,128)(2,1)S(1)} %regroup.1.refs_0_, f32[400,128]{1,0:T(8,128)S(1)} %get-tuple-element.7.refs_1_, bf16[136,2048]{1,0:T(8,128)(2,1)S(1)} %collective-permute-done.22.refs_2_.refs_3_, bf16[136,2048]{1,0:T(8,128)(2,1)S(1)} %collective-permute-done.19.refs_3_.refs_6_, ...), custom_call_target="tpu_custom_call" | custom-call | flops 1966080000 | tf_op jit(solution)/shard_map/quantized_sum/pallas_call | solution.py:240
  152.5 1.4 collective-permute-start.27
  153.9 3.0 %collective-permute-start.25 = (f32[1,2048]{1,0:T(1,128)S(1)}, f32[1,2048]{1,0:T(1,128)S(1)}, u32[]{:S(2)}, u32[]{:S(2)}) collective-permute-start(f32[1,2048]{1,0:T(1,128)S(1)} %gain.1), channel_id=1, source_target_pairs={{0,1},{1,0},{2,3},{3,2},{4,5},{5,4},{6,7},{7,6},{8,9},{9,8},{10,11... | collective-permute-start | bytes 24584 | tf_op jit(solution)/shard_map/ppermute | solution.py:61
  156.9 4.4 %quantized_sum.9 = f32[400,2048]{1,0:T(8,128)} custom-call(bf16[400,1024]{1,0:T(8,128)(2,1)S(1)} %regroup.1.refs_0_, f32[400,128]{1,0:T(8,128)S(1)} %get-tuple-element.7.refs_1_, bf16[136,2048]{1,0:T(8,128)(2,1)S(1)} %collective-permute-done.20.refs_2_.refs_7_, f32[400,2048]{1,0:T(8,128)S(1)} %quantized_sum.8.refs_3_), custom_call_target="tpu_custom_call" | custom-call | flops 983040000 | tf_op jit(solution)/shard_map/quantized_sum/pallas_call | solution.py:240
  161.4 0.6 gather_fusion
  162.1 0.6 copy.35
  (111 shorter events, 2.5 us)
Async XLA Ops:
  0.6 35.2 %copy-start = (bf16[400,2048]{1,0:T(8,128)(2,1)S(1)}, bf16[400,2048]{1,0:T(8,128)(2,1)}, u32[]{:S(2)}) copy-start(bf16[400,2048]{1,0:T(8,128)(2,1)} %param.10) | copy-start | bytes 4915204
  0.6 1.1 copy-start.1
  1.7 0.7 copy-start.8
  2.4 0.7 copy-start.9
  4.0 14.0 %all-to-all-start = ((bf16[8,48,400]{2,1,0:T(8,128)(2,1)}), bf16[8,48,400]{2,1,0:T(8,128)(2,1)S(1)}, u32[]{:S(2)}, u32[]{:S(2)}) async-start(bf16[8,48,400]{2,1,0:T(8,128)(2,1)} %pack.1), calls=%async_computation | async-start | bytes 786432 | tf_op jit(solution)/shard_map/all_to_all | solution.py:307
  12.5 0.7 copy-start.10
  13.2 1.6 copy-start.11
  14.8 1.6 copy-start.12
  18.3 18.5 %collective-permute-start.2 = (bf16[400,256]{1,0:T(8,128)(2,1)S(1)}, bf16[400,256]{1,0:T(8,128)(2,1)S(1)}, u32[]{:S(2)}, u32[]{:S(2)}) collective-permute-start(bf16[400,256]{1,0:T(8,128)(2,1)S(1)} %get-tuple-element.6.refs_0_), channel_id=1, source_target_pairs={{0,3},{1,2},{2,1},{3,0},{4,7},{5,6},{6,5},{7,4},{8,11},{9,10},{10,... | collective-permute-start | bytes 614408 | tf_op jit(solution)/shard_map/ppermute | solution.py:61
  22.0 18.1 %collective-permute-start.1 = (bf16[400,256]{1,0:T(8,128)(2,1)S(1)}, bf16[400,256]{1,0:T(8,128)(2,1)S(1)}, u32[]{:S(2)}, u32[]{:S(2)}) collective-permute-start(bf16[400,256]{1,0:T(8,128)(2,1)S(1)} %get-tuple-element.6.refs_0_), channel_id=1, source_target_pairs={{0,2},{1,3},{2,0},{3,1},{4,6},{5,7},{6,4},{7,5},{8,10},{9,11},{10,... | collective-permute-start | bytes 614408 | tf_op jit(solution)/shard_map/ppermute | solution.py:61
  22.0 13.9 %collective-permute-start = (bf16[400,256]{1,0:T(8,128)(2,1)S(1)}, bf16[400,256]{1,0:T(8,128)(2,1)S(1)}, u32[]{:S(2)}, u32[]{:S(2)}) collective-permute-start(bf16[400,256]{1,0:T(8,128)(2,1)S(1)} %get-tuple-element.6.refs_0_), channel_id=1, source_target_pairs={{0,1},{1,0},{2,3},{3,2},{4,5},{5,4},{6,7},{7,6},{8,9},{9,8},{10,11... | collective-permute-start | bytes 614408 | tf_op jit(solution)/shard_map/ppermute | solution.py:61
  35.8 0.8 copy-start.2
  36.8 1.3 copy-start.4
  37.3 27.4 %collective-permute-start.12 = (bf16[4,1,32,2048]{3,2,0,1:T(8,128)(2,1)S(1)}, bf16[4,1,32,2048]{3,2,0,1:T(8,128)(2,1)S(1)}, u32[]{:S(2)}, u32[]{:S(2)}) collective-permute-start(bf16[4,1,32,2048]{3,2,0,1:T(8,128)(2,1)S(1)} %bitcast.142), channel_id=1, source_target_pairs={{0,4},{4,0},{8,12},{12,8},{16,20},{20,16},{24,28},{28,24},{1,5},{5... | collective-permute-start | bytes 1572872 | tf_op jit(solution)/shard_map/ppermute | solution.py:37
  40.0 4.6 %copy-start.6 = (bf16[400,256]{1,0:T(8,128)(2,1)}, bf16[400,256]{1,0:T(8,128)(2,1)S(1)}, u32[]{:S(2)}) copy-start(bf16[400,256]{1,0:T(8,128)(2,1)S(1)} %collective-permute-done.1.refs_2_) | copy-start | bytes 614404
  40.6 26.3 %collective-permute-start.9 = (bf16[4,1,32,2048]{3,2,0,1:T(8,128)(2,1)S(1)}, bf16[4,1,32,2048]{3,2,0,1:T(8,128)(2,1)S(1)}, u32[]{:S(2)}, u32[]{:S(2)}) collective-permute-start(bf16[4,1,32,2048]{3,2,0,1:T(8,128)(2,1)S(1)} %bitcast.143), channel_id=1, source_target_pairs={{0,4},{4,0},{8,12},{12,8},{16,20},{20,16},{24,28},{28,24},{1,5},{5... | collective-permute-start | bytes 1572872 | tf_op jit(solution)/shard_map/ppermute | solution.py:37
  40.6 8.0 %collective-permute-start.3 = (bf16[56,2048]{1,0:T(8,128)(2,1)S(1)}, bf16[56,2048]{1,0:T(8,128)(2,1)S(1)}, u32[]{:S(2)}, u32[]{:S(2)}) collective-permute-start(bf16[56,2048]{1,0:T(8,128)(2,1)S(1)} %get-tuple-element.14), channel_id=1, source_target_pairs={{0,1},{1,0},{2,3},{3,2},{4,5},{5,4},{6,7},{7,6},{8,9},{9,8},{10,11... | collective-permute-start | bytes 688136 | tf_op jit(solution)/shard_map/ppermute | solution.py:61
  42.1 12.5 %collective-permute-start.5 = (bf16[56,2048]{1,0:T(8,128)(2,1)S(1)}, bf16[56,2048]{1,0:T(8,128)(2,1)S(1)}, u32[]{:S(2)}, u32[]{:S(2)}) collective-permute-start(bf16[56,2048]{1,0:T(8,128)(2,1)S(1)} %get-tuple-element.15), channel_id=1, source_target_pairs={{0,3},{1,2},{2,1},{3,0},{4,7},{5,6},{6,5},{7,4},{8,11},{9,10},{10,... | collective-permute-start | bytes 688136 | tf_op jit(solution)/shard_map/ppermute | solution.py:61
  43.3 21.3 %collective-permute-start.4 = (bf16[56,2048]{1,0:T(8,128)(2,1)S(1)}, bf16[56,2048]{1,0:T(8,128)(2,1)S(1)}, u32[]{:S(2)}, u32[]{:S(2)}) collective-permute-start(bf16[56,2048]{1,0:T(8,128)(2,1)S(1)} %get-tuple-element.16), channel_id=1, source_target_pairs={{0,2},{1,3},{2,0},{3,1},{4,6},{5,7},{6,4},{7,5},{8,10},{9,11},{10,... | collective-permute-start | bytes 688136 | tf_op jit(solution)/shard_map/ppermute | solution.py:61
  48.6 16.1 %copy-start.15 = (bf16[56,2048]{1,0:T(8,128)(2,1)}, bf16[56,2048]{1,0:T(8,128)(2,1)S(1)}, u32[]{:S(2)}) copy-start(bf16[56,2048]{1,0:T(8,128)(2,1)S(1)} %collective-permute-done.3) | copy-start | bytes 688132
  48.6 29.2 %collective-permute-start.6 = (bf16[4,2,32,2048]{3,2,1,0:T(8,128)(2,1)S(1)}, bf16[4,2,32,2048]{3,2,1,0:T(8,128)(2,1)S(1)}, u32[]{:S(2)}, u32[]{:S(2)}) collective-permute-start(bf16[4,2,32,2048]{3,2,1,0:T(8,128)(2,1)S(1)} %bitcast.139), channel_id=1, source_target_pairs={{0,4},{4,0},{8,12},{12,8},{16,20},{20,16},{24,28},{28,24},{1,5},{5... | collective-permute-start | bytes 3145736 | tf_op jit(solution)/shard_map/ppermute | solution.py:37
  54.6 10.1 %copy-start.16 = (bf16[56,2048]{1,0:T(8,128)(2,1)}, bf16[56,2048]{1,0:T(8,128)(2,1)S(1)}, u32[]{:S(2)}) copy-start(bf16[56,2048]{1,0:T(8,128)(2,1)S(1)} %collective-permute-done.5) | copy-start | bytes 688132
  64.6 0.7 copy-start.13
  65.3 6.4 %collective-permute-start.13 = (bf16[2,1,32,2048]{3,2,0,1:T(8,128)(2,1)S(1)}, bf16[2,1,32,2048]{3,2,0,1:T(8,128)(2,1)S(1)}, u32[]{:S(2)}, u32[]{:S(2)}) collective-permute-start(bf16[2,1,32,2048]{3,2,0,1:T(8,128)(2,1)S(1)} %fusion.28), channel_id=1, source_target_pairs={{0,8},{4,20},{8,0},{12,28},{16,24},{20,4},{24,16},{28,12},{1,9},{5... | collective-permute-start | bytes 786440 | tf_op jit(solution)/shard_map/ppermute | solution.py:54
  67.0 9.0 %collective-permute-start.10 = (bf16[2,1,32,2048]{3,2,0,1:T(8,128)(2,1)S(1)}, bf16[2,1,32,2048]{3,2,0,1:T(8,128)(2,1)S(1)}, u32[]{:S(2)}, u32[]{:S(2)}) collective-permute-start(bf16[2,1,32,2048]{3,2,0,1:T(8,128)(2,1)S(1)} %fusion.27), channel_id=1, source_target_pairs={{0,8},{4,20},{8,0},{12,28},{16,24},{20,4},{24,16},{28,12},{1,9},{5... | collective-permute-start | bytes 786440 | tf_op jit(solution)/shard_map/ppermute | solution.py:54
  71.7 8.1 %collective-permute-start.14 = (bf16[1,1,32,2048]{3,2,1,0:T(8,128)(2,1)S(1)}, bf16[1,1,32,2048]{3,2,1,0:T(8,128)(2,1)S(1)}, u32[]{:S(2)}, u32[]{:S(2)}) collective-permute-start(bf16[1,1,32,2048]{3,2,1,0:T(8,128)(2,1)S(1)} %fusion.43), channel_id=1, source_target_pairs={{0,16},{4,12},{8,24},{12,4},{16,0},{20,28},{24,8},{28,20},{1,17},{... | collective-permute-start | bytes 393224 | tf_op jit(solution)/shard_map/ppermute | solution.py:54
  76.1 6.4 %collective-permute-start.11 = (bf16[1,1,32,2048]{3,2,1,0:T(8,128)(2,1)S(1)}, bf16[1,1,32,2048]{3,2,1,0:T(8,128)(2,1)S(1)}, u32[]{:S(2)}, u32[]{:S(2)}) collective-permute-start(bf16[1,1,32,2048]{3,2,1,0:T(8,128)(2,1)S(1)} %fusion.41), channel_id=1, source_target_pairs={{0,16},{4,12},{8,24},{12,4},{16,0},{20,28},{24,8},{28,20},{1,17},{... | collective-permute-start | bytes 393224 | tf_op jit(solution)/shard_map/ppermute | solution.py:54
  78.3 9.3 %collective-permute-start.7 = (bf16[2,2,32,2048]{3,2,1,0:T(8,128)(2,1)S(1)}, bf16[2,2,32,2048]{3,2,1,0:T(8,128)(2,1)S(1)}, u32[]{:S(2)}, u32[]{:S(2)}) collective-permute-start(bf16[2,2,32,2048]{3,2,1,0:T(8,128)(2,1)S(1)} %fusion.19), channel_id=1, source_target_pairs={{0,8},{4,20},{8,0},{12,28},{16,24},{20,4},{24,16},{28,12},{1,9},{5... | collective-permute-start | bytes 1572872 | tf_op jit(solution)/shard_map/ppermute | solution.py:54
  87.8 6.5 %slice-start = ((bf16[56,2048]{1,0:T(8,128)(2,1)}), bf16[48,2048]{1,0:T(8,128)(2,1)S(1)}, s32[]{:S(2)}) async-start(bf16[56,2048]{1,0:T(8,128)(2,1)} %copy-done.13), calls=%async_computation.1 | async-start | bytes 393216 | tf_op jit(solution)/shard_map/slice | solution.py:380
  87.8 6.5 %slice-start.1 = ((bf16[56,2048]{1,0:T(8,128)(2,1)}), bf16[48,2048]{1,0:T(8,128)(2,1)S(1)}, s32[]{:S(2)}) async-start(bf16[56,2048]{1,0:T(8,128)(2,1)} %copy-done.15), calls=%async_computation.2 | async-start | bytes 393216 | tf_op jit(solution)/shard_map/slice | solution.py:380
  87.8 6.5 %slice-start.2 = ((bf16[56,2048]{1,0:T(8,128)(2,1)}), bf16[48,2048]{1,0:T(8,128)(2,1)S(1)}, s32[]{:S(2)}) async-start(bf16[56,2048]{1,0:T(8,128)(2,1)} %copy-done.16), calls=%async_computation.3 | async-start | bytes 393216 | tf_op jit(solution)/shard_map/slice | solution.py:380
  87.8 6.4 %collective-permute-start.8 = (bf16[1,2,32,2048]{3,2,1,0:T(8,128)(2,1)S(1)}, bf16[1,2,32,2048]{3,2,1,0:T(8,128)(2,1)S(1)}, u32[]{:S(2)}, u32[]{:S(2)}) collective-permute-start(bf16[1,2,32,2048]{3,2,1,0:T(8,128)(2,1)S(1)} %fusion.26), channel_id=1, source_target_pairs={{0,16},{4,12},{8,24},{12,4},{16,0},{20,28},{24,8},{28,20},{1,17},{... | collective-permute-start | bytes 786440 | tf_op jit(solution)/shard_map/ppermute | solution.py:54
  94.3 6.1 %copy-start.14 = (bf16[56,2048]{1,0:T(8,128)(2,1)S(1)}, bf16[56,2048]{1,0:T(8,128)(2,1)}, u32[]{:S(2)}) copy-start(bf16[56,2048]{1,0:T(8,128)(2,1)} %copy-done.13) | copy-start | bytes 688132
  95.9 4.6 %collective-permute-start.16 = (f32[2,4,32]{2,1,0:T(4,128)S(1)}, f32[2,4,32]{2,1,0:T(4,128)S(1)}, u32[]{:S(2)}, u32[]{:S(2)}) collective-permute-start(f32[2,4,32]{2,1,0:T(4,128)S(1)} %pad_maximum_fusion.3), channel_id=1, source_target_pairs={{0,2},{1,3},{2,0},{3,1},{4,6},{5,7},{6,4},{7,5},{8,10},{9,11},{10,... | collective-permute-start | bytes 3080 | tf_op jit(solution)/shard_map/ppermute | solution.py:61
  96.0 4.7 %collective-permute-start.15 = (f32[2,4,32]{2,1,0:T(4,128)S(1)}, f32[2,4,32]{2,1,0:T(4,128)S(1)}, u32[]{:S(2)}, u32[]{:S(2)}) collective-permute-start(f32[2,4,32]{2,1,0:T(4,128)S(1)} %get-tuple-element.29), channel_id=1, source_target_pairs={{0,1},{1,0},{2,3},{3,2},{4,5},{5,4},{6,7},{7,6},{8,9},{9,8},{10,11... | collective-permute-start | bytes 3080 | tf_op jit(solution)/shard_map/ppermute | solution.py:61
  99.1 5.4 %collective-permute-start.17 = (f32[2,4,32]{2,1,0:T(4,128)S(1)}, f32[2,4,32]{2,1,0:T(4,128)S(1)}, u32[]{:S(2)}, u32[]{:S(2)}) collective-permute-start(f32[2,4,32]{2,1,0:T(4,128)S(1)} %get-tuple-element.30), channel_id=1, source_target_pairs={{0,3},{1,2},{2,1},{3,0},{4,7},{5,6},{6,5},{7,4},{8,11},{9,10},{10,... | collective-permute-start | bytes 3080 | tf_op jit(solution)/shard_map/ppermute | solution.py:61
  104.7 19.8 %copy-start.3 = (bf16[400,256]{1,0:T(8,128)(2,1)S(1)}, bf16[400,256]{1,0:T(8,128)(2,1)}, u32[]{:S(2)}) copy-start(bf16[400,256]{1,0:T(8,128)(2,1)} %copy-done.2) | copy-start | bytes 614404
  104.7 19.8 %copy-start.5 = (bf16[400,256]{1,0:T(8,128)(2,1)S(1)}, bf16[400,256]{1,0:T(8,128)(2,1)}, u32[]{:S(2)}) copy-start(bf16[400,256]{1,0:T(8,128)(2,1)} %copy-done.4) | copy-start | bytes 614404
  104.7 19.8 %copy-start.7 = (bf16[400,256]{1,0:T(8,128)(2,1)S(1)}, bf16[400,256]{1,0:T(8,128)(2,1)}, u32[]{:S(2)}) copy-start(bf16[400,256]{1,0:T(8,128)(2,1)} %copy-done.6) | copy-start | bytes 614404
  109.2 14.6 %collective-permute-start.18 = (bf16[136,2048]{1,0:T(8,128)(2,1)S(1)}, bf16[136,2048]{1,0:T(8,128)(2,1)S(1)}, u32[]{:S(2)}, u32[]{:S(2)}) collective-permute-start(bf16[136,2048]{1,0:T(8,128)(2,1)S(1)} %concatenate.25.refs_2_.refs_0_), channel_id=1, source_target_pairs={{0,8},{4,20},{8,0},{12,28},{16,24},{20,4},{24,16},{28,12},{1,9},{5... | collective-permute-start | bytes 1671176 | tf_op jit(solution)/shard_map/ppermute | solution.py:54
  111.3 13.1 %collective-permute-start.21 = (bf16[136,2048]{1,0:T(8,128)(2,1)S(1)}, bf16[136,2048]{1,0:T(8,128)(2,1)S(1)}, u32[]{:S(2)}, u32[]{:S(2)}) collective-permute-start(bf16[136,2048]{1,0:T(8,128)(2,1)S(1)} %concatenate.25.refs_2_.refs_0_), channel_id=1, source_target_pairs={{0,16},{4,12},{8,24},{12,4},{16,0},{20,28},{24,8},{28,20},{1,17},{... | collective-permute-start | bytes 1671176 | tf_op jit(solution)/shard_map/ppermute | solution.py:54
  123.8 9.5 %collective-permute-start.19 = (bf16[136,2048]{1,0:T(8,128)(2,1)S(1)}, bf16[136,2048]{1,0:T(8,128)(2,1)S(1)}, u32[]{:S(2)}, u32[]{:S(2)}) collective-permute-start(bf16[136,2048]{1,0:T(8,128)(2,1)S(1)} %collective-permute-done.18.refs_2_), channel_id=1, source_target_pairs={{0,16},{4,12},{8,24},{12,4},{16,0},{20,28},{24,8},{28,20},{1,17},{... | collective-permute-start | bytes 1671176 | tf_op jit(solution)/shard_map/ppermute | solution.py:54
  123.8 9.5 %collective-permute-start.24 = (bf16[136,2048]{1,0:T(8,128)(2,1)S(1)}, bf16[136,2048]{1,0:T(8,128)(2,1)S(1)}, u32[]{:S(2)}, u32[]{:S(2)}) collective-permute-start(bf16[136,2048]{1,0:T(8,128)(2,1)S(1)} %concatenate.25.refs_2_.refs_0_), channel_id=1, source_target_pairs={{0,4},{4,0},{8,12},{12,8},{16,20},{20,16},{24,28},{28,24},{1,5},{5... | collective-permute-start | bytes 1671176 | tf_op jit(solution)/shard_map/ppermute | solution.py:37
  123.8 14.8 %collective-permute-start.23 = (bf16[136,2048]{1,0:T(8,128)(2,1)S(1)}, bf16[136,2048]{1,0:T(8,128)(2,1)S(1)}, u32[]{:S(2)}, u32[]{:S(2)}) collective-permute-start(bf16[136,2048]{1,0:T(8,128)(2,1)S(1)} %collective-permute-done.18.refs_2_), channel_id=1, source_target_pairs={{0,4},{4,0},{8,12},{12,8},{16,20},{20,16},{24,28},{28,24},{1,5},{5... | collective-permute-start | bytes 1671176 | tf_op jit(solution)/shard_map/ppermute | solution.py:37
  124.4 22.6 %collective-permute-start.22 = (bf16[136,2048]{1,0:T(8,128)(2,1)S(1)}, bf16[136,2048]{1,0:T(8,128)(2,1)S(1)}, u32[]{:S(2)}, u32[]{:S(2)}) collective-permute-start(bf16[136,2048]{1,0:T(8,128)(2,1)S(1)} %collective-permute-done.21.refs_2_.refs_4_), channel_id=1, source_target_pairs={{0,4},{4,0},{8,12},{12,8},{16,20},{20,16},{24,28},{28,24},{1,5},{5... | collective-permute-start | bytes 1671176 | tf_op jit(solution)/shard_map/ppermute | solution.py:37
  133.4 19.0 %collective-permute-start.20 = (bf16[136,2048]{1,0:T(8,128)(2,1)S(1)}, bf16[136,2048]{1,0:T(8,128)(2,1)S(1)}, u32[]{:S(2)}, u32[]{:S(2)}) collective-permute-start(bf16[136,2048]{1,0:T(8,128)(2,1)S(1)} %collective-permute-done.19.refs_3_.refs_6_), channel_id=1, source_target_pairs={{0,4},{4,0},{8,12},{12,8},{16,20},{20,16},{24,28},{28,24},{1,5},{5... | collective-permute-start | bytes 1671176 | tf_op jit(solution)/shard_map/ppermute | solution.py:37
  152.5 8.9 %collective-permute-start.27 = (f32[1,2048]{1,0:T(1,128)S(1)}, f32[1,2048]{1,0:T(1,128)S(1)}, u32[]{:S(2)}, u32[]{:S(2)}) collective-permute-start(f32[1,2048]{1,0:T(1,128)S(1)} %gain.1), channel_id=1, source_target_pairs={{0,3},{1,2},{2,1},{3,0},{4,7},{5,6},{6,5},{7,4},{8,11},{9,10},{10,... | collective-permute-start | bytes 24584 | tf_op jit(solution)/shard_map/ppermute | solution.py:61
  153.9 7.5 %collective-permute-start.26 = (f32[1,2048]{1,0:T(1,128)S(1)}, f32[1,2048]{1,0:T(1,128)S(1)}, u32[]{:S(2)}, u32[]{:S(2)}) collective-permute-start(f32[1,2048]{1,0:T(1,128)S(1)} %gain.1), channel_id=1, source_target_pairs={{0,2},{1,3},{2,0},{3,1},{4,6},{5,7},{6,4},{7,5},{8,10},{9,11},{10,... | collective-permute-start | bytes 24584 | tf_op jit(solution)/shard_map/ppermute | solution.py:61
  153.9 7.5 %collective-permute-start.25 = (f32[1,2048]{1,0:T(1,128)S(1)}, f32[1,2048]{1,0:T(1,128)S(1)}, u32[]{:S(2)}, u32[]{:S(2)}) collective-permute-start(f32[1,2048]{1,0:T(1,128)S(1)} %gain.1), channel_id=1, source_target_pairs={{0,1},{1,0},{2,3},{3,2},{4,5},{5,4},{6,7},{7,6},{8,9},{9,8},{10,11... | collective-permute-start | bytes 24584 | tf_op jit(solution)/shard_map/ppermute | solution.py:61

commit v3 on v2

--- a/solution.py
+++ b/solution.py
@@ -18,6 +18,10 @@
 
 def whole(*_):
     return pl.BlockSpec(memory_space=pltpu.VMEM)
+
+
+def anywhere():
+    return pl.BlockSpec(memory_space=pltpu.HBM)
 
 
 def scalar():
@@ -56,16 +60,14 @@
     )
 
 
+def flip_far(value):
+    count = lax.axis_size("dp")
+    return lax.ppermute(value, "dp", [(i, i ^ 6) for i in range(count)])
+
+
 def swap(value, step):
     count = lax.axis_size("seq")
     return lax.ppermute(value, "seq", [(i, i ^ step) for i in range(count)])
-
-
-def pieces(value):
-    high = lax.reduce_precision(value, 8, 7)
-    rest = value - high
-    mid = lax.reduce_precision(rest, 8, 7)
-    return high, mid, rest - mid
 
 
 def cast_pieces(value):
@@ -83,7 +85,20 @@
     return block
 
 
-def pack_kernel(tile_ref, level_ref, draw_ref, out_ref):
+def fetch(pairs, sems):
+    copies = [
+        pltpu.make_async_copy(source, target, sems.at[index])
+        for index, (source, target) in enumerate(pairs)
+    ]
+    for copy in copies:
+        copy.start()
+    return copies
+
+
+def pack_kernel(tile_hbm, level_hbm, draw_hbm, out_ref, tile_ref, level_ref, draw_ref, sems):
+    pairs = ((tile_hbm, tile_ref), (level_hbm, level_ref), (draw_hbm, draw_ref))
+    for copy in fetch(pairs, sems):
+        copy.wait()
     owners, _, width = out_ref.shape
     rows, full = tile_ref.shape
     terms = (level_ref[...].astype(FLOAT),) + cast_pieces(draw_ref[...])
@@ -125,9 +140,15 @@
         )
 
 
-def text_kernel(place_ref, row_ref, column_ref, text_ref, cot_ref, out_ref):
+def text_kernel(
+    place_ref, row_ref, column_ref, text_hbm, cot_hbm, out_ref, part_ref, text_ref, cot_ref, sems
+):
     owners, _, columns = out_ref.shape
-    rows, full = text_ref.shape
+    rows, full = text_hbm.shape
+    cuts = [slice(owner * columns, (owner + 1) * columns) for owner in range(owners)]
+    pairs = [(text_hbm.at[:, cut], text_ref.at[:, cut]) for cut in cuts]
+    pairs += [(cot_hbm.at[:, cut], cot_ref.at[:, cut]) for cut in cuts]
+    copies = fetch(pairs, sems)
     count = row_ref.shape[1]
     mine = place_ref[0]
     base = mine * rows
@@ -144,21 +165,19 @@
     select = jnp.dot(chosen, spread, preferred_element_type=FLOAT).astype(HALF)
     total = jnp.zeros((rows, 1), FLOAT)
     for owner in range(owners):
-        text = text_ref[:, owner * columns : (owner + 1) * columns].astype(FLOAT)
+        copies[owner].wait()
+        text = text_ref[:, cuts[owner]].astype(FLOAT)
         total = total + jnp.sum(text * text, axis=1, keepdims=True)
     inverse = lax.rsqrt(total / full + EPSILON) * is_text
+    for copy in copies[owners:]:
+        copy.wait()
     for step in range(owners):
         owner = mine ^ step
         cut = pl.ds(pl.multiple_of(owner * columns, columns), columns)
         cot = cot_ref[:, cut]
         terms = cot.astype(FLOAT) * text_ref[:, cut].astype(FLOAT) * inverse
-        part = jnp.sum(terms, axis=0, keepdims=True)
-        out_ref[step, :IMG_MOST, :] = jnp.dot(
-            select, cot, preferred_element_type=FLOAT
-        ).astype(HALF)
-        out_ref[step, IMG_MOST:, :] = stacked_lines(
-            cast_pieces(part), EXTRA_ROWS, columns
-        ).astype(HALF)
+        part_ref[step] = jnp.sum(terms, axis=0, keepdims=True)
+        out_ref[step] = jnp.dot(select, cot, preferred_element_type=FLOAT).astype(HALF)
 
 
 def quantize_kernel(slots, replicas, adds, *refs):
@@ -222,6 +241,85 @@
             return carry
 
         lax.fori_loop(0, groups, group, 0, unroll=unroll)
+
+
+def own_gain(gain_ref, mine, columns):
+    return gain_ref[:, pl.ds(pl.multiple_of(mine * columns, columns), columns)]
+
+
+def middle_kernel(sizes, owners, owner_rows, place_ref, row_ref, gain_ref, part_ref, *refs):
+    sums = []
+    for size in sizes:
+        total = refs[0][...]
+        for ref in refs[1:size]:
+            total = total + ref[...].astype(FLOAT)
+        sums.append(total)
+        refs = refs[size:]
+    blocks, emb_ref, cot_ref = refs[:owners], refs[owners], refs[owners + 1]
+    stats = refs[owners + 2 :]
+    mine = place_ref[0]
+    tokens, columns = emb_ref.shape
+    block_rows = tokens // owners
+    shift = block_rows.bit_length() - 1
+    emb = jnp.concatenate(sums, axis=0).astype(HALF)
+    emb_ref[...] = emb
+    emb = emb.astype(FLOAT)
+    line = lax.broadcasted_iota(jnp.int32, (tokens, IMG_MOST), 0)
+    slot = lax.broadcasted_iota(jnp.int32, (tokens, IMG_MOST), 1)
+    absolute = ((line >> shift) ^ mine) * block_rows + (line & (block_rows - 1))
+    cot = jnp.zeros((tokens, columns), FLOAT)
+    for step in range(owners):
+        first = (mine ^ step) * owner_rows
+        start = jnp.sum((row_ref[...] < first).astype(jnp.int32), axis=1, keepdims=True)
+        match = (absolute - start == slot).astype(HALF)
+        cot = cot + jnp.dot(match, blocks[step][...], preferred_element_type=FLOAT)
+    cot_ref[...] = cot.astype(HALF)
+    grad = cot * own_gain(gain_ref, mine, columns)
+    sums = (
+        jnp.sum(emb * emb, axis=1, keepdims=True),
+        jnp.sum(grad * emb, axis=1, keepdims=True),
+    )
+    width = lanes(2 * owners)
+    lane = lax.broadcasted_iota(jnp.int32, (tokens, width), 1)
+    table = jnp.zeros((tokens, width), FLOAT)
+    for step in range(owners):
+        for which, column in enumerate(sums):
+            moved = jnp.concatenate(
+                [
+                    column[(at ^ step) * block_rows : ((at ^ step) + 1) * block_rows]
+                    for at in range(owners)
+                ],
+                axis=0,
+            )
+            table = jnp.where(lane == 2 * step + which, moved, table)
+    turned = table.T
+    for step in range(owners):
+        stats[step][...] = jnp.concatenate(
+            [turned[2 * step : 2 * step + 1], turned[2 * step + 1 : 2 * step + 2], part_ref[step]],
+            axis=1,
+        )
+
+
+def finish_kernel(owners, full, place_ref, gain_ref, emb_ref, cot_ref, draw_ref, *refs):
+    stats, out_ref, scratch = refs[:owners], refs[-2], refs[-1]
+    tokens, columns = emb_ref.shape
+    scratch[...] = jnp.zeros_like(scratch)
+    total = stats[0][...]
+    for ref in stats[1:]:
+        total = total + ref[...]
+    scratch[0:1, :] = total[:, :tokens]
+    scratch[1:2, :] = total[:, tokens : 2 * tokens]
+    turned = scratch[...].T
+    inverse = lax.rsqrt(turned[:, 0:1] / full + EPSILON)
+    cot = cot_ref[...].astype(FLOAT)
+    normed = emb_ref[...].astype(FLOAT) * inverse
+    grad = cot * own_gain(gain_ref, place_ref[0], columns)
+    out_ref[:tokens, :] = (
+        (grad - normed * (turned[:, 1:2] * inverse / full)) * inverse
+    ).astype(HALF)
+    part = total[:, 2 * tokens :] + jnp.sum(cot * normed, axis=0, keepdims=True)
+    terms = cast_pieces(part) + cast_pieces(draw_ref[...])
+    out_ref[tokens:, :] = stacked_lines(terms, EXTRA_ROWS, columns).astype(HALF)
 
 
 def gain_kernel(replicas, *refs):
@@ -257,10 +355,6 @@
     )(tiles, meta, *loads, *([total] if adds else []))
 
 
-def stack_blocks(stats, step):
-    return jnp.stack([stats[:, at ^ step] for at in range(stats.shape[1])], axis=1)
-
-
 def half_of(value, bit, taken):
     shape = value.shape
     high = shape[0] // (2 * bit)
@@ -288,7 +382,7 @@
     places = placeholders[0]
     image_total = places.shape[0]
     tok_rows, model_width = text_hidden.shape[1:]
-    tile_rows, _ = tile_tokens.shape[1:]
+    tile_rows, vision = tile_tokens.shape[1:]
     width, columns = proj_weight.shape
     padded = -(-width // 16) * 16
     kept_labels = tuple(range(0, replicas, 2))
@@ -298,10 +392,16 @@
 
     packed = pl.pallas_call(
         pack_kernel,
-        in_specs=[whole()] * 3,
+        in_specs=[anywhere()] * 3,
         out_specs=whole(),
+        scratch_shapes=[
+            pltpu.VMEM((tile_rows, vision), HALF),
+            pltpu.VMEM((1, vision), jnp.int32),
+            pltpu.VMEM((1, vision), FLOAT),
+            pltpu.SemaphoreType.DMA((3,)),
+        ],
         out_shape=jax.ShapeDtypeStruct((replicas, tile_rows + META_ROWS, width), HALF),
-        compiler_params=grant(4),
+        compiler_params=grant(60),
         name="pack",
     )(tile_tokens[0], bucket_levels[0], row_draws[0])
     exchanged = lax.all_to_all(packed, "dp", 0, 0, tiled=True)
@@ -322,17 +422,26 @@
     )(here, exchanged)
     tile_blocks = [own_tile]
     for step in range(1, seq_count):
-        tile_blocks.append(swap(own_tile, step))
-
-    outgoing = pl.pallas_call(
+        low = step & -step
+        tile_blocks.append(swap(tile_blocks[step ^ low], low))
+
+    outgoing, text_parts = pl.pallas_call(
         text_kernel,
-        in_specs=[scalar()] + [whole()] * 4,
-        out_specs=whole(),
-        out_shape=jax.ShapeDtypeStruct((seq_count, IMG_MOST + EXTRA_ROWS, columns), HALF),
+        in_specs=[scalar()] + [whole()] * 2 + [anywhere()] * 2,
+        out_specs=[whole()] * 2,
+        scratch_shapes=[
+            pltpu.VMEM((tok_rows, model_width), HALF),
+            pltpu.VMEM((tok_rows, model_width), HALF),
+            pltpu.SemaphoreType.DMA((2 * seq_count,)),
+        ],
+        out_shape=[
+            jax.ShapeDtypeStruct((seq_count, IMG_MOST, columns), HALF),
+            jax.ShapeDtypeStruct((seq_count, 1, columns), FLOAT),
+        ],
         cost_estimate=pl.CostEstimate(
             flops=tok_rows * model_width * 4000, bytes_accessed=0, transcendentals=0
         ),
-        compiler_params=grant(16),
+        compiler_params=grant(60),
         name="text_part",
     )(there, placeholders, places.reshape(image_total, 1), text_hidden[0], cotangent[0])
 
@@ -340,7 +449,7 @@
     even = (replicas // 2) * tile_rows
     split = seq_count // 2
     parts = [tile_blocks[:split]] + [[block] for block in tile_blocks[split:]]
-    embedded_parts = []
+    sizes, summands = [], []
     for part, group in enumerate(parts):
 
         def product(cut, kind):
@@ -359,51 +468,50 @@
             for step in range(1, seq_count):
                 returned.append(swap(outgoing[step], step))
         arrived = flip(sent, 0)
-        remaining = list(range(1, levels_of_bits))
-        for bit in range(1, levels_of_bits):
-            stride = 1 << remaining.index(bit)
-            remaining.remove(bit)
-            held = held + arrived.astype(FLOAT)
-            sent = half_of(held, stride, 1).astype(HALF)
-            held = half_of(held, stride, 0)
-            arrived = flip_label(sent, bit)
         held = held + arrived.astype(FLOAT)
-        embedded_parts.append(held.reshape(-1, columns))
-    emb_float = jnp.concatenate(embedded_parts, axis=0).astype(HALF).astype(FLOAT)
-
-    tokens = jnp.arange(image_total, dtype=jnp.int32)
-    absolute = ((tokens // tile_rows) ^ there) * tile_rows + tokens % tile_rows
-    sources = jnp.arange(seq_count, dtype=jnp.int32) ^ there
-    starts = jnp.sum((places[None, :] < (sources * tok_rows)[:, None]).astype(jnp.int32), axis=1)
-    wanted = (absolute[:, None] - starts[None, :])[:, :, None]
-    match = (wanted == jnp.arange(IMG_MOST, dtype=jnp.int32)[None, None, :]).astype(HALF)
-    arrived = jnp.concatenate([block[:IMG_MOST] for block in returned], axis=0)
-    image_cot = jnp.dot(
-        match.reshape(image_total, seq_count * IMG_MOST), arrived, preferred_element_type=FLOAT
-    )
-    text_part = sum(
-        jnp.sum(block[IMG_MOST : IMG_MOST + 3].astype(FLOAT), axis=0) for block in returned
-    )
-
-    column_gain = lax.dynamic_slice_in_dim(norm_gain, seq_index * columns, columns)
-    grad_in = image_cot * column_gain[None, :]
-    stats = jnp.stack(
-        [jnp.sum(emb_float * emb_float, axis=1), jnp.sum(grad_in * emb_float, axis=1)]
-    ).reshape(2, seq_count, tile_rows)
-    for_all = stats
+        if levels_of_bits == 3 and part == len(parts) - 1:
+            sums = [held[0]]
+            for place in (1, 2, 3):
+                sent = held[place].astype(HALF)
+                sums.append(
+                    flip_label(sent, place) if place < 3 else flip_far(sent)
+                )
+        else:
+            for bit in range(1, levels_of_bits):
+                sent = half_of(held, 1, 1).astype(HALF)
+                held = half_of(held, 1, 0)
+                arrived = flip_label(sent, bit)
+                if bit < levels_of_bits - 1:
+                    held = held + arrived.astype(FLOAT)
+            sums = [held, arrived]
+        sizes.append(len(sums))
+        summands += [value.reshape(-1, columns) for value in sums]
+    tokens_of = (image_total, columns)
+    middle = pl.pallas_call(
+        functools.partial(middle_kernel, tuple(sizes), seq_count, tok_rows),
+        in_specs=[scalar()] + [whole()] * (3 + len(summands) + seq_count),
+        out_specs=[whole()] * (2 + seq_count),
+        out_shape=[
+            jax.ShapeDtypeStruct(tokens_of, HALF),
+            jax.ShapeDtypeStruct(tokens_of, HALF),
+        ]
+        + [jax.ShapeDtypeStruct((1, 2 * image_total + columns), FLOAT)] * seq_count,
+        compiler_params=grant(16),
+        name="middle",
+    )(there, placeholders, norm_gain.reshape(1, -1), text_parts, *summands, *returned)
+    embedded, image_cot = middle[:2]
+    stats = [middle[2]]
     for step in range(1, seq_count):
-        for_all = for_all + swap(stack_blocks(stats, step), step)
-    squares, mixed = for_all.reshape(2, image_total)
-    inverse = lax.rsqrt(squares / model_width + EPSILON)[:, None]
-    normed = emb_float * inverse
-    emb_grad = ((grad_in - normed * (mixed[:, None] * inverse / model_width)) * inverse).astype(HALF)
-    gain_part = text_part + jnp.sum(image_cot * normed, axis=0)
-    extra = jnp.stack(
-        pieces(gain_part)
-        + pieces(column_draws[0])
-        + (jnp.zeros_like(gain_part),) * (EXTRA_ROWS - 6)
-    ).astype(HALF)
-    own_load = jnp.concatenate([emb_grad, extra], axis=0)
+        stats.append(swap(middle[2 + step], step))
+    own_load = pl.pallas_call(
+        functools.partial(finish_kernel, seq_count, model_width),
+        in_specs=[scalar()] + [whole()] * (4 + seq_count),
+        out_specs=whole(),
+        out_shape=jax.ShapeDtypeStruct((image_total + EXTRA_ROWS, columns), HALF),
+        scratch_shapes=[pltpu.VMEM((128, image_total), FLOAT)],
+        compiler_params=grant(12),
+        name="finish",
+    )(there, norm_gain.reshape(1, -1), embedded, image_cot, column_draws, *stats)
 
     tiles = pl.pallas_call(
         functools.partial(regroup_kernel, order, tile_rows),
@@ -426,7 +534,7 @@
         loads[3] = flip(loads[4], 0)
         loads[6] = flip_label(loads[2], 2)
         loads[7] = flip(loads[6], 0)
-        batches = ((0, 1), (2, 5), (4,), (3, 6), (7,))
+        batches = ((0, 1), (2, 5), (4,), (3,), (6,), (7,))
     else:
         for bit in range(1, levels_of_bits):
             for slot, load in list(loads.items()):
@@ -448,6 +556,7 @@
     total = None
     for slots in batches:
         total = quantized_sum(tiles, meta, [loads[slot] for slot in slots], slots, replicas, total)
+    sources = jnp.arange(seq_count, dtype=jnp.int32) ^ there
     gain_total = jnp.take(jnp.concatenate(gains, axis=0), sources, axis=0)
     return total[:width], gain_total.reshape(model_width)
 

time: 163 us -> 149 us (0.914)
  waiting for transfers between devices: 79.5 us -> 68.9 us
  local copies, waits for them, and re-layouts: 12.3 us -> 4.06 us
  Pallas kernels: 27.1 us -> 33.7 us
  starting transfers between devices: 32.4 us -> 37 us
  other arithmetic: 5.53 us -> 0.95 us
    ppermute x12, waiting for transfers between devices: 38.5 us -> 26.6 us  [swap(): return lax.ppermute(value, 'seq', [(i, i ^ step) for i in range(count)])]
    pallas_call x2 -> x4, Pallas kernels: 2.61 us -> 8.79 us  [the longest x1 5.04 us: on_device(): pl.pallas_call(text_kernel, in_specs=[scalar()] + [whole()] * 2 + [anywhe...]
    unnamed x36 -> x13, local copies, waits for them, and re-layouts: 7.4 us -> 1.71 us
    reduce_sum x6 -> x0, other arithmetic: 3.4 us -> none  [the longest x1 2.47 us: on_device(): gain_part = text_part + jnp.sum(image_cot * normed, axis=0)]
    ppermute x9, waiting for transfers between devices: 41.1 us -> 38.7 us  [flip_label(): lax.ppermute(value, 'dp', [(i, i ^ (odd if i % 2 else 1 << bit)) for i in...]
    concatenate x1 -> x0, local copies, waits for them, and re-layouts: 2.02 us -> none  [on_device(): own_load = jnp.concatenate([emb_grad, extra], axis=0)]
    all_to_all x1, waiting for transfers between devices: 0.01 us -> 1.88 us  [on_device(): exchanged = lax.all_to_all(packed, 'dp', 0, 0, tiled=True)]
    ppermute x12, starting transfers between devices: 17 us -> 18.8 us  [swap(): return lax.ppermute(value, 'seq', [(i, i ^ step) for i in range(count)])]
  transfers between devices with their start and end apart: 29 -> 30, of which waited for: 14 -> 14; matrix products, arithmetic and copies ran while one was open for 5% -> 4% of each run, Pallas kernels for 16% -> 20%
where the time goes in v3:
time: 149 us
  waiting for transfers between devices  68.9 us (46%)
  starting transfers between devices  37 us (25%)
  Pallas kernels  33.7 us (23%)
  local copies, waits for them, and re-layouts  4.06 us (3%)
  matrix products  3.34 us (2%)
    ppermute x9, waiting for transfers between devices, flip_label(): lax.ppermute(value, 'dp', [(i, i ^ (odd if i % 2 else 1 << bit)) for i in...  38.7 us
    ppermute x12, waiting for transfers between devices, swap(): return lax.ppermute(value, 'seq', [(i, i ^ step) for i in range(count)])  26.6 us
    pallas_call x6, Pallas kernels, quantized_sum(): pl.pallas_call(functools.partial(quantize_kernel, slots, replicas, adds),...  23.8 us
    ppermute x12, starting transfers between devices, swap(): return lax.ppermute(value, 'seq', [(i, i ^ step) for i in range(count)])  18.8 us
    ppermute x9, starting transfers between devices, flip_label(): lax.ppermute(value, 'dp', [(i, i ^ (odd if i % 2 else 1 << bit)) for i in...  10.6 us
    all_to_all x1, starting transfers between devices, on_device(): exchanged = lax.all_to_all(packed, 'dp', 0, 0, tiled=True)  5.21 us
    pallas_call x1, Pallas kernels, on_device(): pl.pallas_call(text_kernel, in_specs=[scalar()] + [whole()] * 2 + [anywhe...  5.04 us
    dot_general x6, matrix products, product(): lax.dot_general(left, weight, (((0,), (0,)), ((), ())), preferred_element...  3.34 us
  transfers between devices with their start and end apart: 30, of which 14 were waited for; matrix products, arithmetic and copies ran while one was open for 4% of the time, Pallas kernels for 20%

profile of v3, /device:TPU:0, one launch (start us, length us, event | category | flops | bytes accessed | tf_op | source)
XLA Modules:
  0.0 149.0 jit_solution(5806841979396266558)
XLA Ops:
  0.6 2.0 %pack.1 = bf16[8,48,400]{2,1,0:T(8,128)(2,1)} custom-call(bf16[32,3200]{1,0:T(8,128)(2,1)} %bitcast.103, s32[1,3200]{1,0:T(1,128)} %bitcast.105, f32[1,3200]{1,0:T(1,128)} %bitcast.106), custom_call_target="tpu_custom_call" | custom-call | tf_op jit(solution)/shard_map/pack/pallas_call | solution.py:393
  2.6 5.2 %all-to-all-start = ((bf16[8,48,400]{2,1,0:T(8,128)(2,1)}), bf16[8,48,400]{2,1,0:T(8,128)(2,1)S(1)}, u32[]{:S(2)}, u32[]{:S(2)}) async-start(bf16[8,48,400]{2,1,0:T(8,128)(2,1)} %pack.1), calls=%async_computation | async-start | bytes 786432 | tf_op jit(solution)/shard_map/all_to_all | solution.py:407
  7.9 1.4 copy.12.column_ref
  9.2 5.0 %text_part.1 = (bf16[4,48,2048]{2,1,0:T(8,128)(2,1)}, f32[4,1,2048]{2,1,0:T(1,128)}) custom-call(s32[1]{0:T(128)} %bitcast.4.place_ref, s32[1,128]{1,0:T(1,128)} %row_ref.3, s32[128,1]{1,0:T(8,128)} %copy.12.column_ref, bf16[128,8192]{1,0:T(8,128)(2,1)} %bitcast.107, bf16[128,8192]{1,0:T(8,128)(2,1)} %bitcast.108), custom_call_target="tpu_custom_call" | custom-call | flops 4194304000 | tf_op jit(solution)/shard_map/text_part/pallas_call | solution.py:428
  14.3 1.9 %all-to-all-done.in_ref = bf16[8,48,400]{2,1,0:T(8,128)(2,1)S(1)} async-done(((bf16[8,48,400]{2,1,0:T(8,128)(2,1)}), bf16[8,48,400]{2,1,0:T(8,128)(2,1)S(1)}, u32[]{:S(2)}, u32[]{:S(2)}) %all-to-all-start) | async-done | bytes 307232 | tf_op jit(solution)/shard_map/all_to_all | solution.py:407
  16.2 0.2 unpack.1
  16.4 2.7 %collective-permute-start.1 = (bf16[400,256]{1,0:T(8,128)(2,1)S(1)}, bf16[400,256]{1,0:T(8,128)(2,1)S(1)}, u32[]{:S(2)}, u32[]{:S(2)}) collective-permute-start(bf16[400,256]{1,0:T(8,128)(2,1)S(1)} %get-tuple-element.14.refs_0_), channel_id=1, source_target_pairs={{0,2},{1,3},{2,0},{3,1},{4,6},{5,7},{6,4},{7,5},{8,10},{9,11},{10,... | collective-permute-start | bytes 614408 | tf_op jit(solution)/shard_map/ppermute | solution.py:70
  19.0 1.6 %collective-permute-start = (bf16[400,256]{1,0:T(8,128)(2,1)S(1)}, bf16[400,256]{1,0:T(8,128)(2,1)S(1)}, u32[]{:S(2)}, u32[]{:S(2)}) collective-permute-start(bf16[400,256]{1,0:T(8,128)(2,1)S(1)} %get-tuple-element.14.refs_0_), channel_id=1, source_target_pairs={{0,1},{1,0},{2,3},{3,2},{4,5},{5,4},{6,7},{7,6},{8,9},{9,8},{10,11... | collective-permute-start | bytes 614408 | tf_op jit(solution)/shard_map/ppermute | solution.py:70
  20.6 6.7 %collective-permute-done.1.refs_2_ = bf16[400,256]{1,0:T(8,128)(2,1)S(1)} collective-permute-done((bf16[400,256]{1,0:T(8,128)(2,1)S(1)}, bf16[400,256]{1,0:T(8,128)(2,1)S(1)}, u32[]{:S(2)}, u32[]{:S(2)}) %collective-permute-start.1) | collective-permute-done | bytes 204832 | tf_op jit(solution)/shard_map/ppermute | solution.py:70
  27.4 0.5 convolution_convert_fusion.2
  27.8 0.1 collective-permute-start.6
  28.0 0.7 convolution_convert_fusion
  28.8 1.0 copy-done.5
  29.9 3.6 %collective-permute-start.15 = (bf16[48,2048]{1,0:T(8,128)(2,1)S(1)}, bf16[48,2048]{1,0:T(8,128)(2,1)S(1)}, u32[]{:S(2)}, u32[]{:S(2)}) collective-permute-start(bf16[48,2048]{1,0:T(8,128)(2,1)S(1)} %get-tuple-element.28), channel_id=1, source_target_pairs={{0,3},{1,2},{2,1},{3,0},{4,7},{5,6},{6,5},{7,4},{8,11},{9,10},{10,... | collective-permute-start | bytes 589832 | tf_op jit(solution)/shard_map/ppermute | solution.py:70
  33.4 0.9 collective-permute-start.13
  34.3 0.7 fusion.7
  35.1 1.2 collective-permute-start.2
  36.3 0.5 fusion.19
  36.7 15.2 %collective-permute-done.2.refs_3_ = bf16[400,256]{1,0:T(8,128)(2,1)S(1)} collective-permute-done((bf16[400,256]{1,0:T(8,128)(2,1)S(1)}, bf16[400,256]{1,0:T(8,128)(2,1)S(1)}, u32[]{:S(2)}, u32[]{:S(2)}) %collective-permute-start.2) | collective-permute-done | bytes 204832 | tf_op jit(solution)/shard_map/ppermute | solution.py:70
  52.0 0.5 convolution_convert_fusion.1
  52.5 0.5 fusion.16
  53.0 0.5 collective-permute-start.9
  53.5 0.1 convert_add_fusion.1
  53.7 1.7 %collective-permute-done.9 = bf16[4,1,32,2048]{3,2,1,0:T(8,128)(2,1)S(1)} collective-permute-done((bf16[4,1,32,2048]{3,2,1,0:T(8,128)(2,1)S(1)}, bf16[4,1,32,2048]{3,2,1,0:T(8,128)(2,1)S(1)}, u32[]{:S(2)}, u32[]{:S(2)}) %collective-permute-start.9) | collective-permute-done | bytes 524320 | tf_op jit(solution)/shard_map/ppermute | solution.py:41
  55.4 2.1 %collective-permute-start.7 = (bf16[2,1,32,2048]{3,2,0,1:T(8,128)(2,1)S(1)}, bf16[2,1,32,2048]{3,2,0,1:T(8,128)(2,1)S(1)}, u32[]{:S(2)}, u32[]{:S(2)}) collective-permute-start(bf16[2,1,32,2048]{3,2,0,1:T(8,128)(2,1)S(1)} %fusion.6), channel_id=1, source_target_pairs={{0,8},{4,20},{8,0},{12,28},{16,24},{20,4},{24,16},{28,12},{1,9},{5... | collective-permute-start | bytes 786440 | tf_op jit(solution)/shard_map/ppermute | solution.py:58
  57.5 0.2 fusion.24
  57.7 1.2 collective-permute-start.12
  58.9 0.3 bitcast_add_fusion
  59.3 3.9 %collective-permute-done.7 = bf16[2,1,32,2048]{3,2,0,1:T(8,128)(2,1)S(1)} collective-permute-done((bf16[2,1,32,2048]{3,2,0,1:T(8,128)(2,1)S(1)}, bf16[2,1,32,2048]{3,2,0,1:T(8,128)(2,1)S(1)}, u32[]{:S(2)}, u32[]{:S(2)}) %collective-permute-start.7) | collective-permute-done | bytes 262176 | tf_op jit(solution)/shard_map/ppermute | solution.py:58
  63.2 2.0 %collective-permute-start.4 = (bf16[2,2,32,2048]{3,2,1,0:T(8,128)(2,1)S(1)}, bf16[2,2,32,2048]{3,2,1,0:T(8,128)(2,1)S(1)}, u32[]{:S(2)}, u32[]{:S(2)}) collective-permute-start(bf16[2,2,32,2048]{3,2,1,0:T(8,128)(2,1)S(1)} %fusion.2), channel_id=1, source_target_pairs={{0,8},{4,20},{8,0},{12,28},{16,24},{20,4},{24,16},{28,12},{1,9},{5... | collective-permute-start | bytes 1572872 | tf_op jit(solution)/shard_map/ppermute | solution.py:58
  65.3 7.1 %collective-permute-done.4 = bf16[2,2,32,2048]{3,2,1,0:T(8,128)(2,1)S(1)} collective-permute-done((bf16[2,2,32,2048]{3,2,1,0:T(8,128)(2,1)S(1)}, bf16[2,2,32,2048]{3,2,1,0:T(8,128)(2,1)S(1)}, u32[]{:S(2)}, u32[]{:S(2)}) %collective-permute-start.4) | collective-permute-done | bytes 524320 | tf_op jit(solution)/shard_map/ppermute | solution.py:58
  72.4 1.7 %collective-permute-start.11 = (bf16[1,32,2048]{2,1,0:T(8,128)(2,1)S(1)}, bf16[1,32,2048]{2,1,0:T(8,128)(2,1)S(1)}, u32[]{:S(2)}, u32[]{:S(2)}) collective-permute-start(bf16[1,32,2048]{2,1,0:T(8,128)(2,1)S(1)} %get-tuple-element.33), channel_id=1, source_target_pairs={{0,16},{4,12},{8,24},{12,4},{16,0},{20,28},{24,8},{28,20},{1,17},{... | collective-permute-start | bytes 393224 | tf_op jit(solution)/shard_map/ppermute | solution.py:58
  74.1 0.1 fusion.1
  74.3 1.5 %collective-permute-start.10 = (bf16[1,32,2048]{2,1,0:T(8,128)(2,1)S(1)}, bf16[1,32,2048]{2,1,0:T(8,128)(2,1)S(1)}, u32[]{:S(2)}, u32[]{:S(2)}) collective-permute-start(bf16[1,32,2048]{2,1,0:T(8,128)(2,1)S(1)} %get-tuple-element.34), channel_id=1, source_target_pairs={{0,8},{4,20},{8,0},{12,28},{16,24},{20,4},{24,16},{28,12},{1,9},{5... | collective-permute-start | bytes 393224 | tf_op jit(solution)/shard_map/ppermute | solution.py:58
  75.8 0.9 collective-permute-start.8
  76.7 1.1 collective-permute-start.5
  77.9 0.4 collective-permute-done.11
  78.3 2.4 %collective-permute-done.10 = bf16[1,32,2048]{2,1,0:T(8,128)(2,1)S(1)} collective-permute-done((bf16[1,32,2048]{2,1,0:T(8,128)(2,1)S(1)}, bf16[1,32,2048]{2,1,0:T(8,128)(2,1)S(1)}, u32[]{:S(2)}, u32[]{:S(2)}) %collective-permute-start.10) | collective-permute-done | bytes 131104 | tf_op jit(solution)/shard_map/ppermute | solution.py:58
  80.8 2.8 %collective-permute-done.5 = bf16[1,2,32,2048]{3,2,1,0:T(8,128)(2,1)S(1)} collective-permute-done((bf16[1,2,32,2048]{3,2,1,0:T(8,128)(2,1)S(1)}, bf16[1,2,32,2048]{3,2,1,0:T(8,128)(2,1)S(1)}, u32[]{:S(2)}, u32[]{:S(2)}) %collective-permute-start.5) | collective-permute-done | bytes 262176 | tf_op jit(solution)/shard_map/ppermute | solution.py:58
  83.6 1.1 middle.1
  84.7 1.6 %collective-permute-start.16 = (f32[1,2304]{1,0:T(1,128)S(1)}, f32[1,2304]{1,0:T(1,128)S(1)}, u32[]{:S(2)}, u32[]{:S(2)}) collective-permute-start(f32[1,2304]{1,0:T(1,128)S(1)} %get-tuple-element.23), channel_id=1, source_target_pairs={{0,1},{1,0},{2,3},{3,2},{4,5},{5,4},{6,7},{7,6},{8,9},{9,8},{10,11... | collective-permute-start | bytes 27656 | tf_op jit(solution)/shard_map/ppermute | solution.py:70
  86.4 2.0 %collective-permute-start.17 = (f32[1,2304]{1,0:T(1,128)S(1)}, f32[1,2304]{1,0:T(1,128)S(1)}, u32[]{:S(2)}, u32[]{:S(2)}) collective-permute-start(f32[1,2304]{1,0:T(1,128)S(1)} %get-tuple-element.24), channel_id=1, source_target_pairs={{0,2},{1,3},{2,0},{3,1},{4,6},{5,7},{6,4},{7,5},{8,10},{9,11},{10,... | collective-permute-start | bytes 27656 | tf_op jit(solution)/shard_map/ppermute | solution.py:70
  88.3 0.9 collective-permute-start.18
  89.2 1.8 %collective-permute-done.17.refs_2_ = f32[1,2304]{1,0:T(1,128)S(1)} collective-permute-done((f32[1,2304]{1,0:T(1,128)S(1)}, f32[1,2304]{1,0:T(1,128)S(1)}, u32[]{:S(2)}, u32[]{:S(2)}) %collective-permute-start.17) | collective-permute-done | bytes 9248 | tf_op jit(solution)/shard_map/ppermute | solution.py:70
  90.9 2.9 %collective-permute-done.18.refs_3_ = f32[1,2304]{1,0:T(1,128)S(1)} collective-permute-done((f32[1,2304]{1,0:T(1,128)S(1)}, f32[1,2304]{1,0:T(1,128)S(1)}, u32[]{:S(2)}, u32[]{:S(2)}) %collective-permute-start.18) | collective-permute-done | bytes 9248 | tf_op jit(solution)/shard_map/ppermute | solution.py:70
  93.8 0.6 finish.1.refs_2_.refs_0_
  94.4 0.6 collective-permute-start.19
  95.0 0.6 collective-permute-start.22
  95.7 13.9 %collective-permute-done.19.refs_2_ = bf16[136,2048]{1,0:T(8,128)(2,1)S(1)} collective-permute-done((bf16[136,2048]{1,0:T(8,128)(2,1)S(1)}, bf16[136,2048]{1,0:T(8,128)(2,1)S(1)}, u32[]{:S(2)}, u32[]{:S(2)}) %collective-permute-start.19) | collective-permute-done | bytes 557088 | tf_op jit(solution)/shard_map/ppermute | solution.py:58
  109.6 0.5 collective-permute-start.24
  110.2 0.7 regroup.1.refs_0_
  111.0 8.2 %collective-permute-done.20.refs_2_.refs_6_ = bf16[136,2048]{1,0:T(8,128)(2,1)S(1)} collective-permute-done((bf16[136,2048]{1,0:T(8,128)(2,1)S(1)}, bf16[136,2048]{1,0:T(8,128)(2,1)S(1)}, u32[]{:S(2)}, u32[]{:S(2)}) %collective-permute-start.20) | collective-permute-done | bytes 557088 | tf_op jit(solution)/shard_map/ppermute | solution.py:58
  119.2 5.3 %quantized_sum.6.refs_4_ = f32[400,2048]{1,0:T(8,128)S(1)} custom-call(bf16[400,1024]{1,0:T(8,128)(2,1)S(1)} %regroup.1.refs_0_, f32[400,128]{1,0:T(8,128)S(1)} %get-tuple-element.15.refs_1_, bf16[136,2048]{1,0:T(8,128)(2,1)S(1)} %finish.1.refs_2_.refs_0_, bf16[136,2048]{1,0:T(8,128)(2,1)S(1)} %collective-permute-done.25.refs_3_.refs_1_), custom_call_target="tpu_custom_call" | custom-call | flops 1966080000 | tf_op jit(solution)/shard_map/quantized_sum/pallas_call | solution.py:338
  124.5 5.6 %quantized_sum.7.refs_3_ = f32[400,2048]{1,0:T(8,128)S(1)} custom-call(bf16[400,1024]{1,0:T(8,128)(2,1)S(1)} %regroup.1.refs_0_, f32[400,128]{1,0:T(8,128)S(1)} %get-tuple-element.15.refs_1_, bf16[136,2048]{1,0:T(8,128)(2,1)S(1)} %collective-permute-done.19.refs_2_, bf16[136,2048]{1,0:T(8,128)(2,1)S(1)} %collective-permute-done.24.refs_3_.refs_5_, ...), custom_call_target="tpu_custom_call" | custom-call | flops 1966080000 | tf_op jit(solution)/shard_map/quantized_sum/pallas_call | solution.py:338
  130.1 2.8 %quantized_sum.8.refs_3_ = f32[400,2048]{1,0:T(8,128)S(1)} custom-call(bf16[400,1024]{1,0:T(8,128)(2,1)S(1)} %regroup.1.refs_0_, f32[400,128]{1,0:T(8,128)S(1)} %get-tuple-element.15.refs_1_, bf16[136,2048]{1,0:T(8,128)(2,1)S(1)} %collective-permute-done.22.refs_2_.refs_4_, f32[400,2048]{1,0:T(8,128)S(1)} %quantized_sum.7.refs_3_), custom_call_target="tpu_custom_call" | custom-call | flops 983040000 | tf_op jit(solution)/shard_map/quantized_sum/pallas_call | solution.py:338
  132.9 2.8 %quantized_sum.9.refs_3_ = f32[400,2048]{1,0:T(8,128)S(1)} custom-call(bf16[400,1024]{1,0:T(8,128)(2,1)S(1)} %regroup.1.refs_0_, f32[400,128]{1,0:T(8,128)S(1)} %get-tuple-element.15.refs_1_, bf16[136,2048]{1,0:T(8,128)(2,1)S(1)} %collective-permute-done.23.refs_2_.refs_3_, f32[400,2048]{1,0:T(8,128)S(1)} %quantized_sum.8.refs_3_), custom_call_target="tpu_custom_call" | custom-call | flops 983040000 | tf_op jit(solution)/shard_map/quantized_sum/pallas_call | solution.py:338
  135.7 2.8 %quantized_sum.10.refs_3_ = f32[400,2048]{1,0:T(8,128)S(1)} custom-call(bf16[400,1024]{1,0:T(8,128)(2,1)S(1)} %regroup.1.refs_0_, f32[400,128]{1,0:T(8,128)S(1)} %get-tuple-element.15.refs_1_, bf16[136,2048]{1,0:T(8,128)(2,1)S(1)} %collective-permute-done.20.refs_2_.refs_6_, f32[400,2048]{1,0:T(8,128)S(1)} %quantized_sum.9.refs_3_), custom_call_target="tpu_custom_call" | custom-call | flops 983040000 | tf_op jit(solution)/shard_map/quantized_sum/pallas_call | solution.py:338
  138.6 0.1 gain.1
  138.7 0.8 collective-permute-start.28
  139.5 3.6 %collective-permute-start.26 = (f32[1,2048]{1,0:T(1,128)S(1)}, f32[1,2048]{1,0:T(1,128)S(1)}, u32[]{:S(2)}, u32[]{:S(2)}) collective-permute-start(f32[1,2048]{1,0:T(1,128)S(1)} %gain.1), channel_id=1, source_target_pairs={{0,1},{1,0},{2,3},{3,2},{4,5},{5,4},{6,7},{7,6},{8,9},{9,8},{10,11... | collective-permute-start | bytes 24584 | tf_op jit(solution)/shard_map/ppermute | solution.py:70
  143.1 4.5 %quantized_sum.11 = f32[400,2048]{1,0:T(8,128)} custom-call(bf16[400,1024]{1,0:T(8,128)(2,1)S(1)} %regroup.1.refs_0_, f32[400,128]{1,0:T(8,128)S(1)} %get-tuple-element.15.refs_1_, bf16[136,2048]{1,0:T(8,128)(2,1)S(1)} %collective-permute-done.21.refs_2_.refs_7_, f32[400,2048]{1,0:T(8,128)S(1)} %quantized_sum.10.refs_3_), custom_call_target="tpu_custom_call" | custom-call | flops 983040000 | tf_op jit(solution)/shard_map/quantized_sum/pallas_call | solution.py:338
  147.7 0.6 gather_fusion
  148.3 0.1 select_bitcast_fusion
  148.3 0.6 copy.21
  (52 shorter events, 0.8 us)
Async XLA Ops:
  0.6 26.7 %copy-start = (bf16[400,2048]{1,0:T(8,128)(2,1)S(1)}, bf16[400,2048]{1,0:T(8,128)(2,1)}, u32[]{:S(2)}) copy-start(bf16[400,2048]{1,0:T(8,128)(2,1)} %param.10) | copy-start | bytes 4915204
  2.6 13.5 %all-to-all-start = ((bf16[8,48,400]{2,1,0:T(8,128)(2,1)}), bf16[8,48,400]{2,1,0:T(8,128)(2,1)S(1)}, u32[]{:S(2)}, u32[]{:S(2)}) async-start(bf16[8,48,400]{2,1,0:T(8,128)(2,1)} %pack.1), calls=%async_computation | async-start | bytes 786432 | tf_op jit(solution)/shard_map/all_to_all | solution.py:407
  16.4 11.0 %collective-permute-start.1 = (bf16[400,256]{1,0:T(8,128)(2,1)S(1)}, bf16[400,256]{1,0:T(8,128)(2,1)S(1)}, u32[]{:S(2)}, u32[]{:S(2)}) collective-permute-start(bf16[400,256]{1,0:T(8,128)(2,1)S(1)} %get-tuple-element.14.refs_0_), channel_id=1, source_target_pairs={{0,2},{1,3},{2,0},{3,1},{4,6},{5,7},{6,4},{7,5},{8,10},{9,11},{10,... | collective-permute-start | bytes 614408 | tf_op jit(solution)/shard_map/ppermute | solution.py:70
  19.0 8.9 %collective-permute-start = (bf16[400,256]{1,0:T(8,128)(2,1)S(1)}, bf16[400,256]{1,0:T(8,128)(2,1)S(1)}, u32[]{:S(2)}, u32[]{:S(2)}) collective-permute-start(bf16[400,256]{1,0:T(8,128)(2,1)S(1)} %get-tuple-element.14.refs_0_), channel_id=1, source_target_pairs={{0,1},{1,0},{2,3},{3,2},{4,5},{5,4},{6,7},{7,6},{8,9},{9,8},{10,11... | collective-permute-start | bytes 614408 | tf_op jit(solution)/shard_map/ppermute | solution.py:70
  27.8 25.1 %collective-permute-start.6 = (bf16[4,1,32,2048]{3,2,0,1:T(8,128)(2,1)S(1)}, bf16[4,1,32,2048]{3,2,0,1:T(8,128)(2,1)S(1)}, u32[]{:S(2)}, u32[]{:S(2)}) collective-permute-start(bf16[4,1,32,2048]{3,2,0,1:T(8,128)(2,1)S(1)} %bitcast.101), channel_id=1, source_target_pairs={{0,4},{4,0},{8,12},{12,8},{16,20},{20,16},{24,28},{28,24},{1,5},{5... | collective-permute-start | bytes 1572872 | tf_op jit(solution)/shard_map/ppermute | solution.py:41
  28.7 1.1 copy-start.5
  29.9 44.4 %collective-permute-start.15 = (bf16[48,2048]{1,0:T(8,128)(2,1)S(1)}, bf16[48,2048]{1,0:T(8,128)(2,1)S(1)}, u32[]{:S(2)}, u32[]{:S(2)}) collective-permute-start(bf16[48,2048]{1,0:T(8,128)(2,1)S(1)} %get-tuple-element.28), channel_id=1, source_target_pairs={{0,3},{1,2},{2,1},{3,0},{4,7},{5,6},{6,5},{7,4},{8,11},{9,10},{10,... | collective-permute-start | bytes 589832 | tf_op jit(solution)/shard_map/ppermute | solution.py:70
  33.4 42.4 %collective-permute-start.14 = (bf16[48,2048]{1,0:T(8,128)(2,1)S(1)}, bf16[48,2048]{1,0:T(8,128)(2,1)S(1)}, u32[]{:S(2)}, u32[]{:S(2)}) collective-permute-start(bf16[48,2048]{1,0:T(8,128)(2,1)S(1)} %get-tuple-element.29), channel_id=1, source_target_pairs={{0,2},{1,3},{2,0},{3,1},{4,6},{5,7},{6,4},{7,5},{8,10},{9,11},{10,... | collective-permute-start | bytes 589832 | tf_op jit(solution)/shard_map/ppermute | solution.py:70
  33.4 43.3 %collective-permute-start.13 = (bf16[48,2048]{1,0:T(8,128)(2,1)S(1)}, bf16[48,2048]{1,0:T(8,128)(2,1)S(1)}, u32[]{:S(2)}, u32[]{:S(2)}) collective-permute-start(bf16[48,2048]{1,0:T(8,128)(2,1)S(1)} %get-tuple-element.30), channel_id=1, source_target_pairs={{0,1},{1,0},{2,3},{3,2},{4,5},{5,4},{6,7},{7,6},{8,9},{9,8},{10,11... | collective-permute-start | bytes 589832 | tf_op jit(solution)/shard_map/ppermute | solution.py:70
  35.1 16.9 %collective-permute-start.2 = (bf16[400,256]{1,0:T(8,128)(2,1)S(1)}, bf16[400,256]{1,0:T(8,128)(2,1)S(1)}, u32[]{:S(2)}, u32[]{:S(2)}) collective-permute-start(bf16[400,256]{1,0:T(8,128)(2,1)S(1)} %collective-permute-done.1.refs_2_), channel_id=1, source_target_pairs={{0,1},{1,0},{2,3},{3,2},{4,5},{5,4},{6,7},{7,6},{8,9},{9,8},{10,11... | collective-permute-start | bytes 614408 | tf_op jit(solution)/shard_map/ppermute | solution.py:70
  52.0 5.7 %collective-permute-start.3 = (bf16[4,2,32,2048]{3,2,1,0:T(8,128)(2,1)S(1)}, bf16[4,2,32,2048]{3,2,1,0:T(8,128)(2,1)S(1)}, u32[]{:S(2)}, u32[]{:S(2)}) collective-permute-start(bf16[4,2,32,2048]{3,2,1,0:T(8,128)(2,1)S(1)} %bitcast.100), channel_id=1, source_target_pairs={{0,4},{4,0},{8,12},{12,8},{16,20},{20,16},{24,28},{28,24},{1,5},{5... | collective-permute-start | bytes 3145736 | tf_op jit(solution)/shard_map/ppermute | solution.py:41
  53.0 2.4 %collective-permute-start.9 = (bf16[4,1,32,2048]{3,2,1,0:T(8,128)(2,1)S(1)}, bf16[4,1,32,2048]{3,2,1,0:T(8,128)(2,1)S(1)}, u32[]{:S(2)}, u32[]{:S(2)}) collective-permute-start(bf16[4,1,32,2048]{3,2,1,0:T(8,128)(2,1)S(1)} %bitcast.102), channel_id=1, source_target_pairs={{0,4},{4,0},{8,12},{12,8},{16,20},{20,16},{24,28},{28,24},{1,5},{5... | collective-permute-start | bytes 1572872 | tf_op jit(solution)/shard_map/ppermute | solution.py:41
  55.4 7.8 %collective-permute-start.7 = (bf16[2,1,32,2048]{3,2,0,1:T(8,128)(2,1)S(1)}, bf16[2,1,32,2048]{3,2,0,1:T(8,128)(2,1)S(1)}, u32[]{:S(2)}, u32[]{:S(2)}) collective-permute-start(bf16[2,1,32,2048]{3,2,0,1:T(8,128)(2,1)S(1)} %fusion.6), channel_id=1, source_target_pairs={{0,8},{4,20},{8,0},{12,28},{16,24},{20,4},{24,16},{28,12},{1,9},{5... | collective-permute-start | bytes 786440 | tf_op jit(solution)/shard_map/ppermute | solution.py:58
  57.7 20.2 %collective-permute-start.12 = (bf16[1,32,2048]{2,1,0:T(8,128)(2,1)S(1)}, bf16[1,32,2048]{2,1,0:T(8,128)(2,1)S(1)}, u32[]{:S(2)}, u32[]{:S(2)}) collective-permute-start(bf16[1,32,2048]{2,1,0:T(8,128)(2,1)S(1)} %get-tuple-element.32), channel_id=1, source_target_pairs={{0,24},{4,28},{8,16},{12,20},{16,8},{20,12},{24,0},{28,4},{1,25},{... | collective-permute-start | bytes 393224 | tf_op jit(solution)/shard_map/ppermute | solution.py:65
  63.2 9.2 %collective-permute-start.4 = (bf16[2,2,32,2048]{3,2,1,0:T(8,128)(2,1)S(1)}, bf16[2,2,32,2048]{3,2,1,0:T(8,128)(2,1)S(1)}, u32[]{:S(2)}, u32[]{:S(2)}) collective-permute-start(bf16[2,2,32,2048]{3,2,1,0:T(8,128)(2,1)S(1)} %fusion.2), channel_id=1, source_target_pairs={{0,8},{4,20},{8,0},{12,28},{16,24},{20,4},{24,16},{28,12},{1,9},{5... | collective-permute-start | bytes 1572872 | tf_op jit(solution)/shard_map/ppermute | solution.py:58
  72.4 5.9 %collective-permute-start.11 = (bf16[1,32,2048]{2,1,0:T(8,128)(2,1)S(1)}, bf16[1,32,2048]{2,1,0:T(8,128)(2,1)S(1)}, u32[]{:S(2)}, u32[]{:S(2)}) collective-permute-start(bf16[1,32,2048]{2,1,0:T(8,128)(2,1)S(1)} %get-tuple-element.33), channel_id=1, source_target_pairs={{0,16},{4,12},{8,24},{12,4},{16,0},{20,28},{24,8},{28,20},{1,17},{... | collective-permute-start | bytes 393224 | tf_op jit(solution)/shard_map/ppermute | solution.py:58
  74.2 9.4 %copy-start.1 = (f32[8192]{0:T(1024)S(1)}, f32[8192]{0:T(1024)}, u32[]{:S(2)}) copy-start(f32[8192]{0:T(1024)} %param.13) | copy-start | bytes 98308
  74.2 9.4 %copy-start.2 = (f32[4,1,2048]{2,1,0:T(1,128)S(1)}, f32[4,1,2048]{2,1,0:T(1,128)}, u32[]{:S(2)}) copy-start(f32[4,1,2048]{2,1,0:T(1,128)} %get-tuple-element.16.part_ref) | copy-start | bytes 98308
  74.2 9.4 %copy-start.4 = (s32[1,128]{1,0:T(1,128)S(1)}, s32[1,128]{1,0:T(1,128)}, u32[]{:S(2)}) copy-start(s32[1,128]{1,0:T(1,128)} %row_ref.3) | copy-start | bytes 1540
  74.3 6.4 %collective-permute-start.10 = (bf16[1,32,2048]{2,1,0:T(8,128)(2,1)S(1)}, bf16[1,32,2048]{2,1,0:T(8,128)(2,1)S(1)}, u32[]{:S(2)}, u32[]{:S(2)}) collective-permute-start(bf16[1,32,2048]{2,1,0:T(8,128)(2,1)S(1)} %get-tuple-element.34), channel_id=1, source_target_pairs={{0,8},{4,20},{8,0},{12,28},{16,24},{20,4},{24,16},{28,12},{1,9},{5... | collective-permute-start | bytes 393224 | tf_op jit(solution)/shard_map/ppermute | solution.py:58
  75.8 5.0 %collective-permute-start.8 = (bf16[1,1,32,2048]{3,2,1,0:T(8,128)(2,1)S(1)}, bf16[1,1,32,2048]{3,2,1,0:T(8,128)(2,1)S(1)}, u32[]{:S(2)}, u32[]{:S(2)}) collective-permute-start(bf16[1,1,32,2048]{3,2,1,0:T(8,128)(2,1)S(1)} %fusion.14), channel_id=1, source_target_pairs={{0,16},{4,12},{8,24},{12,4},{16,0},{20,28},{24,8},{28,20},{1,17},{... | collective-permute-start | bytes 393224 | tf_op jit(solution)/shard_map/ppermute | solution.py:58
  76.7 6.9 %collective-permute-start.5 = (bf16[1,2,32,2048]{3,2,1,0:T(8,128)(2,1)S(1)}, bf16[1,2,32,2048]{3,2,1,0:T(8,128)(2,1)S(1)}, u32[]{:S(2)}, u32[]{:S(2)}) collective-permute-start(bf16[1,2,32,2048]{3,2,1,0:T(8,128)(2,1)S(1)} %fusion.5), channel_id=1, source_target_pairs={{0,16},{4,12},{8,24},{12,4},{16,0},{20,28},{24,8},{28,20},{1,17},{... | collective-permute-start | bytes 786440 | tf_op jit(solution)/shard_map/ppermute | solution.py:58
  77.9 15.9 %copy-start.3 = (f32[1,2048]{1,0:T(1,128)S(1)}, f32[1,2048]{1,0:T(1,128)}, u32[]{:S(2)}) copy-start(f32[1,2048]{1,0:T(1,128)} %draw_ref.1) | copy-start | bytes 24580
  84.7 4.4 %collective-permute-start.16 = (f32[1,2304]{1,0:T(1,128)S(1)}, f32[1,2304]{1,0:T(1,128)S(1)}, u32[]{:S(2)}, u32[]{:S(2)}) collective-permute-start(f32[1,2304]{1,0:T(1,128)S(1)} %get-tuple-element.23), channel_id=1, source_target_pairs={{0,1},{1,0},{2,3},{3,2},{4,5},{5,4},{6,7},{7,6},{8,9},{9,8},{10,11... | collective-permute-start | bytes 27656 | tf_op jit(solution)/shard_map/ppermute | solution.py:70
  86.4 4.6 %collective-permute-start.17 = (f32[1,2304]{1,0:T(1,128)S(1)}, f32[1,2304]{1,0:T(1,128)S(1)}, u32[]{:S(2)}, u32[]{:S(2)}) collective-permute-start(f32[1,2304]{1,0:T(1,128)S(1)} %get-tuple-element.24), channel_id=1, source_target_pairs={{0,2},{1,3},{2,0},{3,1},{4,6},{5,7},{6,4},{7,5},{8,10},{9,11},{10,... | collective-permute-start | bytes 27656 | tf_op jit(solution)/shard_map/ppermute | solution.py:70
  88.3 5.5 %collective-permute-start.18 = (f32[1,2304]{1,0:T(1,128)S(1)}, f32[1,2304]{1,0:T(1,128)S(1)}, u32[]{:S(2)}, u32[]{:S(2)}) collective-permute-start(f32[1,2304]{1,0:T(1,128)S(1)} %get-tuple-element.25), channel_id=1, source_target_pairs={{0,3},{1,2},{2,1},{3,0},{4,7},{5,6},{6,5},{7,4},{8,11},{9,10},{10,... | collective-permute-start | bytes 27656 | tf_op jit(solution)/shard_map/ppermute | solution.py:70
  94.4 15.2 %collective-permute-start.19 = (bf16[136,2048]{1,0:T(8,128)(2,1)S(1)}, bf16[136,2048]{1,0:T(8,128)(2,1)S(1)}, u32[]{:S(2)}, u32[]{:S(2)}) collective-permute-start(bf16[136,2048]{1,0:T(8,128)(2,1)S(1)} %finish.1.refs_2_.refs_0_), channel_id=1, source_target_pairs={{0,8},{4,20},{8,0},{12,28},{16,24},{20,4},{24,16},{28,12},{1,9},{5... | collective-permute-start | bytes 1671176 | tf_op jit(solution)/shard_map/ppermute | solution.py:58
  95.0 15.1 %collective-permute-start.22 = (bf16[136,2048]{1,0:T(8,128)(2,1)S(1)}, bf16[136,2048]{1,0:T(8,128)(2,1)S(1)}, u32[]{:S(2)}, u32[]{:S(2)}) collective-permute-start(bf16[136,2048]{1,0:T(8,128)(2,1)S(1)} %finish.1.refs_2_.refs_0_), channel_id=1, source_target_pairs={{0,16},{4,12},{8,24},{12,4},{16,0},{20,28},{24,8},{28,20},{1,17},{... | collective-permute-start | bytes 1671176 | tf_op jit(solution)/shard_map/ppermute | solution.py:58
  109.6 9.5 %collective-permute-start.20 = (bf16[136,2048]{1,0:T(8,128)(2,1)S(1)}, bf16[136,2048]{1,0:T(8,128)(2,1)S(1)}, u32[]{:S(2)}, u32[]{:S(2)}) collective-permute-start(bf16[136,2048]{1,0:T(8,128)(2,1)S(1)} %collective-permute-done.19.refs_2_), channel_id=1, source_target_pairs={{0,16},{4,12},{8,24},{12,4},{16,0},{20,28},{24,8},{28,20},{1,17},{... | collective-permute-start | bytes 1671176 | tf_op jit(solution)/shard_map/ppermute | solution.py:58
  109.6 9.5 %collective-permute-start.25 = (bf16[136,2048]{1,0:T(8,128)(2,1)S(1)}, bf16[136,2048]{1,0:T(8,128)(2,1)S(1)}, u32[]{:S(2)}, u32[]{:S(2)}) collective-permute-start(bf16[136,2048]{1,0:T(8,128)(2,1)S(1)} %finish.1.refs_2_.refs_0_), channel_id=1, source_target_pairs={{0,4},{4,0},{8,12},{12,8},{16,20},{20,16},{24,28},{28,24},{1,5},{5... | collective-permute-start | bytes 1671176 | tf_op jit(solution)/shard_map/ppermute | solution.py:41
  109.6 14.9 %collective-permute-start.24 = (bf16[136,2048]{1,0:T(8,128)(2,1)S(1)}, bf16[136,2048]{1,0:T(8,128)(2,1)S(1)}, u32[]{:S(2)}, u32[]{:S(2)}) collective-permute-start(bf16[136,2048]{1,0:T(8,128)(2,1)S(1)} %collective-permute-done.19.refs_2_), channel_id=1, source_target_pairs={{0,4},{4,0},{8,12},{12,8},{16,20},{20,16},{24,28},{28,24},{1,5},{5... | collective-permute-start | bytes 1671176 | tf_op jit(solution)/shard_map/ppermute | solution.py:41
  110.1 22.8 %collective-permute-start.23 = (bf16[136,2048]{1,0:T(8,128)(2,1)S(1)}, bf16[136,2048]{1,0:T(8,128)(2,1)S(1)}, u32[]{:S(2)}, u32[]{:S(2)}) collective-permute-start(bf16[136,2048]{1,0:T(8,128)(2,1)S(1)} %collective-permute-done.22.refs_2_.refs_4_), channel_id=1, source_target_pairs={{0,4},{4,0},{8,12},{12,8},{16,20},{20,16},{24,28},{28,24},{1,5},{5... | collective-permute-start | bytes 1671176 | tf_op jit(solution)/shard_map/ppermute | solution.py:41
  119.1 19.4 %collective-permute-start.21 = (bf16[136,2048]{1,0:T(8,128)(2,1)S(1)}, bf16[136,2048]{1,0:T(8,128)(2,1)S(1)}, u32[]{:S(2)}, u32[]{:S(2)}) collective-permute-start(bf16[136,2048]{1,0:T(8,128)(2,1)S(1)} %collective-permute-done.20.refs_2_.refs_6_), channel_id=1, source_target_pairs={{0,4},{4,0},{8,12},{12,8},{16,20},{20,16},{24,28},{28,24},{1,5},{5... | collective-permute-start | bytes 1671176 | tf_op jit(solution)/shard_map/ppermute | solution.py:41
  138.7 9.0 %collective-permute-start.28 = (f32[1,2048]{1,0:T(1,128)S(1)}, f32[1,2048]{1,0:T(1,128)S(1)}, u32[]{:S(2)}, u32[]{:S(2)}) collective-permute-start(f32[1,2048]{1,0:T(1,128)S(1)} %gain.1), channel_id=1, source_target_pairs={{0,3},{1,2},{2,1},{3,0},{4,7},{5,6},{6,5},{7,4},{8,11},{9,10},{10,... | collective-permute-start | bytes 24584 | tf_op jit(solution)/shard_map/ppermute | solution.py:70
  139.5 8.1 %collective-permute-start.27 = (f32[1,2048]{1,0:T(1,128)S(1)}, f32[1,2048]{1,0:T(1,128)S(1)}, u32[]{:S(2)}, u32[]{:S(2)}) collective-permute-start(f32[1,2048]{1,0:T(1,128)S(1)} %gain.1), channel_id=1, source_target_pairs={{0,2},{1,3},{2,0},{3,1},{4,6},{5,7},{6,4},{7,5},{8,10},{9,11},{10,... | collective-permute-start | bytes 24584 | tf_op jit(solution)/shard_map/ppermute | solution.py:70
  139.5 8.1 %collective-permute-start.26 = (f32[1,2048]{1,0:T(1,128)S(1)}, f32[1,2048]{1,0:T(1,128)S(1)}, u32[]{:S(2)}, u32[]{:S(2)}) collective-permute-start(f32[1,2048]{1,0:T(1,128)S(1)} %gain.1), channel_id=1, source_target_pairs={{0,1},{1,0},{2,3},{3,2},{4,5},{5,4},{6,7},{7,6},{8,9},{9,8},{10,11... | collective-permute-start | bytes 24584 | tf_op jit(solution)/shard_map/ppermute | solution.py:70

commit v4 on v3

--- a/solution.py
+++ b/solution.py
@@ -180,12 +180,15 @@
         out_ref[step] = jnp.dot(select, cot, preferred_element_type=FLOAT).astype(HALF)
 
 
-def quantize_kernel(slots, replicas, adds, *refs):
+def quantize_kernel(slots, replicas, adds, chunks, *refs):
     count = len(slots)
     tile_ref, meta_ref = refs[:2]
     loads = refs[2 : count + 2]
     total_ref = refs[count + 2] if adds else None
-    out_ref, gradient, half_draw, row_half, lever, weight = refs[-6:]
+    out_ref, gradient, half_draw, row_half, lever, weight = refs[count + 2 + adds :][:6]
+    if chunks > 1:
+        result, sems = out_ref, refs[-1]
+        out_ref = refs[-2]
     rows, columns = out_ref.shape
     tokens = tile_ref.shape[1] // replicas
     groups = rows // 8
@@ -240,7 +243,19 @@
                 out_ref[cut, strip] = term
             return carry
 
-        lax.fori_loop(0, groups, group, 0, unroll=unroll)
+        if chunks == 1 or index < count - 1:
+            lax.fori_loop(0, groups, group, 0, unroll=unroll)
+            continue
+        copies = []
+        for chunk in range(chunks):
+            size = groups // chunks
+            lax.fori_loop(chunk * size, (chunk + 1) * size, group, 0, unroll=unroll)
+            cut = pl.ds(chunk * size * 8, size * 8)
+            copy = pltpu.make_async_copy(out_ref.at[cut, :], result.at[cut, :], sems.at[chunk])
+            copy.start()
+            copies.append(copy)
+        for copy in copies:
+            copy.wait()
 
 
 def own_gain(gain_ref, mine, columns):
@@ -331,14 +346,15 @@
     refs[-1][...] = total / replicas
 
 
-def quantized_sum(tiles, meta, loads, slots, replicas, total):
+def quantized_sum(tiles, meta, loads, slots, replicas, total, last):
     rows = tiles.shape[0]
     columns = loads[0].shape[1]
     adds = total is not None
+    chunks = 5 if last and rows % 200 == 0 else 1
     return pl.pallas_call(
-        functools.partial(quantize_kernel, slots, replicas, adds),
+        functools.partial(quantize_kernel, slots, replicas, adds, chunks),
         in_specs=[whole()] * (len(slots) + 2 + adds),
-        out_specs=whole(),
+        out_specs=anywhere() if chunks > 1 else whole(),
         out_shape=jax.ShapeDtypeStruct((rows, columns), FLOAT),
         scratch_shapes=[
             pltpu.VMEM((rows, columns), FLOAT),
@@ -346,12 +362,16 @@
             pltpu.VMEM((rows, 128), FLOAT),
             pltpu.VMEM((rows, 128), FLOAT),
             pltpu.VMEM((rows, 128), FLOAT),
-        ],
+        ]
+        + (
+            [pltpu.VMEM((rows, columns), FLOAT), pltpu.SemaphoreType.DMA((chunks,))]
+            if chunks > 1
+            else []
+        ),
         compiler_params=grant(12),
         cost_estimate=pl.CostEstimate(
             flops=len(slots) * rows * columns * 1200, bytes_accessed=0, transcendentals=0
         ),
-        name="quantized_sum",
     )(tiles, meta, *loads, *([total] if adds else []))
 
 
@@ -402,7 +422,6 @@
         ],
         out_shape=jax.ShapeDtypeStruct((replicas, tile_rows + META_ROWS, width), HALF),
         compiler_params=grant(60),
-        name="pack",
     )(tile_tokens[0], bucket_levels[0], row_draws[0])
     exchanged = lax.all_to_all(packed, "dp", 0, 0, tiled=True)
     own_tile, meta = pl.pallas_call(
@@ -418,14 +437,13 @@
             pltpu.VMEM((lanes(2 * replicas), lanes(width)), FLOAT),
         ],
         compiler_params=grant(8),
-        name="unpack",
     )(here, exchanged)
     tile_blocks = [own_tile]
     for step in range(1, seq_count):
         low = step & -step
         tile_blocks.append(swap(tile_blocks[step ^ low], low))
 
-    outgoing, text_parts = pl.pallas_call(
+    text_call = pl.pallas_call(
         text_kernel,
         in_specs=[scalar()] + [whole()] * 2 + [anywhere()] * 2,
         out_specs=[whole()] * 2,
@@ -442,8 +460,10 @@
             flops=tok_rows * model_width * 4000, bytes_accessed=0, transcendentals=0
         ),
         compiler_params=grant(60),
-        name="text_part",
-    )(there, placeholders, places.reshape(image_total, 1), text_hidden[0], cotangent[0])
+    )
+    outgoing, text_parts = text_call(
+        there, placeholders, places.reshape(image_total, 1), text_hidden[0], cotangent[0]
+    )
 
     weight = jnp.pad(proj_weight, ((0, padded - width), (0, 0)))
     even = (replicas // 2) * tile_rows
@@ -469,7 +489,7 @@
                 returned.append(swap(outgoing[step], step))
         arrived = flip(sent, 0)
         held = held + arrived.astype(FLOAT)
-        if levels_of_bits == 3 and part == len(parts) - 1:
+        if levels_of_bits == 3 and part > 0:
             sums = [held[0]]
             for place in (1, 2, 3):
                 sent = held[place].astype(HALF)
@@ -497,7 +517,6 @@
         ]
         + [jax.ShapeDtypeStruct((1, 2 * image_total + columns), FLOAT)] * seq_count,
         compiler_params=grant(16),
-        name="middle",
     )(there, placeholders, norm_gain.reshape(1, -1), text_parts, *summands, *returned)
     embedded, image_cot = middle[:2]
     stats = [middle[2]]
@@ -510,10 +529,9 @@
         out_shape=jax.ShapeDtypeStruct((image_total + EXTRA_ROWS, columns), HALF),
         scratch_shapes=[pltpu.VMEM((128, image_total), FLOAT)],
         compiler_params=grant(12),
-        name="finish",
     )(there, norm_gain.reshape(1, -1), embedded, image_cot, column_draws, *stats)
 
-    tiles = pl.pallas_call(
+    regroup = pl.pallas_call(
         functools.partial(regroup_kernel, order, tile_rows),
         in_specs=[whole()] * seq_count,
         out_specs=whole(),
@@ -522,8 +540,8 @@
             flops=replicas * padded * image_total * 2000, bytes_accessed=0, transcendentals=0
         ),
         compiler_params=grant(8),
-        name="regroup",
-    )(*tile_blocks)
+    )
+    tiles = regroup(*tile_blocks)
 
     loads = {0: own_load}
     if levels_of_bits == 3:
@@ -534,7 +552,7 @@
         loads[3] = flip(loads[4], 0)
         loads[6] = flip_label(loads[2], 2)
         loads[7] = flip(loads[6], 0)
-        batches = ((0, 1), (2, 5), (4,), (3,), (6,), (7,))
+        batches = ((0, 1), (2,), (5,), (4,), (3,), (6,), (7,))
     else:
         for bit in range(1, levels_of_bits):
             for slot, load in list(loads.items()):
@@ -548,14 +566,15 @@
         out_specs=whole(),
         out_shape=jax.ShapeDtypeStruct((1, columns), FLOAT),
         compiler_params=grant(12),
-        name="gain",
     )(*[loads[slot] for slot in range(replicas)])
     gains = [gain_row]
     for step in range(1, seq_count):
         gains.append(swap(gain_row, step))
     total = None
     for slots in batches:
-        total = quantized_sum(tiles, meta, [loads[slot] for slot in slots], slots, replicas, total)
+        total = quantized_sum(
+            tiles, meta, [loads[slot] for slot in slots], slots, replicas, total, slots == batches[-1]
+        )
     sources = jnp.arange(seq_count, dtype=jnp.int32) ^ there
     gain_total = jnp.take(jnp.concatenate(gains, axis=0), sources, axis=0)
     return total[:width], gain_total.reshape(model_width)

time: 149 us -> 146 us (0.980)
  waiting for transfers between devices: 68.9 us -> 65.6 us
  starting transfers between devices: 37 us -> 38.8 us
    ppermute x9, waiting for transfers between devices: 38.7 us -> 33.2 us  [flip_label(): lax.ppermute(value, 'dp', [(i, i ^ (odd if i % 2 else 1 << bit)) for i in...]
    ppermute x1 -> x2, waiting for transfers between devices: 0.01 us -> 3.07 us  [flip_far(): return lax.ppermute(value, 'dp', [(i, i ^ 6) for i in range(count)])]
    ppermute x1 -> x2, starting transfers between devices: 1.19 us -> 3.72 us  [flip_far(): return lax.ppermute(value, 'dp', [(i, i ^ 6) for i in range(count)])]
    pallas_call x8 -> x9, Pallas kernels: 29.6 us -> 28.9 us  [the longest x7 23.1 us: quantized_sum(): pl.pallas_call(functools.partial(quantize_kernel, slots, replicas, adds,...]
  transfers between devices with their start and end apart: 30 -> 31, of which waited for: 14 -> 13; matrix products, arithmetic and copies ran while one was open for 4% -> 4% of each run, Pallas kernels for 20% -> 20%
where the time goes in v4:
time: 146 us
  waiting for transfers between devices  65.6 us (45%)
  starting transfers between devices  38.8 us (27%)
  Pallas kernels  33 us (23%)
  matrix products  3.35 us (2%)
  local copies, waits for them, and re-layouts  3.3 us (2%)
    ppermute x9, waiting for transfers between devices, flip_label(): lax.ppermute(value, 'dp', [(i, i ^ (odd if i % 2 else 1 << bit)) for i in...  33.2 us
    ppermute x12, waiting for transfers between devices, swap(): return lax.ppermute(value, 'seq', [(i, i ^ step) for i in range(count)])  26.6 us
    pallas_call x7, Pallas kernels, quantized_sum(): pl.pallas_call(functools.partial(quantize_kernel, slots, replicas, adds,...  23.1 us
    ppermute x12, starting transfers between devices, swap(): return lax.ppermute(value, 'seq', [(i, i ^ step) for i in range(count)])  18.8 us
    ppermute x9, starting transfers between devices, flip_label(): lax.ppermute(value, 'dp', [(i, i ^ (odd if i % 2 else 1 << bit)) for i in...  9.84 us
    all_to_all x1, starting transfers between devices, on_device(): exchanged = lax.all_to_all(packed, 'dp', 0, 0, tiled=True)  5.21 us
    pallas_call x1, Pallas kernels, on_device(): text_call(there, placeholders, places.reshape(image_total, 1), text_hidde...  5.04 us
    ppermute x2, starting transfers between devices, flip_far(): return lax.ppermute(value, 'dp', [(i, i ^ 6) for i in range(count)])  3.72 us
  transfers between devices with their start and end apart: 31, of which 13 were waited for; matrix products, arithmetic and copies ran while one was open for 4% of the time, Pallas kernels for 20%

profile of v4, /device:TPU:0, one launch (start us, length us, event | category | flops | bytes accessed | tf_op | source)
XLA Modules:
  0.0 146.0 jit_solution(14784319256813713976)
XLA Ops:
  0.6 2.0 %shard_map.104 = bf16[8,48,400]{2,1,0:T(8,128)(2,1)} custom-call(bf16[32,3200]{1,0:T(8,128)(2,1)} %bitcast.98, s32[1,3200]{1,0:T(1,128)} %bitcast.100, f32[1,3200]{1,0:T(1,128)} %bitcast.101), custom_call_target="tpu_custom_call" | custom-call | tf_op jit(solution)/shard_map/pallas_call | solution.py:413
  2.6 5.2 %all-to-all-start = ((bf16[8,48,400]{2,1,0:T(8,128)(2,1)}), bf16[8,48,400]{2,1,0:T(8,128)(2,1)S(1)}, u32[]{:S(2)}, u32[]{:S(2)}) async-start(bf16[8,48,400]{2,1,0:T(8,128)(2,1)} %shard_map.104), calls=%async_computation | async-start | bytes 786432 | tf_op jit(solution)/shard_map/all_to_all | solution.py:426
  7.9 1.4 copy.12.column_ref
  9.2 5.0 %shard_map.107 = (bf16[4,48,2048]{2,1,0:T(8,128)(2,1)}, f32[4,1,2048]{2,1,0:T(1,128)}) custom-call(s32[1]{0:T(128)} %bitcast.4.place_ref, s32[1,128]{1,0:T(1,128)} %row_ref.3, s32[128,1]{1,0:T(8,128)} %copy.12.column_ref, bf16[128,8192]{1,0:T(8,128)(2,1)} %bitcast.102, bf16[128,8192]{1,0:T(8,128)(2,1)} %bitcast.103), custom_call_target="tpu_custom_call" | custom-call | flops 4194304000 | tf_op jit(solution)/shard_map/pallas_call | solution.py:464
  14.3 1.9 %all-to-all-done.in_ref = bf16[8,48,400]{2,1,0:T(8,128)(2,1)S(1)} async-done(((bf16[8,48,400]{2,1,0:T(8,128)(2,1)}), bf16[8,48,400]{2,1,0:T(8,128)(2,1)S(1)}, u32[]{:S(2)}, u32[]{:S(2)}) %all-to-all-start) | async-done | bytes 307232 | tf_op jit(solution)/shard_map/all_to_all | solution.py:426
  16.2 0.2 shard_map.105
  16.4 2.7 %collective-permute-start.1 = (bf16[400,256]{1,0:T(8,128)(2,1)S(1)}, bf16[400,256]{1,0:T(8,128)(2,1)S(1)}, u32[]{:S(2)}, u32[]{:S(2)}) collective-permute-start(bf16[400,256]{1,0:T(8,128)(2,1)S(1)} %get-tuple-element.14.refs_0_), channel_id=1, source_target_pairs={{0,2},{1,3},{2,0},{3,1},{4,6},{5,7},{6,4},{7,5},{8,10},{9,11},{10,... | collective-permute-start | bytes 614408 | tf_op jit(solution)/shard_map/ppermute | solution.py:70
  19.0 1.6 %collective-permute-start = (bf16[400,256]{1,0:T(8,128)(2,1)S(1)}, bf16[400,256]{1,0:T(8,128)(2,1)S(1)}, u32[]{:S(2)}, u32[]{:S(2)}) collective-permute-start(bf16[400,256]{1,0:T(8,128)(2,1)S(1)} %get-tuple-element.14.refs_0_), channel_id=1, source_target_pairs={{0,1},{1,0},{2,3},{3,2},{4,5},{5,4},{6,7},{7,6},{8,9},{9,8},{10,11... | collective-permute-start | bytes 614408 | tf_op jit(solution)/shard_map/ppermute | solution.py:70
  20.6 6.7 %collective-permute-done.1.refs_2_ = bf16[400,256]{1,0:T(8,128)(2,1)S(1)} collective-permute-done((bf16[400,256]{1,0:T(8,128)(2,1)S(1)}, bf16[400,256]{1,0:T(8,128)(2,1)S(1)}, u32[]{:S(2)}, u32[]{:S(2)}) %collective-permute-start.1) | collective-permute-done | bytes 204832 | tf_op jit(solution)/shard_map/ppermute | solution.py:70
  27.4 0.5 convolution_convert_fusion.2
  28.0 0.7 convolution_convert_fusion
  28.8 0.3 copy-done.5
  29.2 3.6 %collective-permute-start.16 = (bf16[48,2048]{1,0:T(8,128)(2,1)S(1)}, bf16[48,2048]{1,0:T(8,128)(2,1)S(1)}, u32[]{:S(2)}, u32[]{:S(2)}) collective-permute-start(bf16[48,2048]{1,0:T(8,128)(2,1)S(1)} %get-tuple-element.30), channel_id=1, source_target_pairs={{0,3},{1,2},{2,1},{3,0},{4,7},{5,6},{6,5},{7,4},{8,11},{9,10},{10,... | collective-permute-start | bytes 589832 | tf_op jit(solution)/shard_map/ppermute | solution.py:70
  32.7 0.9 collective-permute-start.14
  33.6 0.7 fusion.4
  34.3 1.2 collective-permute-start.2
  35.5 0.5 fusion.15
  36.0 15.2 %collective-permute-done.2.refs_3_ = bf16[400,256]{1,0:T(8,128)(2,1)S(1)} collective-permute-done((bf16[400,256]{1,0:T(8,128)(2,1)S(1)}, bf16[400,256]{1,0:T(8,128)(2,1)S(1)}, u32[]{:S(2)}, u32[]{:S(2)}) %collective-permute-start.2) | collective-permute-done | bytes 204832 | tf_op jit(solution)/shard_map/ppermute | solution.py:70
  51.3 0.5 fusion.12
  51.7 0.5 convolution_convert_fusion.1
  52.2 0.5 collective-permute-start.10
  52.8 0.2 fusion.21
  53.0 0.9 collective-permute-done.3
  53.9 2.6 %collective-permute-start.9 = (bf16[1,32,2048]{2,1,0:T(8,128)(2,1)S(1)}, bf16[1,32,2048]{2,1,0:T(8,128)(2,1)S(1)}, u32[]{:S(2)}, u32[]{:S(2)}) collective-permute-start(bf16[1,32,2048]{2,1,0:T(8,128)(2,1)S(1)} %get-tuple-element.37), channel_id=1, source_target_pairs={{0,24},{4,28},{8,16},{12,20},{16,8},{20,12},{24,0},{28,4},{1,25},{... | collective-permute-start | bytes 393224 | tf_op jit(solution)/shard_map/ppermute | solution.py:65
  56.5 0.3 bitcast_add_fusion
  57.0 0.6 collective-permute-start.4
  57.6 0.1 fusion.20
  57.8 8.5 %collective-permute-done.4 = bf16[2,2,32,2048]{3,2,1,0:T(8,128)(2,1)S(1)} collective-permute-done((bf16[2,2,32,2048]{3,2,1,0:T(8,128)(2,1)S(1)}, bf16[2,2,32,2048]{3,2,1,0:T(8,128)(2,1)S(1)}, u32[]{:S(2)}, u32[]{:S(2)}) %collective-permute-start.4) | collective-permute-done | bytes 524320 | tf_op jit(solution)/shard_map/ppermute | solution.py:58
  66.2 0.9 collective-permute-start.8
  67.3 1.6 %collective-permute-start.7 = (bf16[1,32,2048]{2,1,0:T(8,128)(2,1)S(1)}, bf16[1,32,2048]{2,1,0:T(8,128)(2,1)S(1)}, u32[]{:S(2)}, u32[]{:S(2)}) collective-permute-start(bf16[1,32,2048]{2,1,0:T(8,128)(2,1)S(1)} %get-tuple-element.39), channel_id=1, source_target_pairs={{0,8},{4,20},{8,0},{12,28},{16,24},{20,4},{24,16},{28,12},{1,9},{5... | collective-permute-start | bytes 393224 | tf_op jit(solution)/shard_map/ppermute | solution.py:58
  68.9 1.1 collective-permute-start.13
  70.0 0.9 collective-permute-start.12
  70.9 1.5 %collective-permute-start.11 = (bf16[1,32,2048]{2,1,0:T(8,128)(2,1)S(1)}, bf16[1,32,2048]{2,1,0:T(8,128)(2,1)S(1)}, u32[]{:S(2)}, u32[]{:S(2)}) collective-permute-start(bf16[1,32,2048]{2,1,0:T(8,128)(2,1)S(1)} %get-tuple-element.36), channel_id=1, source_target_pairs={{0,8},{4,20},{8,0},{12,28},{16,24},{20,4},{24,16},{28,12},{1,9},{5... | collective-permute-start | bytes 393224 | tf_op jit(solution)/shard_map/ppermute | solution.py:58
  72.4 1.1 collective-permute-start.5
  73.6 3.1 %collective-permute-done.13 = bf16[1,32,2048]{2,1,0:T(8,128)(2,1)S(1)} collective-permute-done((bf16[1,32,2048]{2,1,0:T(8,128)(2,1)S(1)}, bf16[1,32,2048]{2,1,0:T(8,128)(2,1)S(1)}, u32[]{:S(2)}, u32[]{:S(2)}) %collective-permute-start.13) | collective-permute-done | bytes 131104 | tf_op jit(solution)/shard_map/ppermute | solution.py:65
  76.7 1.5 %collective-permute-done.12 = bf16[1,32,2048]{2,1,0:T(8,128)(2,1)S(1)} collective-permute-done((bf16[1,32,2048]{2,1,0:T(8,128)(2,1)S(1)}, bf16[1,32,2048]{2,1,0:T(8,128)(2,1)S(1)}, u32[]{:S(2)}, u32[]{:S(2)}) %collective-permute-start.12) | collective-permute-done | bytes 131104 | tf_op jit(solution)/shard_map/ppermute | solution.py:58
  78.2 0.5 collective-permute-done.11
  78.7 2.3 %collective-permute-done.5 = bf16[1,2,32,2048]{3,2,1,0:T(8,128)(2,1)S(1)} collective-permute-done((bf16[1,2,32,2048]{3,2,1,0:T(8,128)(2,1)S(1)}, bf16[1,2,32,2048]{3,2,1,0:T(8,128)(2,1)S(1)}, u32[]{:S(2)}, u32[]{:S(2)}) %collective-permute-start.5) | collective-permute-done | bytes 262176 | tf_op jit(solution)/shard_map/ppermute | solution.py:58
  81.0 1.2 shard_map.108
  82.2 1.6 %collective-permute-start.17 = (f32[1,2304]{1,0:T(1,128)S(1)}, f32[1,2304]{1,0:T(1,128)S(1)}, u32[]{:S(2)}, u32[]{:S(2)}) collective-permute-start(f32[1,2304]{1,0:T(1,128)S(1)} %get-tuple-element.23), channel_id=1, source_target_pairs={{0,1},{1,0},{2,3},{3,2},{4,5},{5,4},{6,7},{7,6},{8,9},{9,8},{10,11... | collective-permute-start | bytes 27656 | tf_op jit(solution)/shard_map/ppermute | solution.py:70
  83.8 2.0 %collective-permute-start.18 = (f32[1,2304]{1,0:T(1,128)S(1)}, f32[1,2304]{1,0:T(1,128)S(1)}, u32[]{:S(2)}, u32[]{:S(2)}) collective-permute-start(f32[1,2304]{1,0:T(1,128)S(1)} %get-tuple-element.24), channel_id=1, source_target_pairs={{0,2},{1,3},{2,0},{3,1},{4,6},{5,7},{6,4},{7,5},{8,10},{9,11},{10,... | collective-permute-start | bytes 27656 | tf_op jit(solution)/shard_map/ppermute | solution.py:70
  85.8 0.9 collective-permute-start.19
  86.6 1.7 %collective-permute-done.18.refs_2_ = f32[1,2304]{1,0:T(1,128)S(1)} collective-permute-done((f32[1,2304]{1,0:T(1,128)S(1)}, f32[1,2304]{1,0:T(1,128)S(1)}, u32[]{:S(2)}, u32[]{:S(2)}) %collective-permute-start.18) | collective-permute-done | bytes 9248 | tf_op jit(solution)/shard_map/ppermute | solution.py:70
  88.4 2.9 %collective-permute-done.19.refs_3_ = f32[1,2304]{1,0:T(1,128)S(1)} collective-permute-done((f32[1,2304]{1,0:T(1,128)S(1)}, f32[1,2304]{1,0:T(1,128)S(1)}, u32[]{:S(2)}, u32[]{:S(2)}) %collective-permute-start.19) | collective-permute-done | bytes 9248 | tf_op jit(solution)/shard_map/ppermute | solution.py:70
  91.2 0.6 shard_map.109.refs_2_.refs_0_
  91.9 1.0 collective-permute-start.20
  92.8 1.4 collective-permute-start.23
  94.2 13.1 %collective-permute-done.20.refs_2_ = bf16[136,2048]{1,0:T(8,128)(2,1)S(1)} collective-permute-done((bf16[136,2048]{1,0:T(8,128)(2,1)S(1)}, bf16[136,2048]{1,0:T(8,128)(2,1)S(1)}, u32[]{:S(2)}, u32[]{:S(2)}) %collective-permute-start.20) | collective-permute-done | bytes 557088 | tf_op jit(solution)/shard_map/ppermute | solution.py:58
  107.4 0.9 collective-permute-start.21
  108.2 0.5 collective-permute-start.25
  108.8 0.1 collective-permute-start.24
  108.9 0.7 shard_map.106.refs_0_
  109.6 7.2 %collective-permute-done.21.refs_2_.refs_6_ = bf16[136,2048]{1,0:T(8,128)(2,1)S(1)} collective-permute-done((bf16[136,2048]{1,0:T(8,128)(2,1)S(1)}, bf16[136,2048]{1,0:T(8,128)(2,1)S(1)}, u32[]{:S(2)}, u32[]{:S(2)}) %collective-permute-start.21) | collective-permute-done | bytes 557088 | tf_op jit(solution)/shard_map/ppermute | solution.py:58
  116.9 5.3 %shard_map.110.refs_3_ = f32[400,2048]{1,0:T(8,128)S(1)} custom-call(bf16[400,1024]{1,0:T(8,128)(2,1)S(1)} %shard_map.106.refs_0_, f32[400,128]{1,0:T(8,128)S(1)} %get-tuple-element.15.refs_1_, bf16[136,2048]{1,0:T(8,128)(2,1)S(1)} %shard_map.109.refs_2_.refs_0_, bf16[136,2048]{1,0:T(8,128)(2,1)S(1)} %collective-permute-done.26.refs_3_.refs_1_), custom_call_target="tpu_custom_call" | custom-call | flops 1966080000 | tf_op jit(solution)/shard_map/pallas_call | solution.py:354
  122.2 3.0 %shard_map.111.refs_3_ = f32[400,2048]{1,0:T(8,128)S(1)} custom-call(bf16[400,1024]{1,0:T(8,128)(2,1)S(1)} %shard_map.106.refs_0_, f32[400,128]{1,0:T(8,128)S(1)} %get-tuple-element.15.refs_1_, bf16[136,2048]{1,0:T(8,128)(2,1)S(1)} %collective-permute-done.20.refs_2_, f32[400,2048]{1,0:T(8,128)S(1)} %shard_map.110.refs_3_), custom_call_target="tpu_custom_call" | custom-call | flops 983040000 | tf_op jit(solution)/shard_map/pallas_call | solution.py:354
  125.2 2.8 %shard_map.112.refs_3_ = f32[400,2048]{1,0:T(8,128)S(1)} custom-call(bf16[400,1024]{1,0:T(8,128)(2,1)S(1)} %shard_map.106.refs_0_, f32[400,128]{1,0:T(8,128)S(1)} %get-tuple-element.15.refs_1_, bf16[136,2048]{1,0:T(8,128)(2,1)S(1)} %collective-permute-done.25.refs_2_.refs_5_, f32[400,2048]{1,0:T(8,128)S(1)} %shard_map.111.refs_3_), custom_call_target="tpu_custom_call" | custom-call | flops 983040000 | tf_op jit(solution)/shard_map/pallas_call | solution.py:354
  128.0 2.8 %shard_map.113.refs_3_ = f32[400,2048]{1,0:T(8,128)S(1)} custom-call(bf16[400,1024]{1,0:T(8,128)(2,1)S(1)} %shard_map.106.refs_0_, f32[400,128]{1,0:T(8,128)S(1)} %get-tuple-element.15.refs_1_, bf16[136,2048]{1,0:T(8,128)(2,1)S(1)} %collective-permute-done.23.refs_2_.refs_4_, f32[400,2048]{1,0:T(8,128)S(1)} %shard_map.112.refs_3_), custom_call_target="tpu_custom_call" | custom-call | flops 983040000 | tf_op jit(solution)/shard_map/pallas_call | solution.py:354
  130.8 2.8 %shard_map.114.refs_3_ = f32[400,2048]{1,0:T(8,128)S(1)} custom-call(bf16[400,1024]{1,0:T(8,128)(2,1)S(1)} %shard_map.106.refs_0_, f32[400,128]{1,0:T(8,128)S(1)} %get-tuple-element.15.refs_1_, bf16[136,2048]{1,0:T(8,128)(2,1)S(1)} %collective-permute-done.24.refs_2_.refs_3_, f32[400,2048]{1,0:T(8,128)S(1)} %shard_map.113.refs_3_), custom_call_target="tpu_custom_call" | custom-call | flops 983040000 | tf_op jit(solution)/shard_map/pallas_call | solution.py:354
  133.6 2.8 %shard_map.115.refs_3_ = f32[400,2048]{1,0:T(8,128)S(1)} custom-call(bf16[400,1024]{1,0:T(8,128)(2,1)S(1)} %shard_map.106.refs_0_, f32[400,128]{1,0:T(8,128)S(1)} %get-tuple-element.15.refs_1_, bf16[136,2048]{1,0:T(8,128)(2,1)S(1)} %collective-permute-done.21.refs_2_.refs_6_, f32[400,2048]{1,0:T(8,128)S(1)} %shard_map.114.refs_3_), custom_call_target="tpu_custom_call" | custom-call | flops 983040000 | tf_op jit(solution)/shard_map/pallas_call | solution.py:354
  136.5 0.9 collective-permute-start.29
  137.5 3.5 %collective-permute-start.27 = (f32[1,2048]{1,0:T(1,128)S(1)}, f32[1,2048]{1,0:T(1,128)S(1)}, u32[]{:S(2)}, u32[]{:S(2)}) collective-permute-start(f32[1,2048]{1,0:T(1,128)S(1)} %shard_map.117), channel_id=1, source_target_pairs={{0,1},{1,0},{2,3},{3,2},{4,5},{5,4},{6,7},{7,6},{8,9},{9,8},{10,11... | collective-permute-start | bytes 24584 | tf_op jit(solution)/shard_map/ppermute | solution.py:70
  141.0 3.7 %shard_map.116 = f32[400,2048]{1,0:T(8,128)} custom-call(bf16[400,1024]{1,0:T(8,128)(2,1)S(1)} %shard_map.106.refs_0_, f32[400,128]{1,0:T(8,128)S(1)} %get-tuple-element.15.refs_1_, bf16[136,2048]{1,0:T(8,128)(2,1)S(1)} %collective-permute-done.22.refs_2_.refs_7_, f32[400,2048]{1,0:T(8,128)S(1)} %shard_map.115.refs_3_), custom_call_target="tpu_custom_call" | custom-call | flops 983040000 | tf_op jit(solution)/shard_map/pallas_call | solution.py:354
  144.7 0.6 gather_fusion
  145.4 0.6 copy.17
  (52 shorter events, 1.0 us)
Async XLA Ops:
  0.6 26.7 %copy-start = (bf16[400,2048]{1,0:T(8,128)(2,1)S(1)}, bf16[400,2048]{1,0:T(8,128)(2,1)}, u32[]{:S(2)}) copy-start(bf16[400,2048]{1,0:T(8,128)(2,1)} %param.10) | copy-start | bytes 4915204
  2.6 13.5 %all-to-all-start = ((bf16[8,48,400]{2,1,0:T(8,128)(2,1)}), bf16[8,48,400]{2,1,0:T(8,128)(2,1)S(1)}, u32[]{:S(2)}, u32[]{:S(2)}) async-start(bf16[8,48,400]{2,1,0:T(8,128)(2,1)} %shard_map.104), calls=%async_computation | async-start | bytes 786432 | tf_op jit(solution)/shard_map/all_to_all | solution.py:426
  16.4 11.0 %collective-permute-start.1 = (bf16[400,256]{1,0:T(8,128)(2,1)S(1)}, bf16[400,256]{1,0:T(8,128)(2,1)S(1)}, u32[]{:S(2)}, u32[]{:S(2)}) collective-permute-start(bf16[400,256]{1,0:T(8,128)(2,1)S(1)} %get-tuple-element.14.refs_0_), channel_id=1, source_target_pairs={{0,2},{1,3},{2,0},{3,1},{4,6},{5,7},{6,4},{7,5},{8,10},{9,11},{10,... | collective-permute-start | bytes 614408 | tf_op jit(solution)/shard_map/ppermute | solution.py:70
  19.0 8.9 %collective-permute-start = (bf16[400,256]{1,0:T(8,128)(2,1)S(1)}, bf16[400,256]{1,0:T(8,128)(2,1)S(1)}, u32[]{:S(2)}, u32[]{:S(2)}) collective-permute-start(bf16[400,256]{1,0:T(8,128)(2,1)S(1)} %get-tuple-element.14.refs_0_), channel_id=1, source_target_pairs={{0,1},{1,0},{2,3},{3,2},{4,5},{5,4},{6,7},{7,6},{8,9},{9,8},{10,11... | collective-permute-start | bytes 614408 | tf_op jit(solution)/shard_map/ppermute | solution.py:70
  27.8 24.4 %collective-permute-start.6 = (bf16[4,1,32,2048]{3,2,1,0:T(8,128)(2,1)S(1)}, bf16[4,1,32,2048]{3,2,1,0:T(8,128)(2,1)S(1)}, u32[]{:S(2)}, u32[]{:S(2)}) collective-permute-start(bf16[4,1,32,2048]{3,2,1,0:T(8,128)(2,1)S(1)} %bitcast.96), channel_id=1, source_target_pairs={{0,4},{4,0},{8,12},{12,8},{16,20},{20,16},{24,28},{28,24},{1,5},{5... | collective-permute-start | bytes 1572872 | tf_op jit(solution)/shard_map/ppermute | solution.py:41
  28.0 1.1 copy-start.5
  29.2 38.1 %collective-permute-start.16 = (bf16[48,2048]{1,0:T(8,128)(2,1)S(1)}, bf16[48,2048]{1,0:T(8,128)(2,1)S(1)}, u32[]{:S(2)}, u32[]{:S(2)}) collective-permute-start(bf16[48,2048]{1,0:T(8,128)(2,1)S(1)} %get-tuple-element.30), channel_id=1, source_target_pairs={{0,3},{1,2},{2,1},{3,0},{4,7},{5,6},{6,5},{7,4},{8,11},{9,10},{10,... | collective-permute-start | bytes 589832 | tf_op jit(solution)/shard_map/ppermute | solution.py:70
  32.7 36.2 %collective-permute-start.15 = (bf16[48,2048]{1,0:T(8,128)(2,1)S(1)}, bf16[48,2048]{1,0:T(8,128)(2,1)S(1)}, u32[]{:S(2)}, u32[]{:S(2)}) collective-permute-start(bf16[48,2048]{1,0:T(8,128)(2,1)S(1)} %get-tuple-element.31), channel_id=1, source_target_pairs={{0,2},{1,3},{2,0},{3,1},{4,6},{5,7},{6,4},{7,5},{8,10},{9,11},{10,... | collective-permute-start | bytes 589832 | tf_op jit(solution)/shard_map/ppermute | solution.py:70
  32.7 37.3 %collective-permute-start.14 = (bf16[48,2048]{1,0:T(8,128)(2,1)S(1)}, bf16[48,2048]{1,0:T(8,128)(2,1)S(1)}, u32[]{:S(2)}, u32[]{:S(2)}) collective-permute-start(bf16[48,2048]{1,0:T(8,128)(2,1)S(1)} %get-tuple-element.32), channel_id=1, source_target_pairs={{0,1},{1,0},{2,3},{3,2},{4,5},{5,4},{6,7},{7,6},{8,9},{9,8},{10,11... | collective-permute-start | bytes 589832 | tf_op jit(solution)/shard_map/ppermute | solution.py:70
  34.3 16.9 %collective-permute-start.2 = (bf16[400,256]{1,0:T(8,128)(2,1)S(1)}, bf16[400,256]{1,0:T(8,128)(2,1)S(1)}, u32[]{:S(2)}, u32[]{:S(2)}) collective-permute-start(bf16[400,256]{1,0:T(8,128)(2,1)S(1)} %collective-permute-done.1.refs_2_), channel_id=1, source_target_pairs={{0,1},{1,0},{2,3},{3,2},{4,5},{5,4},{6,7},{7,6},{8,9},{9,8},{10,11... | collective-permute-start | bytes 614408 | tf_op jit(solution)/shard_map/ppermute | solution.py:70
  51.2 2.7 %collective-permute-start.3 = (bf16[4,2,32,2048]{3,2,1,0:T(8,128)(2,1)S(1)}, bf16[4,2,32,2048]{3,2,1,0:T(8,128)(2,1)S(1)}, u32[]{:S(2)}, u32[]{:S(2)}) collective-permute-start(bf16[4,2,32,2048]{3,2,1,0:T(8,128)(2,1)S(1)} %bitcast.95), channel_id=1, source_target_pairs={{0,4},{4,0},{8,12},{12,8},{16,20},{20,16},{24,28},{28,24},{1,5},{5... | collective-permute-start | bytes 3145736 | tf_op jit(solution)/shard_map/ppermute | solution.py:41
  52.2 4.7 %collective-permute-start.10 = (bf16[4,1,32,2048]{3,2,1,0:T(8,128)(2,1)S(1)}, bf16[4,1,32,2048]{3,2,1,0:T(8,128)(2,1)S(1)}, u32[]{:S(2)}, u32[]{:S(2)}) collective-permute-start(bf16[4,1,32,2048]{3,2,1,0:T(8,128)(2,1)S(1)} %bitcast.97), channel_id=1, source_target_pairs={{0,4},{4,0},{8,12},{12,8},{16,20},{20,16},{24,28},{28,24},{1,5},{5... | collective-permute-start | bytes 1572872 | tf_op jit(solution)/shard_map/ppermute | solution.py:41
  53.9 17.0 %collective-permute-start.9 = (bf16[1,32,2048]{2,1,0:T(8,128)(2,1)S(1)}, bf16[1,32,2048]{2,1,0:T(8,128)(2,1)S(1)}, u32[]{:S(2)}, u32[]{:S(2)}) collective-permute-start(bf16[1,32,2048]{2,1,0:T(8,128)(2,1)S(1)} %get-tuple-element.37), channel_id=1, source_target_pairs={{0,24},{4,28},{8,16},{12,20},{16,8},{20,12},{24,0},{28,4},{1,25},{... | collective-permute-start | bytes 393224 | tf_op jit(solution)/shard_map/ppermute | solution.py:65
  57.0 9.3 %collective-permute-start.4 = (bf16[2,2,32,2048]{3,2,1,0:T(8,128)(2,1)S(1)}, bf16[2,2,32,2048]{3,2,1,0:T(8,128)(2,1)S(1)}, u32[]{:S(2)}, u32[]{:S(2)}) collective-permute-start(bf16[2,2,32,2048]{3,2,1,0:T(8,128)(2,1)S(1)} %fusion.2), channel_id=1, source_target_pairs={{0,8},{4,20},{8,0},{12,28},{16,24},{20,4},{24,16},{28,12},{1,9},{5... | collective-permute-start | bytes 1572872 | tf_op jit(solution)/shard_map/ppermute | solution.py:58
  66.2 14.8 %copy-start.1 = (f32[8192]{0:T(1024)S(1)}, f32[8192]{0:T(1024)}, u32[]{:S(2)}) copy-start(f32[8192]{0:T(1024)} %param.13) | copy-start | bytes 98308
  66.2 14.8 %copy-start.2 = (f32[4,1,2048]{2,1,0:T(1,128)S(1)}, f32[4,1,2048]{2,1,0:T(1,128)}, u32[]{:S(2)}) copy-start(f32[4,1,2048]{2,1,0:T(1,128)} %get-tuple-element.16.part_ref) | copy-start | bytes 98308
  66.2 14.8 %copy-start.4 = (s32[1,128]{1,0:T(1,128)S(1)}, s32[1,128]{1,0:T(1,128)}, u32[]{:S(2)}) copy-start(s32[1,128]{1,0:T(1,128)} %row_ref.3) | copy-start | bytes 1540
  66.2 6.1 %collective-permute-start.8 = (bf16[1,32,2048]{2,1,0:T(8,128)(2,1)S(1)}, bf16[1,32,2048]{2,1,0:T(8,128)(2,1)S(1)}, u32[]{:S(2)}, u32[]{:S(2)}) collective-permute-start(bf16[1,32,2048]{2,1,0:T(8,128)(2,1)S(1)} %get-tuple-element.38), channel_id=1, source_target_pairs={{0,16},{4,12},{8,24},{12,4},{16,0},{20,28},{24,8},{28,20},{1,17},{... | collective-permute-start | bytes 393224 | tf_op jit(solution)/shard_map/ppermute | solution.py:58
  67.3 6.3 %collective-permute-start.7 = (bf16[1,32,2048]{2,1,0:T(8,128)(2,1)S(1)}, bf16[1,32,2048]{2,1,0:T(8,128)(2,1)S(1)}, u32[]{:S(2)}, u32[]{:S(2)}) collective-permute-start(bf16[1,32,2048]{2,1,0:T(8,128)(2,1)S(1)} %get-tuple-element.39), channel_id=1, source_target_pairs={{0,8},{4,20},{8,0},{12,28},{16,24},{20,4},{24,16},{28,12},{1,9},{5... | collective-permute-start | bytes 393224 | tf_op jit(solution)/shard_map/ppermute | solution.py:58
  68.9 7.8 %collective-permute-start.13 = (bf16[1,32,2048]{2,1,0:T(8,128)(2,1)S(1)}, bf16[1,32,2048]{2,1,0:T(8,128)(2,1)S(1)}, u32[]{:S(2)}, u32[]{:S(2)}) collective-permute-start(bf16[1,32,2048]{2,1,0:T(8,128)(2,1)S(1)} %get-tuple-element.34), channel_id=1, source_target_pairs={{0,24},{4,28},{8,16},{12,20},{16,8},{20,12},{24,0},{28,4},{1,25},{... | collective-permute-start | bytes 393224 | tf_op jit(solution)/shard_map/ppermute | solution.py:65
  70.0 8.2 %collective-permute-start.12 = (bf16[1,32,2048]{2,1,0:T(8,128)(2,1)S(1)}, bf16[1,32,2048]{2,1,0:T(8,128)(2,1)S(1)}, u32[]{:S(2)}, u32[]{:S(2)}) collective-permute-start(bf16[1,32,2048]{2,1,0:T(8,128)(2,1)S(1)} %get-tuple-element.35), channel_id=1, source_target_pairs={{0,16},{4,12},{8,24},{12,4},{16,0},{20,28},{24,8},{28,20},{1,17},{... | collective-permute-start | bytes 393224 | tf_op jit(solution)/shard_map/ppermute | solution.py:58
  70.9 7.9 %collective-permute-start.11 = (bf16[1,32,2048]{2,1,0:T(8,128)(2,1)S(1)}, bf16[1,32,2048]{2,1,0:T(8,128)(2,1)S(1)}, u32[]{:S(2)}, u32[]{:S(2)}) collective-permute-start(bf16[1,32,2048]{2,1,0:T(8,128)(2,1)S(1)} %get-tuple-element.36), channel_id=1, source_target_pairs={{0,8},{4,20},{8,0},{12,28},{16,24},{20,4},{24,16},{28,12},{1,9},{5... | collective-permute-start | bytes 393224 | tf_op jit(solution)/shard_map/ppermute | solution.py:58
  72.4 8.7 %collective-permute-start.5 = (bf16[1,2,32,2048]{3,2,1,0:T(8,128)(2,1)S(1)}, bf16[1,2,32,2048]{3,2,1,0:T(8,128)(2,1)S(1)}, u32[]{:S(2)}, u32[]{:S(2)}) collective-permute-start(bf16[1,2,32,2048]{3,2,1,0:T(8,128)(2,1)S(1)} %fusion.3), channel_id=1, source_target_pairs={{0,16},{4,12},{8,24},{12,4},{16,0},{20,28},{24,8},{28,20},{1,17},{... | collective-permute-start | bytes 786440 | tf_op jit(solution)/shard_map/ppermute | solution.py:58
  73.5 17.7 %copy-start.3 = (f32[1,2048]{1,0:T(1,128)S(1)}, f32[1,2048]{1,0:T(1,128)}, u32[]{:S(2)}) copy-start(f32[1,2048]{1,0:T(1,128)} %draw_ref.1) | copy-start | bytes 24580
  82.2 4.4 %collective-permute-start.17 = (f32[1,2304]{1,0:T(1,128)S(1)}, f32[1,2304]{1,0:T(1,128)S(1)}, u32[]{:S(2)}, u32[]{:S(2)}) collective-permute-start(f32[1,2304]{1,0:T(1,128)S(1)} %get-tuple-element.23), channel_id=1, source_target_pairs={{0,1},{1,0},{2,3},{3,2},{4,5},{5,4},{6,7},{7,6},{8,9},{9,8},{10,11... | collective-permute-start | bytes 27656 | tf_op jit(solution)/shard_map/ppermute | solution.py:70
  83.8 4.6 %collective-permute-start.18 = (f32[1,2304]{1,0:T(1,128)S(1)}, f32[1,2304]{1,0:T(1,128)S(1)}, u32[]{:S(2)}, u32[]{:S(2)}) collective-permute-start(f32[1,2304]{1,0:T(1,128)S(1)} %get-tuple-element.24), channel_id=1, source_target_pairs={{0,2},{1,3},{2,0},{3,1},{4,6},{5,7},{6,4},{7,5},{8,10},{9,11},{10,... | collective-permute-start | bytes 27656 | tf_op jit(solution)/shard_map/ppermute | solution.py:70
  85.8 5.5 %collective-permute-start.19 = (f32[1,2304]{1,0:T(1,128)S(1)}, f32[1,2304]{1,0:T(1,128)S(1)}, u32[]{:S(2)}, u32[]{:S(2)}) collective-permute-start(f32[1,2304]{1,0:T(1,128)S(1)} %get-tuple-element.25), channel_id=1, source_target_pairs={{0,3},{1,2},{2,1},{3,0},{4,7},{5,6},{6,5},{7,4},{8,11},{9,10},{10,... | collective-permute-start | bytes 27656 | tf_op jit(solution)/shard_map/ppermute | solution.py:70
  91.9 15.5 %collective-permute-start.20 = (bf16[136,2048]{1,0:T(8,128)(2,1)S(1)}, bf16[136,2048]{1,0:T(8,128)(2,1)S(1)}, u32[]{:S(2)}, u32[]{:S(2)}) collective-permute-start(bf16[136,2048]{1,0:T(8,128)(2,1)S(1)} %shard_map.109.refs_2_.refs_0_), channel_id=1, source_target_pairs={{0,8},{4,20},{8,0},{12,28},{16,24},{20,4},{24,16},{28,12},{1,9},{5... | collective-permute-start | bytes 1671176 | tf_op jit(solution)/shard_map/ppermute | solution.py:58
  92.8 15.9 %collective-permute-start.23 = (bf16[136,2048]{1,0:T(8,128)(2,1)S(1)}, bf16[136,2048]{1,0:T(8,128)(2,1)S(1)}, u32[]{:S(2)}, u32[]{:S(2)}) collective-permute-start(bf16[136,2048]{1,0:T(8,128)(2,1)S(1)} %shard_map.109.refs_2_.refs_0_), channel_id=1, source_target_pairs={{0,16},{4,12},{8,24},{12,4},{16,0},{20,28},{24,8},{28,20},{1,17},{... | collective-permute-start | bytes 1671176 | tf_op jit(solution)/shard_map/ppermute | solution.py:58
  107.4 9.5 %collective-permute-start.21 = (bf16[136,2048]{1,0:T(8,128)(2,1)S(1)}, bf16[136,2048]{1,0:T(8,128)(2,1)S(1)}, u32[]{:S(2)}, u32[]{:S(2)}) collective-permute-start(bf16[136,2048]{1,0:T(8,128)(2,1)S(1)} %collective-permute-done.20.refs_2_), channel_id=1, source_target_pairs={{0,16},{4,12},{8,24},{12,4},{16,0},{20,28},{24,8},{28,20},{1,17},{... | collective-permute-start | bytes 1671176 | tf_op jit(solution)/shard_map/ppermute | solution.py:58
  108.2 8.7 %collective-permute-start.26 = (bf16[136,2048]{1,0:T(8,128)(2,1)S(1)}, bf16[136,2048]{1,0:T(8,128)(2,1)S(1)}, u32[]{:S(2)}, u32[]{:S(2)}) collective-permute-start(bf16[136,2048]{1,0:T(8,128)(2,1)S(1)} %shard_map.109.refs_2_.refs_0_), channel_id=1, source_target_pairs={{0,4},{4,0},{8,12},{12,8},{16,20},{20,16},{24,28},{28,24},{1,5},{5... | collective-permute-start | bytes 1671176 | tf_op jit(solution)/shard_map/ppermute | solution.py:41
  108.2 17.0 %collective-permute-start.25 = (bf16[136,2048]{1,0:T(8,128)(2,1)S(1)}, bf16[136,2048]{1,0:T(8,128)(2,1)S(1)}, u32[]{:S(2)}, u32[]{:S(2)}) collective-permute-start(bf16[136,2048]{1,0:T(8,128)(2,1)S(1)} %collective-permute-done.20.refs_2_), channel_id=1, source_target_pairs={{0,4},{4,0},{8,12},{12,8},{16,20},{20,16},{24,28},{28,24},{1,5},{5... | collective-permute-start | bytes 1671176 | tf_op jit(solution)/shard_map/ppermute | solution.py:41
  108.8 22.0 %collective-permute-start.24 = (bf16[136,2048]{1,0:T(8,128)(2,1)S(1)}, bf16[136,2048]{1,0:T(8,128)(2,1)S(1)}, u32[]{:S(2)}, u32[]{:S(2)}) collective-permute-start(bf16[136,2048]{1,0:T(8,128)(2,1)S(1)} %collective-permute-done.23.refs_2_.refs_4_), channel_id=1, source_target_pairs={{0,4},{4,0},{8,12},{12,8},{16,20},{20,16},{24,28},{28,24},{1,5},{5... | collective-permute-start | bytes 1671176 | tf_op jit(solution)/shard_map/ppermute | solution.py:41
  116.9 19.5 %collective-permute-start.22 = (bf16[136,2048]{1,0:T(8,128)(2,1)S(1)}, bf16[136,2048]{1,0:T(8,128)(2,1)S(1)}, u32[]{:S(2)}, u32[]{:S(2)}) collective-permute-start(bf16[136,2048]{1,0:T(8,128)(2,1)S(1)} %collective-permute-done.21.refs_2_.refs_6_), channel_id=1, source_target_pairs={{0,4},{4,0},{8,12},{12,8},{16,20},{20,16},{24,28},{28,24},{1,5},{5... | collective-permute-start | bytes 1671176 | tf_op jit(solution)/shard_map/ppermute | solution.py:41
  136.5 8.1 %collective-permute-start.29 = (f32[1,2048]{1,0:T(1,128)S(1)}, f32[1,2048]{1,0:T(1,128)S(1)}, u32[]{:S(2)}, u32[]{:S(2)}) collective-permute-start(f32[1,2048]{1,0:T(1,128)S(1)} %shard_map.117), channel_id=1, source_target_pairs={{0,3},{1,2},{2,1},{3,0},{4,7},{5,6},{6,5},{7,4},{8,11},{9,10},{10,... | collective-permute-start | bytes 24584 | tf_op jit(solution)/shard_map/ppermute | solution.py:70
  137.5 7.2 %collective-permute-start.28 = (f32[1,2048]{1,0:T(1,128)S(1)}, f32[1,2048]{1,0:T(1,128)S(1)}, u32[]{:S(2)}, u32[]{:S(2)}) collective-permute-start(f32[1,2048]{1,0:T(1,128)S(1)} %shard_map.117), channel_id=1, source_target_pairs={{0,2},{1,3},{2,0},{3,1},{4,6},{5,7},{6,4},{7,5},{8,10},{9,11},{10,... | collective-permute-start | bytes 24584 | tf_op jit(solution)/shard_map/ppermute | solution.py:70
  137.5 7.2 %collective-permute-start.27 = (f32[1,2048]{1,0:T(1,128)S(1)}, f32[1,2048]{1,0:T(1,128)S(1)}, u32[]{:S(2)}, u32[]{:S(2)}) collective-permute-start(f32[1,2048]{1,0:T(1,128)S(1)} %shard_map.117), channel_id=1, source_target_pairs={{0,1},{1,0},{2,3},{3,2},{4,5},{5,4},{6,7},{7,6},{8,9},{9,8},{10,11... | collective-permute-start | bytes 24584 | tf_op jit(solution)/shard_map/ppermute | solution.py:70
